TPU v7x, 32 devices: a whole 2x2x4 slice. The times are simulated.
32 devices in a mesh: grp: 2 (over y), subj: 4 (over x, core), vert: 4 (over z).
Axes of the slice: x: 2, y: 2, z: 4, core: 2. Of those that a mesh axis runs over, the one named last changes fastest.
Arguments:
- dosage: bfloat16 [16384, 512], P(('grp', 'subj')), parts along dimension 0, may hold values from 0 to 2
- phenotype: bfloat16 [16384, 20480], P(('grp', 'subj'), 'vert'), parts along dimension 0, may hold values from -12 to 12
- covariates: float32 [16384, 40], P(('grp', 'subj')), parts along dimension 0, may hold values from -7 to 7
Outputs:
- tstat: float32 [1024, 20480], P(('grp', 'subj'), 'vert'), parts along dimension 0
There are 2 independent parts, one for each index of `grp`. A program takes and returns all parts, laid end to end along the dimension named above; each array names one. Nothing has to cross between parts.
All inputs are finite; a program needn't handle non-finite values.
Results may differ from a plain program's by a relative error of at most 0.004.
Values sent between devices are 32-bit elements; how exact they have to be, the bound alone decides.
No kernel may reach another device: no remote copies, remote signals or barrier semaphores. Data moves between devices by JAX's collectives and lax.ppermute only.
A program may use at most 192 MiB of HBM per device.

v0:
```python
import jax
import jax.numpy as jnp
from jax import lax
from jax.sharding import PartitionSpec as P


def split_parts(values):
    upper = values.astype(jnp.bfloat16)
    restored = lax.optimization_barrier(upper).astype(jnp.float32)
    lower = (values - restored).astype(jnp.bfloat16)
    return (upper, lower)


def per_device(dosage, phenotype, covariates):
    local_rows = covariates.shape[0]
    hi = lax.Precision.HIGHEST
    design = jnp.concatenate([jnp.ones((local_rows, 1), jnp.float32), covariates], axis=1)
    design_upper, design_lower = split_parts(design)
    contract = (((0,), (0,)), ((), ()))
    geno = dosage.astype(jnp.float32)
    gram = jnp.dot(design.T, design, precision=hi)
    design_geno = jnp.dot(design.T, geno, precision=hi)
    design_pheno = lax.dot_general(
        design_upper, phenotype, contract, preferred_element_type=jnp.float32
    )
    design_pheno = design_pheno + lax.dot_general(
        design_lower, phenotype, contract, preferred_element_type=jnp.float32
    )
    pheno_square = jnp.sum(jnp.square(phenotype.astype(jnp.float32)), axis=0)
    gram, design_geno, design_pheno, geno_raw, pheno_raw = lax.psum(
        (gram, design_geno, design_pheno, jnp.sum(geno * geno, axis=0), pheno_square), "subj"
    )
    factor = jnp.linalg.cholesky(gram)
    geno_coef = jax.scipy.linalg.cho_solve((factor, True), design_geno)
    pheno_coef = jax.scipy.linalg.cho_solve((factor, True), design_pheno)
    geno_res = geno - jnp.dot(design, geno_coef, precision=hi)
    coef_upper, coef_lower = split_parts(pheno_coef)
    fitted = jnp.dot(design_upper, coef_upper, preferred_element_type=jnp.float32)
    fitted = fitted + jnp.dot(design_upper, coef_lower, preferred_element_type=jnp.float32)
    pheno_res = phenotype.astype(jnp.float32) - (
        fitted + jnp.dot(design_lower, coef_upper, preferred_element_type=jnp.float32)
    )
    geno_var = geno_raw - jnp.sum(design_geno * geno_coef, axis=0)
    pheno_var = pheno_raw - jnp.sum(design_pheno * pheno_coef, axis=0)
    geno_half = geno_res.astype(jnp.bfloat16)
    pheno_half = pheno_res.astype(jnp.bfloat16)
    snp_count = dosage.shape[1]
    owned = snp_count // lax.axis_size("subj")
    partial_value = lax.dot_general(
        geno_half, pheno_half, contract, preferred_element_type=jnp.float32
    )
    cross = lax.psum_scatter(partial_value, "subj", scatter_dimension=0, tiled=True)
    own_var = lax.dynamic_slice_in_dim(geno_var, lax.axis_index("subj") * owned, owned, 0)
    subjects_all = local_rows * lax.axis_size("subj")
    dof = jnp.float32(subjects_all - covariates.shape[1] - 2)
    return cross * jnp.sqrt(dof) / jnp.sqrt(own_var[:, None] * pheno_var[None, :] - cross * cross)


def solution(mesh):
    in_specs = (P(("grp", "subj"), None), P(("grp", "subj"), "vert"), P(("grp", "subj"), None))
    out_specs = P(("grp", "subj"), "vert")
    return jax.shard_map(
        per_device, mesh=mesh, in_specs=in_specs, out_specs=out_specs, check_vma=False
    )
```

profile of v0, /device:TPU:0, one launch (start us, length us, event | category | flops | bytes accessed | tf_op | source)
XLA Modules:
  0.0 246.3 jit_solution(11703205025247056992)
XLA Ops:
  6.5 0.0 all-reduce.5.cloned.1.call-start
  6.5 1.0 pad_convert_fusion
  7.5 3.5 %fusion.10 = f32[41,512]{1,0:T(8,128)} fusion(bf16[2048,512]{1,0:T(8,128)(2,1)} %param.3, f32[2048,40]{0,1:T(8,128)} %param.5), kind=kOutput, calls=%fused_computation.18 | convolution fusion | flops 515899392 | bytes 2508800 | tf_op jit(solution)/shard_map/dot_general | solution.py:22
  11.1 0.0 copy-start
  11.1 0.0 copy-start.2
  11.1 8.9 %fusion.31 = f32[41,5120]{1,0:T(8,128)S(1)} fusion(bf16[2048,41]{0,1:T(8,128)(2,1)S(1)} %pad_convert_fusion, bf16[2048,5120]{1,0:T(8,128)(2,1)} %param.4), kind=kOutput, calls=%fused_computation.43 | convolution fusion | flops 859832320 | bytes 21979136 | tf_op jit(solution)/shard_map/dot_general | solution.py:23
  20.0 4.0 %copy-done = bf16[2048,5120]{1,0:T(8,128)(2,1)S(1)} copy-done((bf16[2048,5120]{1,0:T(8,128)(2,1)S(1)}, bf16[2048,5120]{1,0:T(8,128)(2,1)}, u32[]{:S(2)}) %copy-start) | copy-done | bytes 20971544
  24.0 0.0 copy-done.2
  24.0 0.0 copy-start.1
  24.0 4.7 %convolution_add_fusion = f32[41,5120]{1,0:T(8,128)} fusion(f32[41,5120]{1,0:T(8,128)S(1)} %fusion.31, bf16[2048,5120]{1,0:T(8,128)(2,1)S(1)} %copy-done, f32[2048,40]{0,1:T(8,128)S(1)} %copy-done.2, bf16[2048,41]{0,1:T(8,128)(2,1)S(1)} %pad_convert_fusion), kind=kOutput, calls=%fused_computation.6 | convolution fusion | flops 860294144 | bytes 23146496 | tf_op jit(solution)/shard_map/dot_general | solution.py:26
  28.7 0.0 all-reduce.5.cloned.1.call-update
  28.7 0.0 reduce-scatter.2.cloned.1.call-start
  28.8 0.0 copy-done.1
  28.8 0.5 fusion.7
  29.3 9.1 %fusion.1 = f32[5120]{0:T(1024)S(1)} fusion(bf16[2048,5120]{1,0:T(8,128)(2,1)} %param.4), kind=kLoop, calls=%fused_computation.3 | loop fusion | flops 31452160 | bytes 20992000 | tf_op jit(solution)/shard_map/reduce_sum | solution.py:29
  38.4 0.5 fusion.12
  38.9 13.4 %all-reduce.1 = (f32[41,41]{0,1:T(8,128)S(1)}, f32[5120]{0:T(1024)S(1)}, f32[512]{0:T(512)S(1)}) all-reduce(f32[41,41]{0,1:T(8,128)S(1)} %fusion.12, f32[5120]{0:T(1024)S(1)} %fusion.1, f32[512]{0:T(512)S(1)} %fusion.7), channel_id=1, replica_groups=mesh['grp'=2,'subj'=4,'vert'=4] {'subj'}, use_global_device_ids=true, to_apply=%region_0.0 | all-reduce | flops 7313 | bytes 58504 | tf_op jit(solution)/shard_map/psum | solution.py:30
  52.3 0.1 copy.5
  52.4 3.7 %cholesky.16 = f32[41,41]{1,0:T(8,128)S(1)} custom-call(f32[41,41]{1,0:T(8,128)S(1)} %fusion.24), custom_call_target="Cholesky" | custom-call | tf_op jit(solution)/shard_map/jit(cholesky)/cholesky | solution.py:33
  56.2 0.7 compare_reduce_fusion
  56.9 0.6 fusion.15
  57.5 3.1 %custom-call.16 = f32[1,41,41]{1,2,0:T(8,128)S(1)} custom-call(f32[1,41,41]{2,1,0:T(8,128)S(1)} %fusion.15), custom_call_target="InvertDiagBlocksLowerTriangular" | custom-call | tf_op jit(solution)/shard_map/jit(_cho_solve)/triangular_solve | solution.py:34
  60.7 8.3 %all-reduce.5.cloned.1.call-done = (f32[41,512]{1,0:T(8,128)}, f32[41,5120]{1,0:T(8,128)}) async-done(((f32[41,512]{1,0:T(8,128)}, f32[41,5120]{1,0:T(8,128)}), (f32[41,512]{1,0:T(8,128)}, f32[41,5120]{1,0:T(8,128)})) %all-reduce.5.cloned.1.call-update) | async-done | bytes 923664 | tf_op jit(solution)/shard_map/psum | solution.py:30
  68.9 2.2 fusion.18
  71.1 2.2 multiply_reduce_fusion
  73.3 0.0 copy-start.4
  73.3 16.3 %fusion.32 = f32[2048,5120]{1,0:T(8,128)} fusion(bf16[2048,41]{0,1:T(8,128)(2,1)S(1)} %pad_convert_fusion, bf16[41,5120]{1,0:T(8,128)(2,1)S(1)} %get-tuple-element.11), kind=kOutput, calls=%fused_computation.44 | convolution fusion | flops 859832320 | bytes 42530816 | tf_op jit(solution)/shard_map/dot_general | solution.py:38
  89.6 0.0 copy-done.4
  89.6 0.3 fusion.22
  89.9 0.2 multiply_reduce_fusion.1
  90.2 4.8 %fusion.6 = bf16[2048,512]{1,0:T(8,128)(2,1)} fusion(bf16[2048,512]{1,0:T(8,128)(2,1)S(1)} %copy-done.1, f32[41,512]{1,0:T(8,128)S(1)} %get-tuple-element.14, f32[2048,40]{0,1:T(8,128)S(1)} %copy-done.2), kind=kOutput, calls=%fused_computation.9 | convolution fusion | flops 519045120 | bytes 4605952 | tf_op jit(solution)/shard_map/dot_general | solution.py:36
  95.0 0.0 copy-start.3
  95.0 16.2 %fusion.8 = f32[2048,5120]{1,0:T(8,128)} fusion(bf16[2048,41]{0,1:T(8,128)(2,1)S(1)} %pad_convert_fusion, f32[41,5120]{1,0:T(8,128)S(1)} %get-tuple-element.12, bf16[41,5120]{1,0:T(8,128)(2,1)S(1)} %get-tuple-element.11), kind=kOutput, calls=%fused_computation.14 | convolution fusion | flops 860462080 | bytes 43370496 | tf_op jit(solution)/shard_map/dot_general | solution.py:39
  111.2 0.0 copy-done.3
  111.2 39.7 %fusion.2 = f32[512,5120]{1,0:T(8,128)} fusion(bf16[2048,512]{1,0:T(8,128)(2,1)S(1)} %copy-done.3, bf16[2048,5120]{1,0:T(8,128)(2,1)} %param.4, f32[2048,5120]{1,0:T(8,128)} %fusion.32, f32[2048,5120]{1,0:T(8,128)} %fusion.8, bf16[41,5120]{1,0:T(8,128)(2,1)S(1)} %get-tuple-element.11, f32[2048,40]{0,1:T(8,128)S(1)} %copy-done.2, ...), kind=kOutput, calls=%fused_computation.4 | convolution fusion | flops 11649931264 | bytes 118355968 | tf_op jit(solution)/shard_map/dot_general | solution.py:49
  150.9 0.0 reduce-scatter.2.cloned.1.call-update
  150.9 0.1 dynamic_slice.3
  151.0 84.7 %reduce-scatter.2.cloned.1.call-done = f32[128,5120]{1,0:T(8,128)} async-done(((f32[512,5120]{1,0:T(8,128)}), f32[128,5120]{1,0:T(8,128)}) %reduce-scatter.2.cloned.1.call-update) | async-done | bytes 2621456 | tf_op jit(solution)/shard_map/reduce_scatter | solution.py:52
  235.7 3.8 %rsqrt_multiply_fusion = f32[128,5120]{1,0:T(8,128)} fusion(f32[128,5120]{1,0:T(8,128)} %reduce-scatter.2.cloned.1.call-done, f32[5120]{0:T(1024)S(1)} %sub.26, f32[128]{0:T(128)S(1)} %dynamic_slice.3), kind=kLoop, calls=%fused_computation.11 | loop fusion | flops 3276800 | bytes 5263872 | tf_op jit(solution)/shard_map/div | solution.py:56
  (4 shorter events, 0.0 us)
Async XLA Ops:
  6.5 62.4 %all-reduce.5.cloned.1.call-start = ((), (), s32[]{:S(2)}) async-start(), calls=%async_computation.2 | async-start | bytes 2162688 | tf_op jit(solution)/shard_map/psum | solution.py:30
  11.1 12.9 %copy-start = (bf16[2048,5120]{1,0:T(8,128)(2,1)S(1)}, bf16[2048,5120]{1,0:T(8,128)(2,1)}, u32[]{:S(2)}) copy-start(bf16[2048,5120]{1,0:T(8,128)(2,1)} %param.4) | copy-start | bytes 62914564
  11.1 12.9 %copy-start.2 = (f32[2048,40]{0,1:T(8,128)S(1)}, f32[2048,40]{0,1:T(8,128)}, u32[]{:S(2)}) copy-start(f32[2048,40]{0,1:T(8,128)} %param.5) | copy-start | bytes 983044
  24.0 4.8 %copy-start.1 = (bf16[2048,512]{1,0:T(8,128)(2,1)S(1)}, bf16[2048,512]{1,0:T(8,128)(2,1)}, u32[]{:S(2)}) copy-start(bf16[2048,512]{1,0:T(8,128)(2,1)} %param.3) | copy-start | bytes 6291460
  28.7 207.0 %reduce-scatter.2.cloned.1.call-start = ((), (), s32[]{:S(2)}) async-start(), calls=%async_computation.1 | async-start | bytes 13107200 | tf_op jit(solution)/shard_map/reduce_scatter | solution.py:52
  73.3 16.3 %copy-start.4 = (f32[41,512]{1,0:T(8,128)S(1)}, f32[41,512]{1,0:T(8,128)}, u32[]{:S(2)}) copy-start(f32[41,512]{1,0:T(8,128)} %get-tuple-element.8) | copy-start | bytes 251908
  95.0 16.2 %copy-start.3 = (bf16[2048,512]{1,0:T(8,128)(2,1)S(1)}, bf16[2048,512]{1,0:T(8,128)(2,1)}, u32[]{:S(2)}) copy-start(bf16[2048,512]{1,0:T(8,128)(2,1)} %fusion.6) | copy-start | bytes 6291460
Sparse Core Ops, SparseCore 0:
  28.8 40.0 all-reduce.4
  151.0 84.6 reduce-scatter.1
where the time goes:
time: 247 us; the launch traced here: 246 us
  matrix products  99.5 us (40%)
  waiting for transfers between devices  93 us (38%)
  other arithmetic  21.7 us (9%)
  between operations  13.5 us (5%)
  blocking collectives  13.4 us (5%)
  local copies, waits for them, and re-layouts  5.17 us (2%)
    reduce_scatter x1, waiting for transfers between devices, per_device(): lax.psum_scatter(partial_value, 'subj', scatter_dimension=0, tiled=True)  84.7 us
    dot_general x1, matrix products, per_device(): lax.dot_general(geno_half, pheno_half, contract, preferred_element_type=j...  39.7 us
    dot_general x1, matrix products, per_device(): jnp.dot(design_upper, coef_upper, preferred_element_type=jnp.float32)  16.3 us
    dot_general x1, matrix products, per_device(): jnp.dot(design_upper, coef_lower, preferred_element_type=jnp.float32)  16.2 us
    psum x1, blocking collectives, per_device(): lax.psum((gram, design_geno, design_pheno, jnp.sum(geno * geno, axis=0),...  13.4 us
    reduce_sum x1, other arithmetic, per_device(): pheno_square = jnp.sum(jnp.square(phenotype.astype(jnp.float32)), axis=0)  9.15 us
    dot_general x1, matrix products, per_device(): lax.dot_general(design_upper, phenotype, contract, preferred_element_type...  8.95 us
    psum x1, waiting for transfers between devices, per_device(): lax.psum((gram, design_geno, design_pheno, jnp.sum(geno * geno, axis=0),...  8.26 us
  transfers between devices with their start and end apart: 2, of which 2 were waited for; matrix products, arithmetic and copies ran while one was open for 8% of the time, Pallas kernels for 0%

commit v1 on v0

v1 whole, which is shorter than its diff:
```python
import functools

import jax
import jax.numpy as jnp
from jax import lax
from jax.experimental import pallas as pl
from jax.experimental.pallas import tpu as pltpu
from jax.sharding import PartitionSpec as P

HI = lax.Precision.HIGHEST
F32 = jnp.float32
BF16 = jnp.bfloat16
LANES = 128
LAST = (((1,), (1,)), ((), ()))


def round_up(value, unit):
    return -(-value // unit) * unit


def split_three(values):
    upper = values.astype(BF16)
    rest = values - upper.astype(F32)
    middle = rest.astype(BF16)
    lower = (rest - middle.astype(F32)).astype(BF16)
    return upper, middle, lower


def prepare_kernel(chips, rows, place_ref, geno_ref, cov_ref, left_ref, give_ref, keep_ref, turned, small):
    chip, core = place_ref[0], place_ref[1]
    covs, subjects = cov_ref.shape
    half = give_ref.shape[0] - chips * rows
    turned[...] = geno_ref[...].T
    for slot in range(chips):
        target = lax.rem(chip + slot + 1, chips) * (2 * rows)
        for side, own in ((0, 1 - core), (1, core)):
            base = (side * chips + slot) * rows
            start = pl.multiple_of(target + own * rows, rows)
            left_ref[base : base + rows, :] = turned[pl.ds(start, rows), :]
    design = jnp.concatenate(
        [jnp.ones((1, subjects), F32), cov_ref[...], jnp.zeros((LANES - covs - 1, subjects), F32)], axis=0
    )
    snps = 2 * chips * rows
    parts = split_three(design)
    for index, part in enumerate(parts):
        left_ref[snps + index * 2 * half : snps + (index + 1) * 2 * half, :] = part[: 2 * half, :]
    geno = left_ref[0:snps, :]
    product = sum(
        lax.dot_general(geno, part, LAST, preferred_element_type=F32) for part in reversed(parts)
    )
    wide = geno.astype(F32)
    square = jnp.sum(wide * wide, axis=1, keepdims=True)
    lane = lax.broadcasted_iota(jnp.int32, (snps, LANES), 1)
    product = jnp.where(lane == covs + 1, square, product)
    give_ref[0 : chips * rows, :] = product[: chips * rows]
    keep_ref[0 : chips * rows, :] = product[chips * rows :]
    small[...] = lax.dot_general(design[: 2 * half], design, LAST, precision=HI, preferred_element_type=F32)
    give_ref[chips * rows :, :] = small[pl.ds(pl.multiple_of((1 - core) * half, half), half), :]
    keep_ref[chips * rows :, :] = small[pl.ds(pl.multiple_of(core * half, half), half), :]


def prepare(place, dosage, cov_rows, chips, rows, half):
    subjects, snps = dosage.shape
    smem = pl.BlockSpec(memory_space=pltpu.SMEM)
    vmem = pl.BlockSpec(memory_space=pltpu.VMEM)
    part = jax.ShapeDtypeStruct((chips * rows + half, LANES), F32)
    return pl.pallas_call(
        functools.partial(prepare_kernel, chips, rows),
        out_shape=(jax.ShapeDtypeStruct((snps + 6 * half, subjects), BF16), part, part),
        in_specs=[smem, vmem, vmem],
        out_specs=(vmem, vmem, vmem),
        scratch_shapes=[pltpu.VMEM((snps, subjects), BF16), pltpu.VMEM((2 * half, LANES), F32)],
        compiler_params=pltpu.CompilerParams(vmem_limit_bytes=40 * 2**20),
        cost_estimate=pl.CostEstimate(
            flops=2 * snps * subjects * 1024, bytes_accessed=4 * snps * subjects, transcendentals=0
        ),
        name="prepare",
    )(place, dosage, cov_rows)


def product_kernel(split, half, row, place_ref, left_ref, pheno_ref, give_ref, keep_ref, small):
    core = place_ref[1]
    pheno = pheno_ref[...]
    result = jnp.dot(left_ref[...], pheno, preferred_element_type=F32)
    give_ref[0:split, :] = result[:split]
    keep_ref[0:split, :] = result[split : 2 * split]
    upper = result[2 * split : 2 * split + 2 * half]
    middle = result[2 * split + 2 * half : 2 * split + 4 * half]
    lower = result[2 * split + 4 * half :]
    wide = pheno.astype(F32)
    square = jnp.sum(wide * wide, axis=0, keepdims=True)
    index = lax.broadcasted_iota(jnp.int32, upper.shape, 0)
    small[...] = jnp.where(index == row, square, (lower + middle) + upper)
    give_ref[split:, :] = small[pl.ds(pl.multiple_of((1 - core) * half, half), half), :]
    keep_ref[split:, :] = small[pl.ds(pl.multiple_of(core * half, half), half), :]


def product(place, left, phenotype, start, width, tile, split, half, row):
    height, subjects = left.shape
    first = start // tile
    part = jax.ShapeDtypeStruct((split + half, width), F32)
    return pl.pallas_call(
        functools.partial(product_kernel, split, half, row),
        grid=(width // tile,),
        out_shape=(part, part),
        in_specs=[
            pl.BlockSpec(memory_space=pltpu.SMEM),
            pl.BlockSpec((height, subjects), lambda j: (0, 0)),
            pl.BlockSpec((subjects, tile), lambda j: (0, first + j)),
        ],
        out_specs=(
            pl.BlockSpec((split + half, tile), lambda j: (0, j)),
            pl.BlockSpec((split + half, tile), lambda j: (0, j)),
        ),
        scratch_shapes=[pltpu.VMEM((2 * half, tile), F32)],
        compiler_params=pltpu.CompilerParams(vmem_limit_bytes=30 * 2**20),
        cost_estimate=pl.CostEstimate(
            flops=2 * height * subjects * width,
            bytes_accessed=2 * subjects * width + 8 * split * width,
            transcendentals=0,
        ),
        name=f"product_{start}",
    )(place, left, phenotype)


def finish_kernel(rank, dof, count, *refs):
    mine_ref, other_ref, white_ref, var_ref, half_ref, rest_ref = refs[:6]
    terms, out_ref = refs[6 : 6 + count], refs[-1]
    mixed = jnp.dot(mine_ref[...], half_ref[...], precision=HI, preferred_element_type=F32)
    mixed = mixed + jnp.dot(other_ref[...], rest_ref[...], precision=HI, preferred_element_type=F32)
    white = mixed[:rank]
    pheno_var = mixed[rank : rank + 1] - jnp.sum(white * white, axis=0, keepdims=True)
    fitted = jnp.dot(white_ref[...], white, precision=HI, preferred_element_type=F32)
    cross = terms[0][...]
    for term in terms[1:]:
        cross = cross + term[...]
    cross = cross - fitted
    out_ref[...] = cross * dof * lax.rsqrt(var_ref[:, 0:1] * pheno_var - cross * cross)


def finish(done, total, start, tile, dof, mine, other, white, geno_var, half_rows, rest_rows, terms):
    rows, width = terms[0].shape
    rank = white.shape[1]
    first = start // tile
    whole = lambda a: pl.BlockSpec(a.shape, lambda j: (0, 0))
    block = lambda a: pl.BlockSpec((a.shape[0], tile), lambda j: (0, j))
    args = [mine, other, white, geno_var, half_rows, rest_rows, *terms]
    specs = [whole(a) for a in args[:4]] + [block(a) for a in args[4:]]
    aliases = {}
    if done is not None:
        aliases = {len(args): 0}
        args.append(done)
        specs.append(pl.BlockSpec(memory_space=pl.ANY))
    return pl.pallas_call(
        functools.partial(finish_kernel, rank, dof, len(terms)),
        grid=(width // tile,),
        out_shape=jax.ShapeDtypeStruct((rows, total), F32),
        in_specs=specs,
        out_specs=pl.BlockSpec((rows, tile), lambda j: (0, first + j)),
        input_output_aliases=aliases,
        compiler_params=pltpu.CompilerParams(vmem_limit_bytes=16 * 2**20),
        cost_estimate=pl.CostEstimate(
            flops=2 * 256 * 256 * width, bytes_accessed=16 * rows * width, transcendentals=rows * width
        ),
        name=f"finish_{start}",
    )(*args)


def chunk_widths(total, unit):
    units = total // unit
    if total % unit or units < 4:
        return [total]
    sizes = [2]
    left = units - 4
    while left > 0:
        sizes.append(min(4, left))
        left -= sizes[-1]
    sizes.append(2)
    return [size * unit for size in sizes]


def per_device(dosage, phenotype, covariates):
    devices = lax.axis_size("subj")
    chips = devices // 2
    subjects, snps = dosage.shape
    verts = phenotype.shape[1]
    covs = covariates.shape[1]
    rank = covs + 1
    rows = snps // devices
    half = round_up(covs + 2, 16) // 2
    split = chips * rows
    far = (chips - 1) * rows
    place_index = lax.axis_index("subj")
    core = lax.rem(place_index, 2)
    place = jnp.stack([place_index // 2, core]).astype(jnp.int32)
    sibling = [(i, i ^ 1) for i in range(devices)]

    def reduce_far(give, keep):
        got = lax.ppermute(give, "subj", sibling)
        near = keep[far:split] + got[far:split]
        own_half = keep[split:] + got[split:]
        terms = [near]
        halves = own_half
        for step in range(1, chips):
            low = (step - 1) * rows
            block = jnp.concatenate([keep[low : low + rows] + got[low : low + rows], own_half], axis=0)
            moves = [(i, (i + 2 * step) % devices) for i in range(devices)]
            came = lax.ppermute(block, "subj", moves)
            terms.append(came[:rows])
            halves = halves + came[rows:]
        rest = lax.ppermute(halves, "subj", sibling)
        return terms, halves, rest

    left, give, keep = prepare(place, dosage, covariates.T, chips, rows, half)
    terms, halves, rest = reduce_far(give, keep)
    own = sum(terms[1:], terms[0])
    low_half = jnp.where(core == 0, halves, rest)
    high_half = jnp.where(core == 0, rest, halves)
    gram = jnp.concatenate([low_half, high_half], axis=0)[:rank, :rank]
    factor = jnp.linalg.cholesky(gram)
    inverse = jax.scipy.linalg.solve_triangular(factor, jnp.eye(rank, dtype=F32), lower=True)
    white = jnp.dot(own[:, :rank], inverse.T, precision=HI)
    geno_var = own[:, rank] - jnp.sum(white * white, axis=1)
    geno_var = jnp.broadcast_to(geno_var[:, None], (rows, LANES))
    mixer = jnp.zeros((rank + 1, 2 * half), F32).at[:rank, :rank].set(inverse).at[rank, rank].set(1.0)
    mine = jnp.where(core == 0, mixer[:, :half], mixer[:, half:])
    other = jnp.where(core == 0, mixer[:, half:], mixer[:, :half])
    dof = float(subjects * devices - covs - 2) ** 0.5

    unit = 256
    out = None
    start = 0
    for width in chunk_widths(verts, unit):
        tile = unit if width % unit == 0 else LANES
        give, keep = product(place, left, phenotype, start, width, tile, split, half, rank)
        terms, halves, rest = reduce_far(give, keep)
        out = finish(out, verts, start, tile, dof, mine, other, white, geno_var, halves, rest, terms)
        start += width
    return out


def solution(mesh):
    in_specs = (P(("grp", "subj"), None), P(("grp", "subj"), "vert"), P(("grp", "subj"), None))
    out_specs = P(("grp", "subj"), "vert")
    return jax.shard_map(
        per_device, mesh=mesh, in_specs=in_specs, out_specs=out_specs, check_vma=False
    )
```

time: 247 us -> 164 us (0.66)
  matrix products: 99.5 us -> 0.51 us
  Pallas kernels: 0 us -> 49.9 us
  waiting for transfers between devices: 93 us -> 59.3 us
  local copies, waits for them, and re-layouts: 5.17 us -> 22.3 us
  blocking collectives: 13.4 us -> 0 us
  between operations: 13.5 us -> 0.38 us
  starting transfers between devices: 0.04 us -> 10.5 us
    dot_general x8 -> x1, matrix products: 94.6 us -> 0.28 us  [per_device(): white = jnp.dot(own[:, :rank], inverse.T, precision=HI)]
    reduce_scatter x1 -> x0, waiting for transfers between devices: 84.7 us -> none  [per_device(): lax.psum_scatter(partial_value, 'subj', scatter_dimension=0, tiled=True)]
    ppermute x0 -> x21, waiting for transfers between devices: none -> 59.3 us  [the longest x7 59.2 us: reduce_far(): came = lax.ppermute(block, 'subj', moves)]
    pallas_call x0 -> x13, Pallas kernels: none -> 49.9 us  [the longest x6 29.9 us: product(): pl.pallas_call(functools.partial(product_kernel, split, half, row), grid=...]
    unnamed x10 -> x33, local copies, waits for them, and re-layouts: 3.99 us -> 21.4 us
    psum x1 -> x0, blocking collectives: 13.4 us -> none  [per_device(): lax.psum((gram, design_geno, design_pheno, jnp.sum(geno * geno, axis=0),...]
    add x0 -> x22, other arithmetic: none -> 11.6 us  [the longest x6 5.47 us: reduce_far(): near = keep[far:split] + got[far:split]]
    ppermute x0 -> x21, starting transfers between devices: none -> 10.5 us  [the longest x7 7.41 us: reduce_far(): came = lax.ppermute(block, 'subj', moves)]
  transfers between devices with their start and end apart: 2 -> 21, of which waited for: 2 -> 6; matrix products, arithmetic and copies ran while one was open for 8% -> 13% of each run, Pallas kernels for 0% -> 25%
where the time goes in v1:
time: 164 us; the launch traced here: 163 us
  waiting for transfers between devices  59.3 us (36%)
  Pallas kernels  49.9 us (30%)
  local copies, waits for them, and re-layouts  22.3 us (14%)
  other arithmetic  20.4 us (12%)
  starting transfers between devices  10.5 us (6%)
    ppermute x7, waiting for transfers between devices, reduce_far(): came = lax.ppermute(block, 'subj', moves)  59.2 us
    pallas_call x6, Pallas kernels, product(): pl.pallas_call(functools.partial(product_kernel, split, half, row), grid=...  29.9 us
    unnamed x33, local copies, waits for them, and re-layouts  21.4 us
    pallas_call x6, Pallas kernels, finish(): pl.pallas_call(functools.partial(finish_kernel, rank, dof, len(terms)), g...  16.4 us
    ppermute x7, starting transfers between devices, reduce_far(): came = lax.ppermute(block, 'subj', moves)  7.41 us
    add x6, other arithmetic, reduce_far(): near = keep[far:split] + got[far:split]  5.47 us
    another operation x3, other arithmetic, per_device(): factor = jnp.linalg.cholesky(gram)  4.47 us
    add x7, other arithmetic, reduce_far(): own_half = keep[split:] + got[split:]  4.27 us
  transfers between devices with their start and end apart: 21, of which 6 were waited for; matrix products, arithmetic and copies ran while one was open for 13% of the time, Pallas kernels for 25%

profile of v1, /device:TPU:0, one launch (start us, length us, event | category | flops | bytes accessed | tf_op | source)
XLA Modules:
  0.0 163.3 jit_solution(17081746453035662656)
XLA Ops:
  0.1 1.6 copy-done.12
  1.7 1.0 copy-done.15
  2.6 3.6 %prepare.1 = (bf16[656,2048]{1,0:T(8,128)(2,1)S(1)}, f32[280,128]{1,0:T(8,128)S(1)}, f32[280,128]{1,0:T(8,128)S(1)}) custom-call(s32[2]{0:T(128)S(1)} %pad_add_fusion.place_ref, bf16[2048,512]{1,0:T(8,128)(2,1)S(1)} %copy-done.12, f32[40,2048]{1,0:T(8,128)S(1)} %bitcast.14), custom_call_target="tpu_custom_call" | custom-call | flops 2147483648 | bytes 4194304 | tf_op jit(solution)/shard_map/prepare/pallas_call | solution.py:67
  6.2 7.0 %copy-done = bf16[2048,5120]{1,0:T(8,128)(2,1)S(1)} copy-done((bf16[2048,5120]{1,0:T(8,128)(2,1)S(1)}, bf16[2048,5120]{1,0:T(8,128)(2,1)}, u32[]{:S(2)}) %copy-start) | copy-done | bytes 20971544
  13.2 3.2 %product_0.1 = (f32[280,512]{1,0:T(8,128)}, f32[280,512]{1,0:T(8,128)S(1)}) custom-call(s32[2]{0:T(128)S(1)} %pad_add_fusion.place_ref, bf16[656,2048]{1,0:T(8,128)(2,1)S(1)} %get-tuple-element.46.left_ref, bf16[2048,5120]{1,0:T(8,128)(2,1)S(1)} %copy-done), custom_call_target="tpu_custom_call" | custom-call | flops 1375731712 | bytes 3145728 | tf_op jit(solution)/shard_map/product_0/pallas_call | solution.py:102
  16.4 0.5 collective-permute-start.18
  16.9 6.1 %product_512.1 = (f32[280,1024]{1,0:T(8,128)}, f32[280,1024]{1,0:T(8,128)S(1)}) custom-call(s32[2]{0:T(128)S(1)} %pad_add_fusion.place_ref, bf16[656,2048]{1,0:T(8,128)(2,1)S(1)} %get-tuple-element.46.left_ref, bf16[2048,5120]{1,0:T(8,128)(2,1)} %pheno_ref.11), custom_call_target="tpu_custom_call" | custom-call | flops 2751463424 | bytes 6291456 | tf_op jit(solution)/shard_map/product_512/pallas_call | solution.py:102
  23.0 1.0 copy-done.8
  24.0 0.5 collective-permute-start.15
  24.5 6.1 %product_1536.1 = (f32[280,1024]{1,0:T(8,128)}, f32[280,1024]{1,0:T(8,128)S(1)}) custom-call(s32[2]{0:T(128)S(1)} %pad_add_fusion.place_ref, bf16[656,2048]{1,0:T(8,128)(2,1)S(1)} %get-tuple-element.46.left_ref, bf16[2048,5120]{1,0:T(8,128)(2,1)} %pheno_ref.11), custom_call_target="tpu_custom_call" | custom-call | flops 2751463424 | bytes 6291456 | tf_op jit(solution)/shard_map/product_1536/pallas_call | solution.py:102
  30.6 1.1 copy-done.6
  31.6 6.1 %product_2560.1 = (f32[280,1024]{1,0:T(8,128)}, f32[280,1024]{1,0:T(8,128)S(1)}) custom-call(s32[2]{0:T(128)S(1)} %pad_add_fusion.place_ref, bf16[656,2048]{1,0:T(8,128)(2,1)S(1)} %get-tuple-element.46.left_ref, bf16[2048,5120]{1,0:T(8,128)(2,1)} %pheno_ref.11), custom_call_target="tpu_custom_call" | custom-call | flops 2751463424 | bytes 6291456 | tf_op jit(solution)/shard_map/product_2560/pallas_call | solution.py:102
  37.7 1.0 copy-done.4
  38.7 0.5 collective-permute-start.9
  39.2 6.0 %product_3584.1 = (f32[280,1024]{1,0:T(8,128)}, f32[280,1024]{1,0:T(8,128)S(1)}) custom-call(s32[2]{0:T(128)S(1)} %pad_add_fusion.place_ref, bf16[656,2048]{1,0:T(8,128)(2,1)S(1)} %get-tuple-element.46.left_ref, bf16[2048,5120]{1,0:T(8,128)(2,1)} %pheno_ref.11), custom_call_target="tpu_custom_call" | custom-call | flops 2751463424 | bytes 6291456 | tf_op jit(solution)/shard_map/product_3584/pallas_call | solution.py:102
  45.2 0.9 slice_add_fusion.22
  46.1 0.7 slice_add_fusion.28
  46.8 2.6 %collective-permute-start.1 = (f32[152,128]{1,0:T(8,128)S(1)}, f32[152,128]{1,0:T(8,128)S(1)}, u32[]{:S(2)}, u32[]{:S(2)}) collective-permute-start(f32[152,128]{1,0:T(8,128)S(1)} %pad_maximum_fusion.6), channel_id=1, source_target_pairs={{0,8},{4,12},{8,0},{12,4},{1,9},{5,13},{9,1},{13,5},{2,10},{6,14},... | collective-permute-start | bytes 233480 | tf_op jit(solution)/shard_map/ppermute | solution.py:208
  49.4 7.0 %copy-done.1 = bf16[2048,5120]{1,0:T(8,128)(2,1)S(1)} copy-done((bf16[2048,5120]{1,0:T(8,128)(2,1)S(1)}, bf16[2048,5120]{1,0:T(8,128)(2,1)}, u32[]{:S(2)}) %copy-start.1) | copy-done | bytes 20971544
  56.4 2.5 %product_4608.1 = (f32[280,512]{1,0:T(8,128)S(1)}, f32[280,512]{1,0:T(8,128)S(1)}) custom-call(s32[2]{0:T(128)S(1)} %pad_add_fusion.place_ref, bf16[656,2048]{1,0:T(8,128)(2,1)S(1)} %get-tuple-element.46.left_ref, bf16[2048,5120]{1,0:T(8,128)(2,1)S(1)} %copy-done.1), custom_call_target="tpu_custom_call" | custom-call | flops 1375731712 | bytes 3145728 | tf_op jit(solution)/shard_map/product_4608/pallas_call | solution.py:102
  58.9 0.8 copy-done.10
  59.7 0.8 copy-done.13
  60.6 0.3 collective-permute-start.2
  60.9 0.9 slice_add_fusion.20
  61.7 0.1 collective-permute-done.2
  61.8 0.3 collective-permute-start.6
  62.1 0.1 copy.41
  62.2 3.7 %cholesky.17 = f32[41,41]{1,0:T(8,128)S(1)} custom-call(f32[41,41]{1,0:T(8,128)S(1)} %fusion.6), custom_call_target="Cholesky" | custom-call | tf_op jit(solution)/shard_map/jit(cholesky)/cholesky | solution.py:220
  66.0 0.7 compare_reduce_fusion
  66.7 0.6 fusion.3
  67.3 3.1 %custom-call.7 = f32[1,41,41]{1,2,0:T(8,128)S(1)} custom-call(f32[1,41,41]{2,1,0:T(8,128)S(1)} %fusion.3), custom_call_target="InvertDiagBlocksLowerTriangular" | custom-call | tf_op jit(solution)/shard_map/jit(_solve_triangular)/triangular_solve | solution.py:221
  70.4 0.2 fusion.4
  70.8 0.3 multiply_reduce_fusion
  71.0 0.1 copy.34
  71.2 0.1 copy.40.refs_2_
  71.3 0.3 scatter.9
  71.6 0.2 fusion
  71.9 0.3 collective-permute-start.3
  72.2 1.2 slice_add_fusion.8
  73.4 0.8 slice_add_fusion.24
  74.2 0.3 collective-permute-start.19
  74.7 9.1 %collective-permute-done.19 = f32[152,512]{1,0:T(8,128)S(1)} collective-permute-done((f32[152,512]{1,0:T(8,128)S(1)}, f32[152,512]{1,0:T(8,128)S(1)}, u32[]{:S(2)}, u32[]{:S(2)}) %collective-permute-start.19) | collective-permute-done | bytes 311328 | tf_op jit(solution)/shard_map/ppermute | solution.py:208
  83.8 0.3 collective-permute-start.4
  84.2 0.9 slice_add_fusion.13
  85.1 1.4 slice_add_fusion
  86.5 1.8 %collective-permute-start.16 = (f32[152,1024]{1,0:T(8,128)S(1)}, f32[152,1024]{1,0:T(8,128)S(1)}, u32[]{:S(2)}, u32[]{:S(2)}) collective-permute-start(f32[152,1024]{1,0:T(8,128)S(1)} %pad_maximum_fusion.3), channel_id=1, source_target_pairs={{0,8},{4,12},{8,0},{12,4},{1,9},{5,13},{9,1},{13,5},{2,10},{6,14},... | collective-permute-start | bytes 1867784 | tf_op jit(solution)/shard_map/ppermute | solution.py:208
  88.4 0.9 slice_add_fusion.15
  89.3 1.4 slice_add_fusion.2
  90.7 1.2 collective-permute-start.13
  91.9 0.9 slice_add_fusion.17
  92.8 1.4 slice_add_fusion.4
  94.2 1.2 collective-permute-start.10
  95.4 0.2 slice_add_fusion.6
  95.6 11.7 %collective-permute-done.16 = f32[152,1024]{1,0:T(8,128)S(1)} collective-permute-done((f32[152,1024]{1,0:T(8,128)S(1)}, f32[152,1024]{1,0:T(8,128)S(1)}, u32[]{:S(2)}, u32[]{:S(2)}) %collective-permute-start.16) | collective-permute-done | bytes 622624 | tf_op jit(solution)/shard_map/ppermute | solution.py:208
  107.5 13.3 %collective-permute-done.13 = f32[152,1024]{1,0:T(8,128)S(1)} collective-permute-done((f32[152,1024]{1,0:T(8,128)S(1)}, f32[152,1024]{1,0:T(8,128)S(1)}, u32[]{:S(2)}, u32[]{:S(2)}) %collective-permute-start.13) | collective-permute-done | bytes 622624 | tf_op jit(solution)/shard_map/ppermute | solution.py:208
  120.7 13.3 %collective-permute-done.10 = f32[152,1024]{1,0:T(8,128)S(1)} collective-permute-done((f32[152,1024]{1,0:T(8,128)S(1)}, f32[152,1024]{1,0:T(8,128)S(1)}, u32[]{:S(2)}, u32[]{:S(2)}) %collective-permute-start.10) | collective-permute-done | bytes 622624 | tf_op jit(solution)/shard_map/ppermute | solution.py:208
  134.1 11.8 %collective-permute-done.7 = f32[152,1024]{1,0:T(8,128)S(1)} collective-permute-done((f32[152,1024]{1,0:T(8,128)S(1)}, f32[152,1024]{1,0:T(8,128)S(1)}, u32[]{:S(2)}, u32[]{:S(2)}) %collective-permute-start.7) | collective-permute-done | bytes 622624 | tf_op jit(solution)/shard_map/ppermute | solution.py:208
  145.9 0.6 collective-permute-start.8
  146.7 1.9 %finish_0.1.refs_8_ = f32[128,5120]{1,0:T(8,128)} custom-call(f32[42,24]{1,0:T(8,128)S(1)} %get-tuple-element.72.refs_0_, f32[42,24]{1,0:T(8,128)S(1)} %get-tuple-element.71.refs_1_, f32[128,41]{1,0:T(8,128)S(1)} %copy.40.refs_2_, f32[128,128]{1,0:T(8,128)S(1)} %broadcast_in_dim.12.refs_3_, f32[24,512]{1,0:T(8,128)S(1)} %slice_add_fusion.23.refs_4_, ...), custom_call_target="tpu_custom_call" | custom-call | flops 67108864 | bytes 1048576 | tf_op jit(solution)/shard_map/finish_0/pallas_call | solution.py:154
  148.8 3.2 %finish_512.1.refs_8_ = f32[128,5120]{1,0:T(8,128)} custom-call(f32[42,24]{1,0:T(8,128)S(1)} %get-tuple-element.72.refs_0_, f32[42,24]{1,0:T(8,128)S(1)} %get-tuple-element.71.refs_1_, f32[128,41]{1,0:T(8,128)S(1)} %copy.40.refs_2_, f32[128,128]{1,0:T(8,128)S(1)} %broadcast_in_dim.12.refs_3_, ...), custom_call_target="tpu_custom_call", output_to_operand_aliasing={{}: (8, {})} | custom-call | flops 134217728 | bytes 2097152 | tf_op jit(solution)/shard_map/finish_512/pallas_call | solution.py:154
  151.9 3.1 %finish_1536.1.refs_8_ = f32[128,5120]{1,0:T(8,128)} custom-call(f32[42,24]{1,0:T(8,128)S(1)} %get-tuple-element.72.refs_0_, f32[42,24]{1,0:T(8,128)S(1)} %get-tuple-element.71.refs_1_, f32[128,41]{1,0:T(8,128)S(1)} %copy.40.refs_2_, f32[128,128]{1,0:T(8,128)S(1)} %broadcast_in_dim.12.refs_3_, ...), custom_call_target="tpu_custom_call", output_to_operand_aliasing={{}: (8, {})} | custom-call | flops 134217728 | bytes 2097152 | tf_op jit(solution)/shard_map/finish_1536/pallas_call | solution.py:154
  155.1 3.1 %finish_2560.1.refs_8_ = f32[128,5120]{1,0:T(8,128)} custom-call(f32[42,24]{1,0:T(8,128)S(1)} %get-tuple-element.72.refs_0_, f32[42,24]{1,0:T(8,128)S(1)} %get-tuple-element.71.refs_1_, f32[128,41]{1,0:T(8,128)S(1)} %copy.40.refs_2_, f32[128,128]{1,0:T(8,128)S(1)} %broadcast_in_dim.12.refs_3_, ...), custom_call_target="tpu_custom_call", output_to_operand_aliasing={{}: (8, {})} | custom-call | flops 134217728 | bytes 2097152 | tf_op jit(solution)/shard_map/finish_2560/pallas_call | solution.py:154
  158.2 3.1 %finish_3584.1.refs_8_ = f32[128,5120]{1,0:T(8,128)} custom-call(f32[42,24]{1,0:T(8,128)S(1)} %get-tuple-element.72.refs_0_, f32[42,24]{1,0:T(8,128)S(1)} %get-tuple-element.71.refs_1_, f32[128,41]{1,0:T(8,128)S(1)} %copy.40.refs_2_, f32[128,128]{1,0:T(8,128)S(1)} %broadcast_in_dim.12.refs_3_, ...), custom_call_target="tpu_custom_call", output_to_operand_aliasing={{}: (8, {})} | custom-call | flops 134217728 | bytes 2097152 | tf_op jit(solution)/shard_map/finish_3584/pallas_call | solution.py:154
  161.4 1.9 %finish_4608.1 = f32[128,5120]{1,0:T(8,128)} custom-call(f32[42,24]{1,0:T(8,128)S(1)} %get-tuple-element.72.refs_0_, f32[42,24]{1,0:T(8,128)S(1)} %get-tuple-element.71.refs_1_, f32[128,41]{1,0:T(8,128)S(1)} %copy.40.refs_2_, f32[128,128]{1,0:T(8,128)S(1)} %broadcast_in_dim.12.refs_3_, ...), custom_call_target="tpu_custom_call", output_to_operand_aliasing={{}: (8, {})} | custom-call | flops 67108864 | bytes 1048576 | tf_op jit(solution)/shard_map/finish_4608/pallas_call | solution.py:154
  (78 shorter events, 1.4 us)
Async XLA Ops:
  0.1 1.6 copy-start.12
  1.7 1.0 copy-start.15
  6.2 7.0 %copy-start = (bf16[2048,5120]{1,0:T(8,128)(2,1)S(1)}, bf16[2048,5120]{1,0:T(8,128)(2,1)}, u32[]{:S(2)}) copy-start(bf16[2048,5120]{1,0:T(8,128)(2,1)} %pheno_ref.11) | copy-start | bytes 62914564
  16.4 55.4 %collective-permute-start.18 = (f32[280,512]{1,0:T(8,128)}, f32[280,512]{1,0:T(8,128)}, u32[]{:S(2)}, u32[]{:S(2)}) collective-permute-start(f32[280,512]{1,0:T(8,128)} %get-tuple-element.58), channel_id=1, source_target_pairs={{0,4},{4,0},{8,12},{12,8},{1,5},{5,1},{9,13},{13,9},{2,6},{6,2},{1... | collective-permute-start | bytes 1720328 | tf_op jit(solution)/shard_map/ppermute | solution.py:199
  16.9 28.3 %collective-permute-start = (f32[280,128]{1,0:T(8,128)S(1)}, f32[280,128]{1,0:T(8,128)}, u32[]{:S(2)}, u32[]{:S(2)}) collective-permute-start(f32[280,128]{1,0:T(8,128)S(1)} %get-tuple-element.45), channel_id=1, source_target_pairs={{0,4},{4,0},{8,12},{12,8},{1,5},{5,1},{9,13},{13,9},{2,6},{6,2},{1... | collective-permute-start | bytes 430088 | tf_op jit(solution)/shard_map/ppermute | solution.py:199
  23.0 1.0 copy-start.8
  24.0 60.1 %collective-permute-start.15 = (f32[280,1024]{1,0:T(8,128)}, f32[280,1024]{1,0:T(8,128)}, u32[]{:S(2)}, u32[]{:S(2)}) collective-permute-start(f32[280,1024]{1,0:T(8,128)} %get-tuple-element.56), channel_id=1, source_target_pairs={{0,4},{4,0},{8,12},{12,8},{1,5},{5,1},{9,13},{13,9},{2,6},{6,2},{1... | collective-permute-start | bytes 3440648 | tf_op jit(solution)/shard_map/ppermute | solution.py:199
  30.6 1.1 copy-start.6
  31.6 54.9 %collective-permute-start.12 = (f32[280,1024]{1,0:T(8,128)}, f32[280,1024]{1,0:T(8,128)}, u32[]{:S(2)}, u32[]{:S(2)}) collective-permute-start(f32[280,1024]{1,0:T(8,128)} %get-tuple-element.54), channel_id=1, source_target_pairs={{0,4},{4,0},{8,12},{12,8},{1,5},{5,1},{9,13},{13,9},{2,6},{6,2},{1... | collective-permute-start | bytes 3440648 | tf_op jit(solution)/shard_map/ppermute | solution.py:199
  37.7 1.0 copy-start.4
  38.7 52.0 %collective-permute-start.9 = (f32[280,1024]{1,0:T(8,128)}, f32[280,1024]{1,0:T(8,128)}, u32[]{:S(2)}, u32[]{:S(2)}) collective-permute-start(f32[280,1024]{1,0:T(8,128)} %get-tuple-element.52), channel_id=1, source_target_pairs={{0,4},{4,0},{8,12},{12,8},{1,5},{5,1},{9,13},{13,9},{2,6},{6,2},{1... | collective-permute-start | bytes 3440648 | tf_op jit(solution)/shard_map/ppermute | solution.py:199
  45.2 13.7 %copy-start.2 = (f32[280,1024]{1,0:T(8,128)}, f32[280,1024]{1,0:T(8,128)S(1)}, u32[]{:S(2)}) copy-start(f32[280,1024]{1,0:T(8,128)S(1)} %get-tuple-element.49) | copy-start | bytes 3440644
  46.8 13.7 %collective-permute-start.1 = (f32[152,128]{1,0:T(8,128)S(1)}, f32[152,128]{1,0:T(8,128)S(1)}, u32[]{:S(2)}, u32[]{:S(2)}) collective-permute-start(f32[152,128]{1,0:T(8,128)S(1)} %pad_maximum_fusion.6), channel_id=1, source_target_pairs={{0,8},{4,12},{8,0},{12,4},{1,9},{5,13},{9,1},{13,5},{2,10},{6,14},... | collective-permute-start | bytes 233480 | tf_op jit(solution)/shard_map/ppermute | solution.py:208
  49.4 7.0 %copy-start.1 = (bf16[2048,5120]{1,0:T(8,128)(2,1)S(1)}, bf16[2048,5120]{1,0:T(8,128)(2,1)}, u32[]{:S(2)}) copy-start(bf16[2048,5120]{1,0:T(8,128)(2,1)} %pheno_ref.11) | copy-start | bytes 62914564
  58.9 0.8 copy-start.10
  59.7 0.8 copy-start.13
  60.6 11.3 %copy-start.14 = (f32[280,512]{1,0:T(8,128)S(1)}, f32[280,512]{1,0:T(8,128)}, u32[]{:S(2)}) copy-start(f32[280,512]{1,0:T(8,128)} %copy-done.13) | copy-start | bytes 1720324
  60.6 1.2 collective-permute-start.2
  61.8 32.4 %collective-permute-start.6 = (f32[280,1024]{1,0:T(8,128)}, f32[280,1024]{1,0:T(8,128)S(1)}, u32[]{:S(2)}, u32[]{:S(2)}) collective-permute-start(f32[280,1024]{1,0:T(8,128)} %get-tuple-element.50), channel_id=1, source_target_pairs={{0,4},{4,0},{8,12},{12,8},{1,5},{5,1},{9,13},{13,9},{2,6},{6,2},{1... | collective-permute-start | bytes 3440648 | tf_op jit(solution)/shard_map/ppermute | solution.py:199
  71.9 2.3 %collective-permute-start.3 = (f32[280,512]{1,0:T(8,128)S(1)}, f32[280,512]{1,0:T(8,128)S(1)}, u32[]{:S(2)}, u32[]{:S(2)}) collective-permute-start(f32[280,512]{1,0:T(8,128)S(1)} %copy-done.14), channel_id=1, source_target_pairs={{0,4},{4,0},{8,12},{12,8},{1,5},{5,1},{9,13},{13,9},{2,6},{6,2},{1... | collective-permute-start | bytes 1720328 | tf_op jit(solution)/shard_map/ppermute | solution.py:199
  72.2 2.4 %copy-start.11 = (f32[280,512]{1,0:T(8,128)S(1)}, f32[280,512]{1,0:T(8,128)}, u32[]{:S(2)}) copy-start(f32[280,512]{1,0:T(8,128)} %copy-done.10) | copy-start | bytes 1720324
  74.2 9.6 %collective-permute-start.19 = (f32[152,512]{1,0:T(8,128)S(1)}, f32[152,512]{1,0:T(8,128)S(1)}, u32[]{:S(2)}, u32[]{:S(2)}) collective-permute-start(f32[152,512]{1,0:T(8,128)S(1)} %pad_maximum_fusion.5), channel_id=1, source_target_pairs={{0,8},{4,12},{8,0},{12,4},{1,9},{5,13},{9,1},{13,5},{2,10},{6,14},... | collective-permute-start | bytes 933896 | tf_op jit(solution)/shard_map/ppermute | solution.py:208
  74.6 9.6 %copy-start.9 = (f32[280,1024]{1,0:T(8,128)S(1)}, f32[280,1024]{1,0:T(8,128)}, u32[]{:S(2)}) copy-start(f32[280,1024]{1,0:T(8,128)} %copy-done.8) | copy-start | bytes 3440644
  83.8 62.1 %collective-permute-start.4 = (f32[152,512]{1,0:T(8,128)S(1)}, f32[152,512]{1,0:T(8,128)S(1)}, u32[]{:S(2)}, u32[]{:S(2)}) collective-permute-start(f32[152,512]{1,0:T(8,128)S(1)} %pad_maximum_fusion.4), channel_id=1, source_target_pairs={{0,8},{4,12},{8,0},{12,4},{1,9},{5,13},{9,1},{13,5},{2,10},{6,14},... | collective-permute-start | bytes 933896 | tf_op jit(solution)/shard_map/ppermute | solution.py:208
  84.1 62.4 %collective-permute-start.20 = (f32[24,512]{1,0:T(8,128)S(1)}, f32[24,512]{1,0:T(8,128)S(1)}, u32[]{:S(2)}, u32[]{:S(2)}) collective-permute-start(f32[24,512]{1,0:T(8,128)S(1)} %slice_add_fusion.23.refs_4_), channel_id=1, source_target_pairs={{0,4},{4,0},{8,12},{12,8},{1,5},{5,1},{9,13},{13,9},{2,6},{6,2},{1... | collective-permute-start | bytes 147464 | tf_op jit(solution)/shard_map/ppermute | solution.py:211
  86.5 1.9 %copy-start.7 = (f32[280,1024]{1,0:T(8,128)S(1)}, f32[280,1024]{1,0:T(8,128)}, u32[]{:S(2)}) copy-start(f32[280,1024]{1,0:T(8,128)} %copy-done.6) | copy-start | bytes 3440644
  86.5 20.8 %collective-permute-start.16 = (f32[152,1024]{1,0:T(8,128)S(1)}, f32[152,1024]{1,0:T(8,128)S(1)}, u32[]{:S(2)}, u32[]{:S(2)}) collective-permute-start(f32[152,1024]{1,0:T(8,128)S(1)} %pad_maximum_fusion.3), channel_id=1, source_target_pairs={{0,8},{4,12},{8,0},{12,4},{1,9},{5,13},{9,1},{13,5},{2,10},{6,14},... | collective-permute-start | bytes 1867784 | tf_op jit(solution)/shard_map/ppermute | solution.py:208
  90.6 1.3 copy-start.5
  90.7 30.0 %collective-permute-start.13 = (f32[152,1024]{1,0:T(8,128)S(1)}, f32[152,1024]{1,0:T(8,128)S(1)}, u32[]{:S(2)}, u32[]{:S(2)}) collective-permute-start(f32[152,1024]{1,0:T(8,128)S(1)} %pad_maximum_fusion.2), channel_id=1, source_target_pairs={{0,8},{4,12},{8,0},{12,4},{1,9},{5,13},{9,1},{13,5},{2,10},{6,14},... | collective-permute-start | bytes 1867784 | tf_op jit(solution)/shard_map/ppermute | solution.py:208
  94.1 1.3 copy-start.3
  94.2 39.8 %collective-permute-start.10 = (f32[152,1024]{1,0:T(8,128)S(1)}, f32[152,1024]{1,0:T(8,128)S(1)}, u32[]{:S(2)}, u32[]{:S(2)}) collective-permute-start(f32[152,1024]{1,0:T(8,128)S(1)} %pad_maximum_fusion.1), channel_id=1, source_target_pairs={{0,8},{4,12},{8,0},{12,4},{1,9},{5,13},{9,1},{13,5},{2,10},{6,14},... | collective-permute-start | bytes 1867784 | tf_op jit(solution)/shard_map/ppermute | solution.py:208
  107.4 38.5 %collective-permute-start.7 = (f32[152,1024]{1,0:T(8,128)S(1)}, f32[152,1024]{1,0:T(8,128)S(1)}, u32[]{:S(2)}, u32[]{:S(2)}) collective-permute-start(f32[152,1024]{1,0:T(8,128)S(1)} %pad_maximum_fusion), channel_id=1, source_target_pairs={{0,8},{4,12},{8,0},{12,4},{1,9},{5,13},{9,1},{13,5},{2,10},{6,14},... | collective-permute-start | bytes 1867784 | tf_op jit(solution)/shard_map/ppermute | solution.py:208
  120.7 28.1 %collective-permute-start.17 = (f32[24,1024]{1,0:T(8,128)S(1)}, f32[24,1024]{1,0:T(8,128)S(1)}, u32[]{:S(2)}, u32[]{:S(2)}) collective-permute-start(f32[24,1024]{1,0:T(8,128)S(1)} %slice_add_fusion.12.refs_4_), channel_id=1, source_target_pairs={{0,4},{4,0},{8,12},{12,8},{1,5},{5,1},{9,13},{13,9},{2,6},{6,2},{1... | collective-permute-start | bytes 294920 | tf_op jit(solution)/shard_map/ppermute | solution.py:211
  134.1 17.9 %collective-permute-start.14 = (f32[24,1024]{1,0:T(8,128)S(1)}, f32[24,1024]{1,0:T(8,128)S(1)}, u32[]{:S(2)}, u32[]{:S(2)}) collective-permute-start(f32[24,1024]{1,0:T(8,128)S(1)} %slice_add_fusion.14.refs_4_), channel_id=1, source_target_pairs={{0,4},{4,0},{8,12},{12,8},{1,5},{5,1},{9,13},{13,9},{2,6},{6,2},{1... | collective-permute-start | bytes 294920 | tf_op jit(solution)/shard_map/ppermute | solution.py:211
  145.8 9.3 %collective-permute-start.11 = (f32[24,1024]{1,0:T(8,128)S(1)}, f32[24,1024]{1,0:T(8,128)S(1)}, u32[]{:S(2)}, u32[]{:S(2)}) collective-permute-start(f32[24,1024]{1,0:T(8,128)S(1)} %slice_add_fusion.16.refs_4_), channel_id=1, source_target_pairs={{0,4},{4,0},{8,12},{12,8},{1,5},{5,1},{9,13},{13,9},{2,6},{6,2},{1... | collective-permute-start | bytes 294920 | tf_op jit(solution)/shard_map/ppermute | solution.py:211
  145.9 12.4 %collective-permute-start.8 = (f32[24,1024]{1,0:T(8,128)S(1)}, f32[24,1024]{1,0:T(8,128)S(1)}, u32[]{:S(2)}, u32[]{:S(2)}) collective-permute-start(f32[24,1024]{1,0:T(8,128)S(1)} %slice_add_fusion.18.refs_4_), channel_id=1, source_target_pairs={{0,4},{4,0},{8,12},{12,8},{1,5},{5,1},{9,13},{13,9},{2,6},{6,2},{1... | collective-permute-start | bytes 294920 | tf_op jit(solution)/shard_map/ppermute | solution.py:211
  146.5 14.9 %collective-permute-start.5 = (f32[24,512]{1,0:T(8,128)S(1)}, f32[24,512]{1,0:T(8,128)S(1)}, u32[]{:S(2)}, u32[]{:S(2)}) collective-permute-start(f32[24,512]{1,0:T(8,128)S(1)} %slice_add_fusion.25.refs_4_), channel_id=1, source_target_pairs={{0,4},{4,0},{8,12},{12,8},{1,5},{5,1},{9,13},{13,9},{2,6},{6,2},{1... | collective-permute-start | bytes 147464 | tf_op jit(solution)/shard_map/ppermute | solution.py:211

commit v2 on v0

v2 whole, which is shorter than its diff:
```python
import functools

import jax
import jax.numpy as jnp
from jax import lax
from jax.experimental import pallas as pl
from jax.experimental.pallas import tpu as pltpu
from jax.sharding import PartitionSpec as P


HI = lax.Precision.HIGHEST
F32 = jnp.float32
BF16 = jnp.bfloat16
LANES = 128
TILE = 512
STRIP = 256
SQUARE = 1
OPEN_LIMIT = 20 * 2**20
LIMIT = 12 * 2**20
PIECES = 4
LAST = (((1,), (1,)), ((), ()))


def round_up(value, unit):
    return -(-value // unit) * unit


def split_three(values):
    upper = values.astype(BF16)
    rest = values - upper.astype(F32)
    middle = rest.astype(BF16)
    lower = (rest - middle.astype(F32)).astype(BF16)
    return upper, middle, lower


def block_copies(source, target, sems, first, axis):
    count = PIECES if axis == 0 else max(target.shape[1] // STRIP, 1)
    step = target.shape[axis] // count
    copies = []
    for i in range(count):
        part = (slice(i * step, (i + 1) * step), slice(None))[:: 1 if axis == 0 else -1]
        copies.append(pltpu.make_async_copy(source.at[part], target.at[part], sems.at[first + i]))
    return copies


def column_block(ref, start, width):
    return ref.at[:, start : start + width]


def multiply(left_ref, pheno_ref, copies, outs, small, core, rows, half):
    give_far, give_near, keep_far, keep_near = outs
    width = give_far.shape[1]
    far = give_far.shape[0] - half
    split = far + rows
    step = min(STRIP, width) if copies else min(TILE, width)
    for low in range(0, width, step):
        high = low + step
        if copies:
            copies[low // step].wait()
        pheno = pheno_ref[:, low:high]
        result = jnp.dot(left_ref[...], pheno, preferred_element_type=F32)
        give_far[0:far, low:high] = result[:far]
        give_near[:, low:high] = result[far:split]
        keep_far[0:far, low:high] = result[split : split + far]
        keep_near[:, low:high] = result[split + far : 2 * split]
        upper = result[2 * split : 2 * split + 2 * half]
        middle = result[2 * split + 2 * half : 2 * split + 4 * half]
        lower = result[2 * split + 4 * half :]
        wide = pheno.astype(F32)
        square = jnp.sum(wide * wide, axis=0, keepdims=True)
        place = lax.broadcasted_iota(jnp.int32, upper.shape, 0)
        small[:, low:high] = jnp.where(place == SQUARE, square, (lower + middle) + upper)
    give_far[far:, :] = small[pl.ds(pl.multiple_of((1 - core) * half, half), half), :]
    keep_far[far:, :] = small[pl.ds(pl.multiple_of(core * half, half), half), :]


def part_shapes(chips, rows, half, width):
    far = jax.ShapeDtypeStruct(((chips - 1) * rows + half, width), F32)
    near = jax.ShapeDtypeStruct((rows, width), F32)
    return (far, near, far, near)


def with_design(left_ref, geno, outs, small, core, place, half):
    give_far, _, keep_far, _ = outs
    far = give_far.shape[0] - half
    snps = geno.shape[1]
    size = 2 * half
    design = left_ref[snps:, :]
    product = jnp.dot(design, geno[...], preferred_element_type=F32)
    product = (product[2 * size :] + product[size : 2 * size]) + product[:size]
    wide = geno[...].astype(F32)
    square = jnp.sum(wide * wide, axis=0, keepdims=True)
    row = lax.broadcasted_iota(jnp.int32, (size, snps), 0)
    product = jnp.where(row == SQUARE, square, product)
    product = jnp.concatenate([product, jnp.zeros((LANES - size, snps), F32)], axis=0)
    place[...] = product.T
    gram = lax.dot_general(design, design, LAST, preferred_element_type=F32)
    total = jnp.zeros((size, size), F32)
    for tall, flat in ((2, 0), (0, 2), (1, 1), (1, 0), (0, 1), (0, 0)):
        total = total + gram[tall * size : (tall + 1) * size, flat * size : (flat + 1) * size]
    small[:, 0:LANES] = jnp.concatenate([total, jnp.zeros((size, LANES - size), F32)], axis=1)
    give_far[far:, :] = small[pl.ds(pl.multiple_of((1 - core) * half, half), half), 0:LANES]
    keep_far[far:, :] = small[pl.ds(pl.multiple_of(core * half, half), half), 0:LANES]


def open_kernel(chips, rows, half, widths, place_ref, geno_ref, cov_ref, pheno_ref, *refs):
    left_ref, base, outs = refs[0], refs[1:5], refs[5:9]
    ahead_refs = refs[9:-7]
    geno, turned, design, first, small, table, sems = refs[-7:]
    chip, core = place_ref[0], place_ref[1]
    covs, subjects = cov_ref.shape
    snps = 2 * chips * rows
    cov_copy = pltpu.make_async_copy(cov_ref, design.at[8 : 8 + covs], sems.at[0])
    cov_copy.start()
    geno_copies = block_copies(geno_ref, geno, sems, 1, 0)
    first_copies = block_copies(column_block(pheno_ref, 0, widths[0]), first, sems, 1 + PIECES, 1)
    used = 1 + PIECES + len(first_copies)
    ahead_copies = []
    start = widths[0]
    for index, ahead_ref in enumerate(ahead_refs):
        block = column_block(pheno_ref, start, ahead_ref.shape[1])
        ahead_copies += block_copies(block, ahead_ref, sems, used + index * PIECES, 0)
        start += ahead_ref.shape[1]
    for copy in geno_copies + first_copies + ahead_copies:
        copy.start()
    top = lax.broadcasted_iota(jnp.int32, (8, subjects), 0)
    design[0:8, :] = jnp.where(top == 0, 1.0, 0.0)
    if 2 * half > 8 + covs:
        design[8 + covs :, :] = jnp.zeros((2 * half - 8 - covs, subjects), F32)
    cov_copy.wait()
    for index, part in enumerate(split_three(design[...])):
        left_ref[snps + index * 2 * half : snps + (index + 1) * 2 * half, :] = part
    step = subjects // PIECES
    for index, copy in enumerate(geno_copies):
        copy.wait()
        turned[:, index * step : (index + 1) * step] = geno[index * step : (index + 1) * step, :].T
    with_design(left_ref, geno, base, small, core, table, half)
    for slot in range(chips):
        target = lax.rem(chip + slot + 1, chips) * (2 * rows)
        for side, own in ((0, 1 - core), (1, core)):
            low = (side * chips + slot) * rows
            start = pl.multiple_of(target + own * rows, rows)
            left_ref[low : low + rows, :] = turned[pl.ds(start, rows), :]
            if slot < chips - 1:
                base[2 * side][slot * rows : (slot + 1) * rows, :] = table[pl.ds(start, rows), :]
            else:
                base[2 * side + 1][...] = table[pl.ds(start, rows), :]
    multiply(left_ref, first, first_copies, outs, small, core, rows, half)
    for copy in ahead_copies:
        copy.wait()


def cost(flops, moved):
    return pl.CostEstimate(flops=flops, bytes_accessed=moved, transcendentals=0)


SMEM = pl.BlockSpec(memory_space=pltpu.SMEM)
VMEM = pl.BlockSpec(memory_space=pltpu.VMEM)
HBM = pl.BlockSpec(memory_space=pltpu.HBM)


def open_up(place, dosage, cov_rows, phenotype, chips, rows, half, widths):
    width = widths[0]
    subjects, snps = dosage.shape
    height = snps + 6 * half
    left = jax.ShapeDtypeStruct((height, subjects), BF16)
    ahead = [jax.ShapeDtypeStruct((subjects, later), BF16) for later in widths[1:]]
    parts = part_shapes(chips, rows, half, LANES) + part_shapes(chips, rows, half, width)
    return pl.pallas_call(
        functools.partial(open_kernel, chips, rows, half, widths),
        out_shape=(left, *parts, *ahead),
        in_specs=[SMEM, HBM, HBM, HBM],
        out_specs=(VMEM,) * (9 + len(ahead)),
        scratch_shapes=[
            pltpu.VMEM((subjects, snps), BF16),
            pltpu.VMEM((snps, subjects), BF16),
            pltpu.VMEM((2 * half, subjects), F32),
            pltpu.VMEM((subjects, width), BF16),
            pltpu.VMEM((2 * half, max(width, LANES)), F32),
            pltpu.VMEM((snps, LANES), F32),
            pltpu.SemaphoreType.DMA((1 + len(widths) * PIECES + max(width // STRIP, 1),)),
        ],
        compiler_params=pltpu.CompilerParams(vmem_limit_bytes=OPEN_LIMIT),
        cost_estimate=cost(2 * height * subjects * width, 4 * snps * subjects),
        name="open",
    )(place, dosage, cov_rows, phenotype)


def product_kernel(rows, half, place_ref, left_ref, pheno_ref, *refs):
    multiply(left_ref, pheno_ref, [], refs[:4], refs[4], place_ref[1], rows, half)


def product(place, left, phenotype, chips, rows, half):
    height, subjects = left.shape
    width = phenotype.shape[1]
    return pl.pallas_call(
        functools.partial(product_kernel, rows, half),
        out_shape=part_shapes(chips, rows, half, width),
        in_specs=[SMEM, VMEM, VMEM],
        out_specs=(VMEM,) * 4,
        scratch_shapes=[pltpu.VMEM((2 * half, width), F32)],
        compiler_params=pltpu.CompilerParams(vmem_limit_bytes=LIMIT),
        cost_estimate=cost(2 * height * subjects * width, 2 * subjects * width),
    )(place, left, phenotype)


def solve_kernel(live, half, count, *refs):
    place_ref, half_ref, rest_ref = refs[:3]
    terms, (inverse_ref, white_ref, var_ref, work) = refs[3 : 3 + count], refs[3 + count :]
    core = place_ref[1]
    size = 2 * half
    work[pl.ds(pl.multiple_of(core * half, half), half), :] = half_ref[...]
    work[pl.ds(pl.multiple_of((1 - core) * half, half), half), :] = rest_ref[...]
    row = lax.broadcasted_iota(jnp.int32, (size, LANES), 0)
    lane = lax.broadcasted_iota(jnp.int32, (size, LANES), 1)
    left = jnp.where(lane < size, work[...], 0.0)
    right = jnp.where(lane == row, 1.0, 0.0)
    scaled = jnp.zeros((size, LANES), F32)
    for step in live:
        pivot = jnp.broadcast_to(left[:, step : step + 1], (size, LANES))
        top = jnp.broadcast_to(pivot[step : step + 1], (size, LANES))
        ratio = jnp.where(row > step, pivot / top, 0.0)
        root = lax.rsqrt(top)
        root = root * (1.5 - 0.5 * top * root * root)
        scaled = jnp.where(row == step, right * root, scaled)
        left = left - ratio * left[step : step + 1]
        right = right - ratio * right[step : step + 1]
    inverse_ref[...] = scaled
    own = terms[0][...]
    for term in terms[1:]:
        own = own + term[...]
    wide = jnp.concatenate([scaled, jnp.zeros((LANES - size, LANES), F32)], axis=0)
    white = lax.dot_general(own, wide, LAST, precision=HI, preferred_element_type=F32)
    white_ref[...] = white
    var_ref[...] = jnp.broadcast_to(
        own[:, SQUARE : SQUARE + 1] - jnp.sum(white * white, axis=1, keepdims=True), var_ref.shape
    )


def solve(place, half_rows, rest_rows, terms, live):
    half = half_rows.shape[0]
    wide = jax.ShapeDtypeStruct(terms[0].shape, F32)
    return pl.pallas_call(
        functools.partial(solve_kernel, live, half, len(terms)),
        out_shape=(jax.ShapeDtypeStruct((2 * half, LANES), F32), wide, wide),
        in_specs=[SMEM] + [VMEM] * (2 + len(terms)),
        out_specs=(VMEM,) * 3,
        scratch_shapes=[pltpu.VMEM((2 * half, LANES), F32)],
        compiler_params=pltpu.CompilerParams(vmem_limit_bytes=LIMIT),
        cost_estimate=cost(5 * 10**9, 2**16),
        name="solve",
    )(place, half_rows, rest_rows, *terms)


def finish_kernel(dof, count, *refs):
    place_ref, inverse_ref, white_ref, var_ref, half_ref, rest_ref = refs[:6]
    terms, out_ref, small = refs[6 : 6 + count], refs[-2], refs[-1]
    half = half_ref.shape[0]
    rows, tile = out_ref.shape
    core = place_ref[1]
    low = pl.multiple_of(pl.program_id(0) * tile, tile)
    small[pl.ds(pl.multiple_of(core * half, half), half), :] = half_ref[:, pl.ds(low, tile)]
    small[pl.ds(pl.multiple_of((1 - core) * half, half), half), :] = rest_ref[:, pl.ds(low, tile)]
    white = jnp.dot(inverse_ref[:, : 2 * half], small[...], precision=HI, preferred_element_type=F32)
    pheno_var = small[SQUARE : SQUARE + 1, :] - jnp.sum(white * white, axis=0, keepdims=True)
    fitted = jnp.dot(white_ref[:, : 2 * half], white, precision=HI, preferred_element_type=F32)
    cross = terms[0][0:rows, pl.ds(low, tile)]
    for term in terms[1:]:
        cross = cross + term[0:rows, pl.ds(low, tile)]
    cross = cross - fitted
    out_ref[...] = cross * dof * lax.rsqrt(var_ref[:, 0:1] * pheno_var - cross * cross)


def finish(done, total, place, start, dof, inverse, white, geno_var, half_rows, rest_rows, terms):
    rows, width = terms[0].shape
    tile = min(STRIP, width)
    first = start // tile
    args = [place, inverse, white, geno_var, half_rows, rest_rows, *terms]
    specs = [SMEM] + [VMEM] * (len(args) - 1)
    aliases = {}
    if done is not None:
        aliases = {len(args): 0}
        args.append(done)
        specs.append(HBM)
    return pl.pallas_call(
        functools.partial(finish_kernel, dof, len(terms)),
        grid=(width // tile,),
        out_shape=jax.ShapeDtypeStruct((rows, total), F32),
        in_specs=specs,
        out_specs=pl.BlockSpec((rows, tile), lambda j: (0, first + j)),
        scratch_shapes=[pltpu.VMEM((2 * half_rows.shape[0], tile), F32)],
        input_output_aliases=aliases,
        compiler_params=pltpu.CompilerParams(vmem_limit_bytes=LIMIT),
        cost_estimate=pl.CostEstimate(
            flops=2 * 256 * 256 * width, bytes_accessed=16 * rows * width, transcendentals=rows * width
        ),
    )(*args)


def chunk_widths(total):
    units = total // TILE
    if total % TILE or units < 3:
        return [total]
    sizes = [1]
    left = units - 2
    while left > 0:
        sizes.append(min(2, left))
        left -= sizes[-1]
    sizes.append(1)
    return [size * TILE for size in sizes]


def associate(dosage, phenotype, covariates):
    devices = lax.axis_size("subj")
    chips = devices // 2
    subjects, snps = dosage.shape
    verts = phenotype.shape[1]
    covs = covariates.shape[1]
    rows = snps // devices
    half = round_up(8 + covs, 16) // 2
    live = [0] + list(range(8, 8 + covs))
    far = (chips - 1) * rows
    place_index = lax.axis_index("subj")
    place = jnp.stack([place_index // 2, lax.rem(place_index, 2)]).astype(jnp.int32)
    sibling = [(i, i ^ 1) for i in range(devices)]

    def near_sums(parts):
        give_far, give_near, keep_far, keep_near = parts
        got_far = lax.ppermute(give_far, "subj", sibling)
        got_near = lax.ppermute(give_near, "subj", sibling)
        summed = keep_far + got_far
        if chips == 2:
            return [keep_near, got_near], [summed]
        own_half = summed[far:]
        blocks = [jnp.concatenate([summed[low : low + rows], own_half], axis=0) for low in range(0, far, rows)]
        return [keep_near, got_near], blocks

    def far_terms(blocks):
        came = []
        for step, block in enumerate(blocks, 1):
            moves = [(i, (i + 2 * step) % devices) for i in range(devices)]
            came.append(lax.ppermute(block, "subj", moves))
        return came

    def gather_half(blocks, came):
        halves = blocks[0][rows:]
        for block in came:
            halves = halves + block[rows:]
        rest = lax.ppermute(halves, "subj", sibling)
        return halves, rest

    widths = chunk_widths(verts)
    left, *parts = open_up(
        place, dosage, covariates.T, phenotype, chips, rows, half, widths
    )
    ahead = parts[8:]
    sums = [near_sums(parts[4:8])]
    came = [far_terms(sums[0][1])]
    terms, blocks = near_sums(parts[:4])
    base_came = far_terms(blocks)
    halves, rest = gather_half(blocks, base_came)
    inverse, white, geno_var = solve(
        place, halves, rest, terms + [block[:rows] for block in base_came], live
    )
    dof = float(subjects * devices - covs - 2) ** 0.5

    start = widths[0]
    for index in range(1, len(widths)):
        parts = product(place, left, ahead[index - 1], chips, rows, half)
        start += widths[index]
        sums.append(near_sums(parts))
        came.append(far_terms(sums[-1][1]))
    out = None
    start = 0
    for index, width in enumerate(widths):
        terms, blocks = sums[index]
        halves, rest = gather_half(blocks, came[index])
        out = finish(
            out, verts, place, start, dof, inverse, white, geno_var, halves, rest, terms + came[index]
        )
        start += width
    return out


def solution(mesh):
    in_specs = (P(("grp", "subj"), None), P(("grp", "subj"), "vert"), P(("grp", "subj"), None))
    out_specs = P(("grp", "subj"), "vert")
    return jax.shard_map(associate, mesh=mesh, in_specs=in_specs, out_specs=out_specs, check_vma=False)
```

time: 247 us -> 124 us (0.50)
  matrix products: 99.5 us -> 0 us
  Pallas kernels: 0 us -> 48.3 us
  waiting for transfers between devices: 93 us -> 54.5 us
  other arithmetic: 21.7 us -> 0.58 us
  starting transfers between devices: 0.04 us -> 17.2 us
  blocking collectives: 13.4 us -> 0 us
  between operations: 13.5 us -> 0.19 us
  local copies, waits for them, and re-layouts: 5.17 us -> 2.57 us
    dot_general x8 -> x0, matrix products: 94.6 us -> none  [the longest x1 39.7 us: per_device(): lax.dot_general(geno_half, pheno_half, contract, preferred_element_type=j...]
    reduce_scatter x1 -> x0, waiting for transfers between devices: 84.7 us -> none  [per_device(): lax.psum_scatter(partial_value, 'subj', scatter_dimension=0, tiled=True)]
    ppermute x0 -> x28, waiting for transfers between devices: none -> 54.5 us  [the longest x7 53.5 us: far_terms(): came.append(lax.ppermute(block, 'subj', moves))]
    pallas_call x0 -> x13, Pallas kernels: none -> 48.3 us  [the longest x6 18.1 us: finish(): pl.pallas_call(functools.partial(finish_kernel, dof, len(terms)), grid=(w...]
    ppermute x0 -> x28, starting transfers between devices: none -> 17.2 us  [the longest x7 11.6 us: far_terms(): came.append(lax.ppermute(block, 'subj', moves))]
    psum x1 -> x0, blocking collectives: 13.4 us -> none  [per_device(): lax.psum((gram, design_geno, design_pheno, jnp.sum(geno * geno, axis=0),...]
    reduce_sum x2 -> x0, other arithmetic: 9.66 us -> none  [the longest x1 9.15 us: per_device(): pheno_square = jnp.sum(jnp.square(phenotype.astype(jnp.float32)), axis=0)]
    psum x1 -> x0, waiting for transfers between devices: 8.26 us -> none  [per_device(): lax.psum((gram, design_geno, design_pheno, jnp.sum(geno * geno, axis=0),...]
  transfers between devices with their start and end apart: 2 -> 28, of which waited for: 2 -> 9; matrix products, arithmetic and copies ran while one was open for 8% -> 0% of each run, Pallas kernels for 0% -> 31%
where the time goes in v2:
time: 124 us; the launch traced here: 123 us
  waiting for transfers between devices  54.5 us (44%)
  Pallas kernels  48.3 us (39%)
  starting transfers between devices  17.2 us (14%)
  local copies, waits for them, and re-layouts  2.57 us (2%)
    ppermute x7, waiting for transfers between devices, far_terms(): came.append(lax.ppermute(block, 'subj', moves))  53.5 us
    pallas_call x6, Pallas kernels, finish(): pl.pallas_call(functools.partial(finish_kernel, dof, len(terms)), grid=(w...  18.1 us
    pallas_call x5, Pallas kernels, product(): pl.pallas_call(functools.partial(product_kernel, rows, half), out_shape=p...  16.1 us
    ppermute x7, starting transfers between devices, far_terms(): came.append(lax.ppermute(block, 'subj', moves))  11.6 us
    pallas_call x1, Pallas kernels, open_up(): pl.pallas_call(functools.partial(open_kernel, chips, rows, half, widths),...  8.09 us
    pallas_call x1, Pallas kernels, solve(): pl.pallas_call(functools.partial(solve_kernel, live, half, len(terms)), o...  6.05 us
    unnamed x4, local copies, waits for them, and re-layouts  2.56 us
  transfers between devices with their start and end apart: 28, of which 9 were waited for; matrix products, arithmetic and copies ran while one was open for 0% of the time, Pallas kernels for 31%

profile of v2, /device:TPU:0, one launch (start us, length us, event | category | flops | bytes accessed | tf_op | source)
XLA Modules:
  0.0 123.4 jit_solution(14217060646958975644)
XLA Ops:
  0.0 0.1 pad_add_fusion.place_ref.refs_0_
  0.1 1.6 %copy-done = bf16[2048,512]{1,0:T(8,128)(2,1)S(1)} copy-done((bf16[2048,512]{1,0:T(8,128)(2,1)S(1)}, bf16[2048,512]{1,0:T(8,128)(2,1)}, u32[]{:S(2)}) %copy-start) | copy-done | bytes 2097176
  1.7 1.0 copy-done.1
  2.6 8.1 %open.1 = (bf16[656,2048]{1,0:T(8,128)(2,1)S(1)}, f32[152,128]{1,0:T(8,128)S(1)}, f32[128,128]{1,0:T(8,128)S(1)}, f32[152,128]{1,0:T(8,128)S(1)}, f32[128,128]{1...) custom-call(s32[2]{0:T(128)S(1)} %pad_add_fusion.place_ref.refs_0_, ...), custom_call_target="tpu_custom_call" | custom-call | flops 1375731712 | bytes 4194304 | tf_op jit(solution)/shard_map/open/pallas_call | solution.py:169
  10.7 0.6 collective-permute-start
  11.3 3.5 %shard_map.38 = (f32[152,1024]{1,0:T(8,128)S(1)}, f32[128,1024]{1,0:T(8,128)S(1)}, f32[152,1024]{1,0:T(8,128)S(1)}, f32[128,1024]{1,0:T(8,128)S(1)}) custom-call(s32[2]{0:T(128)S(1)} %pad_add_fusion.place_ref.refs_0_, bf16[656,2048]{1,0:T(8,128)(2,1)S(1)} %get-tuple-element.49.left_ref, bf16[2048,1024]{1,0:T(8,128)(2,1)S(1)} %get-tuple-element.55.pheno_ref), custom_call_target="tpu_custom_call" | custom-call | flops 2751463424 | bytes 4194304 | tf_op jit(solution)/shard_map/pallas_call | solution.py:196
  14.8 0.1 collective-permute-start.8
  14.9 3.5 %shard_map.39 = (f32[152,1024]{1,0:T(8,128)S(1)}, f32[128,1024]{1,0:T(8,128)S(1)}, f32[152,1024]{1,0:T(8,128)S(1)}, f32[128,1024]{1,0:T(8,128)S(1)}) custom-call(s32[2]{0:T(128)S(1)} %pad_add_fusion.place_ref.refs_0_, bf16[656,2048]{1,0:T(8,128)(2,1)S(1)} %get-tuple-element.49.left_ref, bf16[2048,1024]{1,0:T(8,128)(2,1)S(1)} %get-tuple-element.60.pheno_ref), custom_call_target="tpu_custom_call" | custom-call | flops 2751463424 | bytes 4194304 | tf_op jit(solution)/shard_map/pallas_call | solution.py:196
  18.4 0.6 collective-permute-start.12
  19.0 3.5 %shard_map.40 = (f32[152,1024]{1,0:T(8,128)S(1)}, f32[128,1024]{1,0:T(8,128)S(1)}, f32[152,1024]{1,0:T(8,128)S(1)}, f32[128,1024]{1,0:T(8,128)S(1)}) custom-call(s32[2]{0:T(128)S(1)} %pad_add_fusion.place_ref.refs_0_, bf16[656,2048]{1,0:T(8,128)(2,1)S(1)} %get-tuple-element.49.left_ref, bf16[2048,1024]{1,0:T(8,128)(2,1)S(1)} %get-tuple-element.65.pheno_ref), custom_call_target="tpu_custom_call" | custom-call | flops 2751463424 | bytes 4194304 | tf_op jit(solution)/shard_map/pallas_call | solution.py:196
  22.5 0.1 collective-permute-start.16
  22.5 0.5 collective-permute-start.24
  23.0 0.0 collective-permute-done
  23.1 2.6 %collective-permute-start.1 = (f32[152,128]{1,0:T(8,128)S(1)}, f32[152,128]{1,0:T(8,128)S(1)}, u32[]{:S(2)}, u32[]{:S(2)}) collective-permute-start(f32[152,128]{1,0:T(8,128)S(1)} %add.43), channel_id=1, source_target_pairs={{0,8},{4,12},{8,0},{12,4},{1,9},{5,13},{9,1},{13,5},{2,10},{6,14},... | collective-permute-start | bytes 233480 | tf_op jit(solution)/shard_map/ppermute | solution.py:342
  25.7 2.1 %shard_map.37 = (f32[152,512]{1,0:T(8,128)S(1)}, f32[128,512]{1,0:T(8,128)S(1)}, f32[152,512]{1,0:T(8,128)S(1)}, f32[128,512]{1,0:T(8,128)S(1)}) custom-call(s32[2]{0:T(128)S(1)} %pad_add_fusion.place_ref.refs_0_, bf16[656,2048]{1,0:T(8,128)(2,1)S(1)} %get-tuple-element.49.left_ref, bf16[2048,512]{1,0:T(8,128)(2,1)S(1)} %get-tuple-element.50.pheno_ref), custom_call_target="tpu_custom_call" | custom-call | flops 1375731712 | bytes 2097152 | tf_op jit(solution)/shard_map/pallas_call | solution.py:196
  27.8 0.8 collective-permute-done.1
  28.6 3.5 %shard_map.41 = (f32[152,1024]{1,0:T(8,128)S(1)}, f32[128,1024]{1,0:T(8,128)S(1)}, f32[152,1024]{1,0:T(8,128)S(1)}, f32[128,1024]{1,0:T(8,128)S(1)}) custom-call(s32[2]{0:T(128)S(1)} %pad_add_fusion.place_ref.refs_0_, bf16[656,2048]{1,0:T(8,128)(2,1)S(1)} %get-tuple-element.49.left_ref, bf16[2048,1024]{1,0:T(8,128)(2,1)S(1)} %get-tuple-element.70.pheno_ref), custom_call_target="tpu_custom_call" | custom-call | flops 2751463424 | bytes 4194304 | tf_op jit(solution)/shard_map/pallas_call | solution.py:196
  32.2 0.6 collective-permute-start.3
  32.7 0.1 collective-permute-start.20
  32.8 0.0 collective-permute-done.12
  32.8 0.4 collective-permute-start.2
  33.3 0.1 add.47
  33.4 0.1 add.49
  33.5 0.1 collective-permute-done.3.refs_4_
  33.6 0.4 collective-permute-start.27
  34.0 0.8 collective-permute-done.2.refs_2_
  34.8 1.7 %collective-permute-start.25 = (f32[152,512]{1,0:T(8,128)S(1)}, f32[152,512]{1,0:T(8,128)S(1)}, u32[]{:S(2)}, u32[]{:S(2)}) collective-permute-start(f32[152,512]{1,0:T(8,128)S(1)} %add.55), channel_id=1, source_target_pairs={{0,8},{4,12},{8,0},{12,4},{1,9},{5,13},{9,1},{13,5},{2,10},{6,14},... | collective-permute-start | bytes 933896 | tf_op jit(solution)/shard_map/ppermute | solution.py:342
  36.5 0.0 collective-permute-done.4
  36.5 0.3 collective-permute-start.9
  36.8 0.0 collective-permute-done.16
  36.8 1.7 %collective-permute-start.13 = (f32[152,1024]{1,0:T(8,128)S(1)}, f32[152,1024]{1,0:T(8,128)S(1)}, u32[]{:S(2)}, u32[]{:S(2)}) collective-permute-start(f32[152,1024]{1,0:T(8,128)S(1)} %add.49), channel_id=1, source_target_pairs={{0,8},{4,12},{8,0},{12,4},{1,9},{5,13},{9,1},{13,5},{2,10},{6,14},... | collective-permute-start | bytes 1867784 | tf_op jit(solution)/shard_map/ppermute | solution.py:342
  38.6 6.0 %solve.1 = (f32[48,128]{1,0:T(8,128)S(1)}, f32[128,128]{1,0:T(8,128)S(1)}, f32[128,128]{1,0:T(8,128)S(1)}) custom-call(s32[2]{0:T(128)S(1)} %pad_add_fusion.place_ref.refs_0_, f32[24,128]{1,0:T(8,128)S(1)} %slice_add_fusion.6.refs_1_, f32[24,128]{1,0:T(8,128)S(1)} %collective-permute-done.2.refs_2_, f32[128,128]{1,0:T(8,128)S(1)} %get-tuple-element.44.refs_3_, ...), custom_call_target="tpu_custom_call" | custom-call | flops 5000000000 | bytes 65536 | tf_op jit(solution)/shard_map/solve/pallas_call | solution.py:243
  44.7 0.1 add.51
  44.8 0.0 collective-permute-done.20
  44.8 0.1 collective-permute-start.15
  44.9 0.2 collective-permute-done.25.refs_8_
  45.0 1.7 %collective-permute-start.17 = (f32[152,1024]{1,0:T(8,128)S(1)}, f32[152,1024]{1,0:T(8,128)S(1)}, u32[]{:S(2)}, u32[]{:S(2)}) collective-permute-start(f32[152,1024]{1,0:T(8,128)S(1)} %add.51), channel_id=1, source_target_pairs={{0,8},{4,12},{8,0},{12,4},{1,9},{5,13},{9,1},{13,5},{2,10},{6,14},... | collective-permute-start | bytes 1867784 | tf_op jit(solution)/shard_map/ppermute | solution.py:342
  46.8 0.1 add.53
  46.9 0.1 collective-permute-start.19
  46.9 11.4 %collective-permute-done.9.refs_8_ = f32[152,1024]{1,0:T(8,128)S(1)} collective-permute-done((f32[152,1024]{1,0:T(8,128)S(1)}, f32[152,1024]{1,0:T(8,128)S(1)}, u32[]{:S(2)}, u32[]{:S(2)}) %collective-permute-start.9) | collective-permute-done | bytes 622624 | tf_op jit(solution)/shard_map/ppermute | solution.py:342
  58.4 1.7 %collective-permute-start.21 = (f32[152,1024]{1,0:T(8,128)S(1)}, f32[152,1024]{1,0:T(8,128)S(1)}, u32[]{:S(2)}, u32[]{:S(2)}) collective-permute-start(f32[152,1024]{1,0:T(8,128)S(1)} %add.53), channel_id=1, source_target_pairs={{0,8},{4,12},{8,0},{12,4},{1,9},{5,13},{9,1},{13,5},{2,10},{6,14},... | collective-permute-start | bytes 1867784 | tf_op jit(solution)/shard_map/ppermute | solution.py:342
  60.1 11.6 %collective-permute-done.13.refs_8_ = f32[152,1024]{1,0:T(8,128)S(1)} collective-permute-done((f32[152,1024]{1,0:T(8,128)S(1)}, f32[152,1024]{1,0:T(8,128)S(1)}, u32[]{:S(2)}, u32[]{:S(2)}) %collective-permute-start.13) | collective-permute-done | bytes 622624 | tf_op jit(solution)/shard_map/ppermute | solution.py:342
  71.7 0.0 collective-permute-start.23
  71.7 0.0 collective-permute-done.15.refs_7_
  71.7 0.6 collective-permute-start.11
  72.3 12.7 %collective-permute-done.17.refs_8_ = f32[152,1024]{1,0:T(8,128)S(1)} collective-permute-done((f32[152,1024]{1,0:T(8,128)S(1)}, f32[152,1024]{1,0:T(8,128)S(1)}, u32[]{:S(2)}, u32[]{:S(2)}) %collective-permute-start.17) | collective-permute-done | bytes 622624 | tf_op jit(solution)/shard_map/ppermute | solution.py:342
  85.1 1.7 %collective-permute-start.5 = (f32[152,512]{1,0:T(8,128)S(1)}, f32[152,512]{1,0:T(8,128)S(1)}, u32[]{:S(2)}, u32[]{:S(2)}) collective-permute-start(f32[152,512]{1,0:T(8,128)S(1)} %add.45), channel_id=1, source_target_pairs={{0,8},{4,12},{8,0},{12,4},{1,9},{5,13},{9,1},{13,5},{2,10},{6,14},... | collective-permute-start | bytes 933896 | tf_op jit(solution)/shard_map/ppermute | solution.py:342
  86.8 0.0 collective-permute-done.19.refs_7_
  86.8 0.1 collective-permute-start.26
  86.9 11.5 %collective-permute-done.21.refs_8_ = f32[152,1024]{1,0:T(8,128)S(1)} collective-permute-done((f32[152,1024]{1,0:T(8,128)S(1)}, f32[152,1024]{1,0:T(8,128)S(1)}, u32[]{:S(2)}, u32[]{:S(2)}) %collective-permute-start.21) | collective-permute-done | bytes 622624 | tf_op jit(solution)/shard_map/ppermute | solution.py:342
  98.4 0.6 collective-permute-start.7
  99.0 5.2 %collective-permute-done.5.refs_8_ = f32[152,512]{1,0:T(8,128)S(1)} collective-permute-done((f32[152,512]{1,0:T(8,128)S(1)}, f32[152,512]{1,0:T(8,128)S(1)}, u32[]{:S(2)}, u32[]{:S(2)}) %collective-permute-start.5) | collective-permute-done | bytes 311328 | tf_op jit(solution)/shard_map/ppermute | solution.py:342
  104.2 0.0 collective-permute-start.10
  104.2 0.0 collective-permute-done.26.refs_5_
  104.2 0.5 collective-permute-start.14
  104.8 0.0 collective-permute-done.18.refs_5_
  104.8 0.1 collective-permute-start.22
  104.8 2.3 %shard_map.42.refs_9_ = f32[128,5120]{1,0:T(8,128)} custom-call(s32[2]{0:T(128)S(1)} %pad_add_fusion.place_ref.refs_0_, f32[48,128]{1,0:T(8,128)S(1)} %get-tuple-element.46.refs_1_, f32[128,128]{1,0:T(8,128)S(1)} %get-tuple-element.47.refs_2_, f32[128,128]{1,0:T(8,128)S(1)} %get-tuple-element.48.refs_3_, f32[24,512]{1,0:T(8,128)S(1)} %slice_add_fusion.4.refs_4_, ...), custom_call_target="tpu_custom_call" | custom-call | flops 67108864 | bytes 1048576 | tf_op jit(solution)/shard_map/pallas_call | solution.py:285
  107.1 0.4 collective-permute-start.6
  107.5 3.4 %shard_map.43.refs_9_ = f32[128,5120]{1,0:T(8,128)} custom-call(s32[2]{0:T(128)S(1)} %pad_add_fusion.place_ref.refs_0_, f32[48,128]{1,0:T(8,128)S(1)} %get-tuple-element.46.refs_1_, f32[128,128]{1,0:T(8,128)S(1)} %get-tuple-element.47.refs_2_, f32[128,128]{1,0:T(8,128)S(1)} %get-tuple-element.48.refs_3_, ...), custom_call_target="tpu_custom_call", output_to_operand_aliasing={{}: (9, {})} | custom-call | flops 134217728 | bytes 2097152 | tf_op jit(solution)/shard_map/pallas_call | solution.py:285
  110.9 3.4 %shard_map.44.refs_9_ = f32[128,5120]{1,0:T(8,128)} custom-call(s32[2]{0:T(128)S(1)} %pad_add_fusion.place_ref.refs_0_, f32[48,128]{1,0:T(8,128)S(1)} %get-tuple-element.46.refs_1_, f32[128,128]{1,0:T(8,128)S(1)} %get-tuple-element.47.refs_2_, f32[128,128]{1,0:T(8,128)S(1)} %get-tuple-element.48.refs_3_, ...), custom_call_target="tpu_custom_call", output_to_operand_aliasing={{}: (9, {})} | custom-call | flops 134217728 | bytes 2097152 | tf_op jit(solution)/shard_map/pallas_call | solution.py:285
  114.3 3.4 %shard_map.45.refs_9_ = f32[128,5120]{1,0:T(8,128)} custom-call(s32[2]{0:T(128)S(1)} %pad_add_fusion.place_ref.refs_0_, f32[48,128]{1,0:T(8,128)S(1)} %get-tuple-element.46.refs_1_, f32[128,128]{1,0:T(8,128)S(1)} %get-tuple-element.47.refs_2_, f32[128,128]{1,0:T(8,128)S(1)} %get-tuple-element.48.refs_3_, ...), custom_call_target="tpu_custom_call", output_to_operand_aliasing={{}: (9, {})} | custom-call | flops 134217728 | bytes 2097152 | tf_op jit(solution)/shard_map/pallas_call | solution.py:285
  117.7 3.4 %shard_map.46.refs_9_ = f32[128,5120]{1,0:T(8,128)} custom-call(s32[2]{0:T(128)S(1)} %pad_add_fusion.place_ref.refs_0_, f32[48,128]{1,0:T(8,128)S(1)} %get-tuple-element.46.refs_1_, f32[128,128]{1,0:T(8,128)S(1)} %get-tuple-element.47.refs_2_, f32[128,128]{1,0:T(8,128)S(1)} %get-tuple-element.48.refs_3_, ...), custom_call_target="tpu_custom_call", output_to_operand_aliasing={{}: (9, {})} | custom-call | flops 134217728 | bytes 2097152 | tf_op jit(solution)/shard_map/pallas_call | solution.py:285
  121.1 2.3 %shard_map.47 = f32[128,5120]{1,0:T(8,128)} custom-call(s32[2]{0:T(128)S(1)} %pad_add_fusion.place_ref.refs_0_, f32[48,128]{1,0:T(8,128)S(1)} %get-tuple-element.46.refs_1_, f32[128,128]{1,0:T(8,128)S(1)} %get-tuple-element.47.refs_2_, f32[128,128]{1,0:T(8,128)S(1)} %get-tuple-element.48.refs_3_, ...), custom_call_target="tpu_custom_call", output_to_operand_aliasing={{}: (9, {})} | custom-call | flops 67108864 | bytes 1048576 | tf_op jit(solution)/shard_map/pallas_call | solution.py:285
  (25 shorter events, 0.2 us)
Async XLA Ops:
  0.1 1.6 %copy-start = (bf16[2048,512]{1,0:T(8,128)(2,1)S(1)}, bf16[2048,512]{1,0:T(8,128)(2,1)}, u32[]{:S(2)}) copy-start(bf16[2048,512]{1,0:T(8,128)(2,1)} %geno_ref.1) | copy-start | bytes 6291460
  1.7 1.0 copy-start.1
  10.7 12.3 %collective-permute-start = (f32[152,128]{1,0:T(8,128)S(1)}, f32[152,128]{1,0:T(8,128)S(1)}, u32[]{:S(2)}, u32[]{:S(2)}) collective-permute-start(f32[152,128]{1,0:T(8,128)S(1)} %get-tuple-element.43), channel_id=1, source_target_pairs={{0,4},{4,0},{8,12},{12,8},{1,5},{5,1},{9,13},{13,9},{2,6},{6,2},{1... | collective-permute-start | bytes 233480 | tf_op jit(solution)/shard_map/ppermute | solution.py:329
  14.8 17.9 %collective-permute-start.8 = (f32[152,1024]{1,0:T(8,128)S(1)}, f32[152,1024]{1,0:T(8,128)S(1)}, u32[]{:S(2)}, u32[]{:S(2)}) collective-permute-start(f32[152,1024]{1,0:T(8,128)S(1)} %get-tuple-element.57), channel_id=1, source_target_pairs={{0,4},{4,0},{8,12},{12,8},{1,5},{5,1},{9,13},{13,9},{2,6},{6,2},{1... | collective-permute-start | bytes 1867784 | tf_op jit(solution)/shard_map/ppermute | solution.py:329
  18.4 14.4 %collective-permute-start.12 = (f32[152,1024]{1,0:T(8,128)S(1)}, f32[152,1024]{1,0:T(8,128)S(1)}, u32[]{:S(2)}, u32[]{:S(2)}) collective-permute-start(f32[152,1024]{1,0:T(8,128)S(1)} %get-tuple-element.62), channel_id=1, source_target_pairs={{0,4},{4,0},{8,12},{12,8},{1,5},{5,1},{9,13},{13,9},{2,6},{6,2},{1... | collective-permute-start | bytes 1867784 | tf_op jit(solution)/shard_map/ppermute | solution.py:329
  22.5 14.4 %collective-permute-start.16 = (f32[152,1024]{1,0:T(8,128)S(1)}, f32[152,1024]{1,0:T(8,128)S(1)}, u32[]{:S(2)}, u32[]{:S(2)}) collective-permute-start(f32[152,1024]{1,0:T(8,128)S(1)} %get-tuple-element.67), channel_id=1, source_target_pairs={{0,4},{4,0},{8,12},{12,8},{1,5},{5,1},{9,13},{13,9},{2,6},{6,2},{1... | collective-permute-start | bytes 1867784 | tf_op jit(solution)/shard_map/ppermute | solution.py:329
  22.5 9.6 %collective-permute-start.24 = (f32[152,512]{1,0:T(8,128)S(1)}, f32[152,512]{1,0:T(8,128)S(1)}, u32[]{:S(2)}, u32[]{:S(2)}) collective-permute-start(f32[152,512]{1,0:T(8,128)S(1)} %get-tuple-element.76), channel_id=1, source_target_pairs={{0,4},{4,0},{8,12},{12,8},{1,5},{5,1},{9,13},{13,9},{2,6},{6,2},{1... | collective-permute-start | bytes 933896 | tf_op jit(solution)/shard_map/ppermute | solution.py:329
  23.1 5.6 %collective-permute-start.1 = (f32[152,128]{1,0:T(8,128)S(1)}, f32[152,128]{1,0:T(8,128)S(1)}, u32[]{:S(2)}, u32[]{:S(2)}) collective-permute-start(f32[152,128]{1,0:T(8,128)S(1)} %add.43), channel_id=1, source_target_pairs={{0,8},{4,12},{8,0},{12,4},{1,9},{5,13},{9,1},{13,5},{2,10},{6,14},... | collective-permute-start | bytes 233480 | tf_op jit(solution)/shard_map/ppermute | solution.py:342
  28.6 7.9 %collective-permute-start.4 = (f32[152,512]{1,0:T(8,128)S(1)}, f32[152,512]{1,0:T(8,128)S(1)}, u32[]{:S(2)}, u32[]{:S(2)}) collective-permute-start(f32[152,512]{1,0:T(8,128)S(1)} %get-tuple-element.52), channel_id=1, source_target_pairs={{0,4},{4,0},{8,12},{12,8},{1,5},{5,1},{9,13},{13,9},{2,6},{6,2},{1... | collective-permute-start | bytes 933896 | tf_op jit(solution)/shard_map/ppermute | solution.py:329
  32.2 1.5 %collective-permute-start.3 = (f32[128,128]{1,0:T(8,128)S(1)}, f32[128,128]{1,0:T(8,128)S(1)}, u32[]{:S(2)}, u32[]{:S(2)}) collective-permute-start(f32[128,128]{1,0:T(8,128)S(1)} %get-tuple-element.45), channel_id=1, source_target_pairs={{0,4},{4,0},{8,12},{12,8},{1,5},{5,1},{9,13},{13,9},{2,6},{6,2},{1... | collective-permute-start | bytes 196616 | tf_op jit(solution)/shard_map/ppermute | solution.py:330
  32.7 12.0 %collective-permute-start.20 = (f32[152,1024]{1,0:T(8,128)S(1)}, f32[152,1024]{1,0:T(8,128)S(1)}, u32[]{:S(2)}, u32[]{:S(2)}) collective-permute-start(f32[152,1024]{1,0:T(8,128)S(1)} %get-tuple-element.72), channel_id=1, source_target_pairs={{0,4},{4,0},{8,12},{12,8},{1,5},{5,1},{9,13},{13,9},{2,6},{6,2},{1... | collective-permute-start | bytes 1867784 | tf_op jit(solution)/shard_map/ppermute | solution.py:329
  32.8 2.0 %collective-permute-start.2 = (f32[24,128]{1,0:T(8,128)S(1)}, f32[24,128]{1,0:T(8,128)S(1)}, u32[]{:S(2)}, u32[]{:S(2)}) collective-permute-start(f32[24,128]{1,0:T(8,128)S(1)} %slice_add_fusion.6.refs_1_), channel_id=1, source_target_pairs={{0,4},{4,0},{8,12},{12,8},{1,5},{5,1},{9,13},{13,9},{2,6},{6,2},{1... | collective-permute-start | bytes 36872 | tf_op jit(solution)/shard_map/ppermute | solution.py:349
  33.6 13.2 %collective-permute-start.27 = (f32[128,512]{1,0:T(8,128)S(1)}, f32[128,512]{1,0:T(8,128)S(1)}, u32[]{:S(2)}, u32[]{:S(2)}) collective-permute-start(f32[128,512]{1,0:T(8,128)S(1)} %get-tuple-element.78), channel_id=1, source_target_pairs={{0,4},{4,0},{8,12},{12,8},{1,5},{5,1},{9,13},{13,9},{2,6},{6,2},{1... | collective-permute-start | bytes 786440 | tf_op jit(solution)/shard_map/ppermute | solution.py:330
  34.8 10.2 %collective-permute-start.25 = (f32[152,512]{1,0:T(8,128)S(1)}, f32[152,512]{1,0:T(8,128)S(1)}, u32[]{:S(2)}, u32[]{:S(2)}) collective-permute-start(f32[152,512]{1,0:T(8,128)S(1)} %add.55), channel_id=1, source_target_pairs={{0,8},{4,12},{8,0},{12,4},{1,9},{5,13},{9,1},{13,5},{2,10},{6,14},... | collective-permute-start | bytes 933896 | tf_op jit(solution)/shard_map/ppermute | solution.py:342
  36.5 21.8 %collective-permute-start.9 = (f32[152,1024]{1,0:T(8,128)S(1)}, f32[152,1024]{1,0:T(8,128)S(1)}, u32[]{:S(2)}, u32[]{:S(2)}) collective-permute-start(f32[152,1024]{1,0:T(8,128)S(1)} %add.47), channel_id=1, source_target_pairs={{0,8},{4,12},{8,0},{12,4},{1,9},{5,13},{9,1},{13,5},{2,10},{6,14},... | collective-permute-start | bytes 1867784 | tf_op jit(solution)/shard_map/ppermute | solution.py:342
  36.8 34.9 %collective-permute-start.13 = (f32[152,1024]{1,0:T(8,128)S(1)}, f32[152,1024]{1,0:T(8,128)S(1)}, u32[]{:S(2)}, u32[]{:S(2)}) collective-permute-start(f32[152,1024]{1,0:T(8,128)S(1)} %add.49), channel_id=1, source_target_pairs={{0,8},{4,12},{8,0},{12,4},{1,9},{5,13},{9,1},{13,5},{2,10},{6,14},... | collective-permute-start | bytes 1867784 | tf_op jit(solution)/shard_map/ppermute | solution.py:342
  44.8 27.0 %collective-permute-start.15 = (f32[128,1024]{1,0:T(8,128)S(1)}, f32[128,1024]{1,0:T(8,128)S(1)}, u32[]{:S(2)}, u32[]{:S(2)}) collective-permute-start(f32[128,1024]{1,0:T(8,128)S(1)} %get-tuple-element.64), channel_id=1, source_target_pairs={{0,4},{4,0},{8,12},{12,8},{1,5},{5,1},{9,13},{13,9},{2,6},{6,2},{1... | collective-permute-start | bytes 1572872 | tf_op jit(solution)/shard_map/ppermute | solution.py:330
  45.0 40.0 %collective-permute-start.17 = (f32[152,1024]{1,0:T(8,128)S(1)}, f32[152,1024]{1,0:T(8,128)S(1)}, u32[]{:S(2)}, u32[]{:S(2)}) collective-permute-start(f32[152,1024]{1,0:T(8,128)S(1)} %add.51), channel_id=1, source_target_pairs={{0,8},{4,12},{8,0},{12,4},{1,9},{5,13},{9,1},{13,5},{2,10},{6,14},... | collective-permute-start | bytes 1867784 | tf_op jit(solution)/shard_map/ppermute | solution.py:342
  46.9 39.9 %collective-permute-start.19 = (f32[128,1024]{1,0:T(8,128)S(1)}, f32[128,1024]{1,0:T(8,128)S(1)}, u32[]{:S(2)}, u32[]{:S(2)}) collective-permute-start(f32[128,1024]{1,0:T(8,128)S(1)} %get-tuple-element.69), channel_id=1, source_target_pairs={{0,4},{4,0},{8,12},{12,8},{1,5},{5,1},{9,13},{13,9},{2,6},{6,2},{1... | collective-permute-start | bytes 1572872 | tf_op jit(solution)/shard_map/ppermute | solution.py:330
  58.4 40.0 %collective-permute-start.21 = (f32[152,1024]{1,0:T(8,128)S(1)}, f32[152,1024]{1,0:T(8,128)S(1)}, u32[]{:S(2)}, u32[]{:S(2)}) collective-permute-start(f32[152,1024]{1,0:T(8,128)S(1)} %add.53), channel_id=1, source_target_pairs={{0,8},{4,12},{8,0},{12,4},{1,9},{5,13},{9,1},{13,5},{2,10},{6,14},... | collective-permute-start | bytes 1867784 | tf_op jit(solution)/shard_map/ppermute | solution.py:342
  71.7 26.7 %collective-permute-start.23 = (f32[128,1024]{1,0:T(8,128)S(1)}, f32[128,1024]{1,0:T(8,128)S(1)}, u32[]{:S(2)}, u32[]{:S(2)}) collective-permute-start(f32[128,1024]{1,0:T(8,128)S(1)} %get-tuple-element.74), channel_id=1, source_target_pairs={{0,4},{4,0},{8,12},{12,8},{1,5},{5,1},{9,13},{13,9},{2,6},{6,2},{1... | collective-permute-start | bytes 1572872 | tf_op jit(solution)/shard_map/ppermute | solution.py:330
  71.7 46.0 %collective-permute-start.11 = (f32[128,1024]{1,0:T(8,128)S(1)}, f32[128,1024]{1,0:T(8,128)S(1)}, u32[]{:S(2)}, u32[]{:S(2)}) collective-permute-start(f32[128,1024]{1,0:T(8,128)S(1)} %get-tuple-element.59), channel_id=1, source_target_pairs={{0,4},{4,0},{8,12},{12,8},{1,5},{5,1},{9,13},{13,9},{2,6},{6,2},{1... | collective-permute-start | bytes 1572872 | tf_op jit(solution)/shard_map/ppermute | solution.py:330
  85.1 19.2 %collective-permute-start.5 = (f32[152,512]{1,0:T(8,128)S(1)}, f32[152,512]{1,0:T(8,128)S(1)}, u32[]{:S(2)}, u32[]{:S(2)}) collective-permute-start(f32[152,512]{1,0:T(8,128)S(1)} %add.45), channel_id=1, source_target_pairs={{0,8},{4,12},{8,0},{12,4},{1,9},{5,13},{9,1},{13,5},{2,10},{6,14},... | collective-permute-start | bytes 933896 | tf_op jit(solution)/shard_map/ppermute | solution.py:342
  86.8 17.4 %collective-permute-start.26 = (f32[24,512]{1,0:T(8,128)S(1)}, f32[24,512]{1,0:T(8,128)S(1)}, u32[]{:S(2)}, u32[]{:S(2)}) collective-permute-start(f32[24,512]{1,0:T(8,128)S(1)} %slice_add_fusion.4.refs_4_), channel_id=1, source_target_pairs={{0,4},{4,0},{8,12},{12,8},{1,5},{5,1},{9,13},{13,9},{2,6},{6,2},{1... | collective-permute-start | bytes 147464 | tf_op jit(solution)/shard_map/ppermute | solution.py:349
  98.4 6.4 %collective-permute-start.18 = (f32[24,1024]{1,0:T(8,128)S(1)}, f32[24,1024]{1,0:T(8,128)S(1)}, u32[]{:S(2)}, u32[]{:S(2)}) collective-permute-start(f32[24,1024]{1,0:T(8,128)S(1)} %slice_add_fusion.1.refs_4_), channel_id=1, source_target_pairs={{0,4},{4,0},{8,12},{12,8},{1,5},{5,1},{9,13},{13,9},{2,6},{6,2},{1... | collective-permute-start | bytes 294920 | tf_op jit(solution)/shard_map/ppermute | solution.py:349
  98.4 22.7 %collective-permute-start.7 = (f32[128,512]{1,0:T(8,128)S(1)}, f32[128,512]{1,0:T(8,128)S(1)}, u32[]{:S(2)}, u32[]{:S(2)}) collective-permute-start(f32[128,512]{1,0:T(8,128)S(1)} %get-tuple-element.54), channel_id=1, source_target_pairs={{0,4},{4,0},{8,12},{12,8},{1,5},{5,1},{9,13},{13,9},{2,6},{6,2},{1... | collective-permute-start | bytes 786440 | tf_op jit(solution)/shard_map/ppermute | solution.py:330
  104.2 13.5 %collective-permute-start.10 = (f32[24,1024]{1,0:T(8,128)S(1)}, f32[24,1024]{1,0:T(8,128)S(1)}, u32[]{:S(2)}, u32[]{:S(2)}) collective-permute-start(f32[24,1024]{1,0:T(8,128)S(1)} %slice_add_fusion.3.refs_4_), channel_id=1, source_target_pairs={{0,4},{4,0},{8,12},{12,8},{1,5},{5,1},{9,13},{13,9},{2,6},{6,2},{1... | collective-permute-start | bytes 294920 | tf_op jit(solution)/shard_map/ppermute | solution.py:349
  104.2 10.1 %collective-permute-start.14 = (f32[24,1024]{1,0:T(8,128)S(1)}, f32[24,1024]{1,0:T(8,128)S(1)}, u32[]{:S(2)}, u32[]{:S(2)}) collective-permute-start(f32[24,1024]{1,0:T(8,128)S(1)} %slice_add_fusion.2.refs_4_), channel_id=1, source_target_pairs={{0,4},{4,0},{8,12},{12,8},{1,5},{5,1},{9,13},{13,9},{2,6},{6,2},{1... | collective-permute-start | bytes 294920 | tf_op jit(solution)/shard_map/ppermute | solution.py:349
  104.8 2.3 %collective-permute-start.22 = (f32[24,1024]{1,0:T(8,128)S(1)}, f32[24,1024]{1,0:T(8,128)S(1)}, u32[]{:S(2)}, u32[]{:S(2)}) collective-permute-start(f32[24,1024]{1,0:T(8,128)S(1)} %slice_add_fusion.refs_4_), channel_id=1, source_target_pairs={{0,4},{4,0},{8,12},{12,8},{1,5},{5,1},{9,13},{13,9},{2,6},{6,2},{1... | collective-permute-start | bytes 294920 | tf_op jit(solution)/shard_map/ppermute | solution.py:349
  107.1 14.0 %collective-permute-start.6 = (f32[24,512]{1,0:T(8,128)S(1)}, f32[24,512]{1,0:T(8,128)S(1)}, u32[]{:S(2)}, u32[]{:S(2)}) collective-permute-start(f32[24,512]{1,0:T(8,128)S(1)} %slice_add_fusion.5.refs_4_), channel_id=1, source_target_pairs={{0,4},{4,0},{8,12},{12,8},{1,5},{5,1},{9,13},{13,9},{2,6},{6,2},{1... | collective-permute-start | bytes 147464 | tf_op jit(solution)/shard_map/ppermute | solution.py:349

commit v3 on v2

--- a/solution.py
+++ b/solution.py
@@ -18,6 +18,7 @@
 OPEN_LIMIT = 20 * 2**20
 LIMIT = 12 * 2**20
 PIECES = 4
+GROUPS = 4
 LAST = (((1,), (1,)), ((), ()))
 
 
@@ -80,33 +81,57 @@
     return (far, near, far, near)
 
 
-def with_design(left_ref, geno, outs, small, core, place, half):
+def design_kernel(chips, rows, half, place_ref, left_ref, geno_ref, *refs):
+    outs, (small, table) = refs[:4], refs[4:]
     give_far, _, keep_far, _ = outs
+    chip, core = place_ref[0], place_ref[1]
     far = give_far.shape[0] - half
-    snps = geno.shape[1]
+    snps = geno_ref.shape[1]
     size = 2 * half
     design = left_ref[snps:, :]
-    product = jnp.dot(design, geno[...], preferred_element_type=F32)
+    product = jnp.dot(design, geno_ref[...], preferred_element_type=F32)
     product = (product[2 * size :] + product[size : 2 * size]) + product[:size]
-    wide = geno[...].astype(F32)
+    wide = geno_ref[...].astype(F32)
     square = jnp.sum(wide * wide, axis=0, keepdims=True)
     row = lax.broadcasted_iota(jnp.int32, (size, snps), 0)
     product = jnp.where(row == SQUARE, square, product)
     product = jnp.concatenate([product, jnp.zeros((LANES - size, snps), F32)], axis=0)
-    place[...] = product.T
+    table[...] = product.T
+    for slot in range(chips):
+        target = lax.rem(chip + slot + 1, chips) * (2 * rows)
+        for side, own in ((0, 1 - core), (1, core)):
+            start = pl.multiple_of(target + own * rows, rows)
+            if slot < chips - 1:
+                outs[2 * side][slot * rows : (slot + 1) * rows, :] = table[pl.ds(start, rows), :]
+            else:
+                outs[2 * side + 1][...] = table[pl.ds(start, rows), :]
     gram = lax.dot_general(design, design, LAST, preferred_element_type=F32)
     total = jnp.zeros((size, size), F32)
     for tall, flat in ((2, 0), (0, 2), (1, 1), (1, 0), (0, 1), (0, 0)):
         total = total + gram[tall * size : (tall + 1) * size, flat * size : (flat + 1) * size]
-    small[:, 0:LANES] = jnp.concatenate([total, jnp.zeros((size, LANES - size), F32)], axis=1)
-    give_far[far:, :] = small[pl.ds(pl.multiple_of((1 - core) * half, half), half), 0:LANES]
-    keep_far[far:, :] = small[pl.ds(pl.multiple_of(core * half, half), half), 0:LANES]
+    small[...] = jnp.concatenate([total, jnp.zeros((size, LANES - size), F32)], axis=1)
+    give_far[far:, :] = small[pl.ds(pl.multiple_of((1 - core) * half, half), half), :]
+    keep_far[far:, :] = small[pl.ds(pl.multiple_of(core * half, half), half), :]
+
+
+def with_design(place, left, geno, chips, rows, half):
+    subjects, snps = geno.shape
+    return pl.pallas_call(
+        functools.partial(design_kernel, chips, rows, half),
+        out_shape=part_shapes(chips, rows, half, LANES),
+        in_specs=[SMEM, VMEM, VMEM],
+        out_specs=(VMEM,) * 4,
+        scratch_shapes=[pltpu.VMEM((2 * half, LANES), F32), pltpu.VMEM((snps, LANES), F32)],
+        compiler_params=pltpu.CompilerParams(vmem_limit_bytes=LIMIT),
+        cost_estimate=cost(2 * 6 * half * subjects * snps, 2 * subjects * snps),
+        name="with_design",
+    )(place, left, geno)
 
 
 def open_kernel(chips, rows, half, widths, place_ref, geno_ref, cov_ref, pheno_ref, *refs):
-    left_ref, base, outs = refs[0], refs[1:5], refs[5:9]
-    ahead_refs = refs[9:-7]
-    geno, turned, design, first, small, table, sems = refs[-7:]
+    left_ref, geno, outs = refs[0], refs[1], refs[2:6]
+    ahead_refs = refs[6:-5]
+    turned, design, first, small, sems = refs[-5:]
     chip, core = place_ref[0], place_ref[1]
     covs, subjects = cov_ref.shape
     snps = 2 * chips * rows
@@ -121,7 +146,7 @@
         block = column_block(pheno_ref, start, ahead_ref.shape[1])
         ahead_copies += block_copies(block, ahead_ref, sems, used + index * PIECES, 0)
         start += ahead_ref.shape[1]
-    for copy in geno_copies + first_copies + ahead_copies:
+    for copy in geno_copies + first_copies:
         copy.start()
     top = lax.broadcasted_iota(jnp.int32, (8, subjects), 0)
     design[0:8, :] = jnp.where(top == 0, 1.0, 0.0)
@@ -130,21 +155,19 @@
     cov_copy.wait()
     for index, part in enumerate(split_three(design[...])):
         left_ref[snps + index * 2 * half : snps + (index + 1) * 2 * half, :] = part
-    step = subjects // PIECES
-    for index, copy in enumerate(geno_copies):
-        copy.wait()
+    step = subjects // GROUPS
+    for index in range(GROUPS):
+        for copy in geno_copies[index * PIECES // GROUPS : (index + 1) * PIECES // GROUPS]:
+            copy.wait()
         turned[:, index * step : (index + 1) * step] = geno[index * step : (index + 1) * step, :].T
-    with_design(left_ref, geno, base, small, core, table, half)
+    for copy in ahead_copies:
+        copy.start()
     for slot in range(chips):
         target = lax.rem(chip + slot + 1, chips) * (2 * rows)
         for side, own in ((0, 1 - core), (1, core)):
             low = (side * chips + slot) * rows
             start = pl.multiple_of(target + own * rows, rows)
             left_ref[low : low + rows, :] = turned[pl.ds(start, rows), :]
-            if slot < chips - 1:
-                base[2 * side][slot * rows : (slot + 1) * rows, :] = table[pl.ds(start, rows), :]
-            else:
-                base[2 * side + 1][...] = table[pl.ds(start, rows), :]
     multiply(left_ref, first, first_copies, outs, small, core, rows, half)
     for copy in ahead_copies:
         copy.wait()
@@ -152,6 +175,10 @@
 
 def cost(flops, moved):
     return pl.CostEstimate(flops=flops, bytes_accessed=moved, transcendentals=0)
+
+
+def in_hbm(array):
+    return pltpu.with_memory_space_constraint(array, pltpu.HBM)
 
 
 SMEM = pl.BlockSpec(memory_space=pltpu.SMEM)
@@ -164,44 +191,57 @@
     subjects, snps = dosage.shape
     height = snps + 6 * half
     left = jax.ShapeDtypeStruct((height, subjects), BF16)
-    ahead = [jax.ShapeDtypeStruct((subjects, later), BF16) for later in widths[1:]]
-    parts = part_shapes(chips, rows, half, LANES) + part_shapes(chips, rows, half, width)
+    ahead = [jax.ShapeDtypeStruct((subjects, later), BF16) for later in widths[1:2]]
+    geno = jax.ShapeDtypeStruct((subjects, snps), BF16)
+    parts = part_shapes(chips, rows, half, width)
     return pl.pallas_call(
         functools.partial(open_kernel, chips, rows, half, widths),
-        out_shape=(left, *parts, *ahead),
+        out_shape=(left, geno, *parts, *ahead),
         in_specs=[SMEM, HBM, HBM, HBM],
-        out_specs=(VMEM,) * (9 + len(ahead)),
+        out_specs=(VMEM,) * (6 + len(ahead)),
         scratch_shapes=[
-            pltpu.VMEM((subjects, snps), BF16),
             pltpu.VMEM((snps, subjects), BF16),
             pltpu.VMEM((2 * half, subjects), F32),
             pltpu.VMEM((subjects, width), BF16),
-            pltpu.VMEM((2 * half, max(width, LANES)), F32),
-            pltpu.VMEM((snps, LANES), F32),
-            pltpu.SemaphoreType.DMA((1 + len(widths) * PIECES + max(width // STRIP, 1),)),
+            pltpu.VMEM((2 * half, width), F32),
+            pltpu.SemaphoreType.DMA((1 + 2 * PIECES + max(width // STRIP, 1),)),
         ],
         compiler_params=pltpu.CompilerParams(vmem_limit_bytes=OPEN_LIMIT),
         cost_estimate=cost(2 * height * subjects * width, 4 * snps * subjects),
         name="open",
-    )(place, dosage, cov_rows, phenotype)
-
-
-def product_kernel(rows, half, place_ref, left_ref, pheno_ref, *refs):
-    multiply(left_ref, pheno_ref, [], refs[:4], refs[4], place_ref[1], rows, half)
-
-
-def product(place, left, phenotype, chips, rows, half):
+    )(place, in_hbm(dosage), in_hbm(cov_rows), in_hbm(phenotype))
+
+
+def product_kernel(rows, half, start, place_ref, left_ref, here_ref, pheno_ref, *refs):
+    outs, later, (small, sems) = refs[:4], refs[4:-2], refs[-2:]
+    core = place_ref[1]
+    copies = []
+    for target in later:
+        copies += block_copies(column_block(pheno_ref, start, target.shape[1]), target, sems, 0, 0)
+    for copy in copies:
+        copy.start()
+
+    @pl.when(core >= 0)
+    def _():
+        multiply(left_ref, here_ref, [], outs, small, core, rows, half)
+
+    for copy in copies:
+        copy.wait()
+
+
+def product(place, left, here, phenotype, start, later, chips, rows, half):
     height, subjects = left.shape
-    width = phenotype.shape[1]
-    return pl.pallas_call(
-        functools.partial(product_kernel, rows, half),
-        out_shape=part_shapes(chips, rows, half, width),
-        in_specs=[SMEM, VMEM, VMEM],
-        out_specs=(VMEM,) * 4,
-        scratch_shapes=[pltpu.VMEM((2 * half, width), F32)],
+    width = here.shape[1]
+    ahead = [jax.ShapeDtypeStruct((subjects, size), BF16) for size in later]
+    return pl.pallas_call(
+        functools.partial(product_kernel, rows, half, start + width),
+        out_shape=(*part_shapes(chips, rows, half, width), *ahead),
+        in_specs=[SMEM, VMEM, VMEM, HBM],
+        out_specs=(VMEM,) * (4 + len(ahead)),
+        scratch_shapes=[pltpu.VMEM((2 * half, width), F32), pltpu.SemaphoreType.DMA((PIECES,))],
         compiler_params=pltpu.CompilerParams(vmem_limit_bytes=LIMIT),
         cost_estimate=cost(2 * height * subjects * width, 2 * subjects * width),
-    )(place, left, phenotype)
+    )(place, left, here, in_hbm(phenotype))
 
 
 def solve_kernel(live, half, count, *refs):
@@ -273,7 +313,7 @@
 
 def finish(done, total, place, start, dof, inverse, white, geno_var, half_rows, rest_rows, terms):
     rows, width = terms[0].shape
-    tile = min(STRIP, width)
+    tile = min(TILE, width)
     first = start // tile
     args = [place, inverse, white, geno_var, half_rows, rest_rows, *terms]
     specs = [SMEM] + [VMEM] * (len(args) - 1)
@@ -297,16 +337,80 @@
     )(*args)
 
 
+def fit_kernel(count, *refs):
+    place_ref, inverse_ref, white_ref, half_ref, rest_ref = refs[:5]
+    terms, (cross_ref, var_ref, small) = refs[5 : 5 + count], refs[5 + count :]
+    half = half_ref.shape[0]
+    core = place_ref[1]
+    small[pl.ds(pl.multiple_of(core * half, half), half), :] = half_ref[...]
+    small[pl.ds(pl.multiple_of((1 - core) * half, half), half), :] = rest_ref[...]
+    white = jnp.dot(inverse_ref[:, : 2 * half], small[...], precision=HI, preferred_element_type=F32)
+    pheno_var = small[SQUARE : SQUARE + 1, :] - jnp.sum(white * white, axis=0, keepdims=True)
+    var_ref[...] = jnp.broadcast_to(pheno_var, var_ref.shape)
+    fitted = jnp.dot(white_ref[:, : 2 * half], white, precision=HI, preferred_element_type=F32)
+    cross = terms[0][...]
+    for term in terms[1:]:
+        cross = cross + term[...]
+    cross_ref[...] = cross - fitted
+
+
+def fit(place, inverse, white, half_rows, rest_rows, terms):
+    rows, width = terms[0].shape
+    args = [place, inverse, white, half_rows, rest_rows, *terms]
+    return pl.pallas_call(
+        functools.partial(fit_kernel, len(terms)),
+        out_shape=(jax.ShapeDtypeStruct((rows, width), F32), jax.ShapeDtypeStruct((8, width), F32)),
+        in_specs=[SMEM] + [VMEM] * (len(args) - 1),
+        out_specs=(VMEM, VMEM),
+        scratch_shapes=[pltpu.VMEM((2 * half_rows.shape[0], width), F32)],
+        compiler_params=pltpu.CompilerParams(vmem_limit_bytes=LIMIT),
+        cost_estimate=cost(2 * 256 * 256 * width, 16 * rows * width),
+        name="fit",
+    )(*args)
+
+
+def close_kernel(dof, count, *refs):
+    geno_var_ref, pheno_var_ref = refs[:2]
+    terms, out_ref = refs[2 : 2 + count], refs[-1]
+    tile = out_ref.shape[1]
+    low = pl.multiple_of(pl.program_id(0) * tile, tile)
+    cross = terms[0][:, pl.ds(low, tile)]
+    for term in terms[1:]:
+        cross = cross + term[:, pl.ds(low, tile)]
+    pheno_var = pheno_var_ref[0:1, pl.ds(low, tile)]
+    out_ref[...] = cross * dof * lax.rsqrt(geno_var_ref[:, 0:1] * pheno_var - cross * cross)
+
+
+def close(done, total, start, dof, geno_var, pheno_var, terms):
+    rows, width = terms[0].shape
+    tile = min(STRIP, width)
+    first = start // tile
+    args = [geno_var, pheno_var, *terms]
+    specs = [VMEM] * len(args)
+    aliases = {}
+    if done is not None:
+        aliases = {len(args): 0}
+        args.append(done)
+        specs.append(HBM)
+    return pl.pallas_call(
+        functools.partial(close_kernel, dof, len(terms)),
+        grid=(width // tile,),
+        out_shape=jax.ShapeDtypeStruct((rows, total), F32),
+        in_specs=specs,
+        out_specs=pl.BlockSpec((rows, tile), lambda j: (0, first + j)),
+        input_output_aliases=aliases,
+        compiler_params=pltpu.CompilerParams(vmem_limit_bytes=LIMIT),
+        cost_estimate=cost(8 * rows * width, 12 * rows * width),
+        name="close",
+    )(*args)
+
+
 def chunk_widths(total):
     units = total // TILE
-    if total % TILE or units < 3:
+    if total % TILE or units < 2:
         return [total]
-    sizes = [1]
-    left = units - 2
-    while left > 0:
-        sizes.append(min(2, left))
-        left -= sizes[-1]
-    sizes.append(1)
+    wide, odd = divmod(max(units - 4, 0), 2)
+    sizes = [1] * min(units - units // 2, 2) + [2] * wide + [1] * odd + [1] * min(units // 2, 2)
     return [size * TILE for size in sizes]
 
 
@@ -324,16 +428,20 @@
     place = jnp.stack([place_index // 2, lax.rem(place_index, 2)]).astype(jnp.int32)
     sibling = [(i, i ^ 1) for i in range(devices)]
 
-    def near_sums(parts):
+    def near_sums(parts, apart=False):
         give_far, give_near, keep_far, keep_near = parts
         got_far = lax.ppermute(give_far, "subj", sibling)
         got_near = lax.ppermute(give_near, "subj", sibling)
+        terms = [keep_near, got_near]
+        if apart:
+            blocks = [keep_far[low : low + rows] + got_far[low : low + rows] for low in range(0, far, rows)]
+            return terms, blocks, keep_far[far:] + got_far[far:]
         summed = keep_far + got_far
         if chips == 2:
-            return [keep_near, got_near], [summed]
+            return terms, [summed], summed[rows:]
         own_half = summed[far:]
         blocks = [jnp.concatenate([summed[low : low + rows], own_half], axis=0) for low in range(0, far, rows)]
-        return [keep_near, got_near], blocks
+        return terms, blocks, own_half
 
     def far_terms(blocks):
         came = []
@@ -342,42 +450,56 @@
             came.append(lax.ppermute(block, "subj", moves))
         return came
 
-    def gather_half(blocks, came):
-        halves = blocks[0][rows:]
+    def gather_half(halves, came):
         for block in came:
-            halves = halves + block[rows:]
+            halves = halves + block
         rest = lax.ppermute(halves, "subj", sibling)
         return halves, rest
 
     widths = chunk_widths(verts)
-    left, *parts = open_up(
+    last = len(widths)
+    left, geno, *parts = open_up(
         place, dosage, covariates.T, phenotype, chips, rows, half, widths
     )
-    ahead = parts[8:]
-    sums = [near_sums(parts[4:8])]
+    ahead = parts[4:]
+    sums = [near_sums(parts[:4])]
     came = [far_terms(sums[0][1])]
-    terms, blocks = near_sums(parts[:4])
+    parts = with_design(place, left, geno, chips, rows, half)
+    terms, blocks, own_half = near_sums(parts)
     base_came = far_terms(blocks)
-    halves, rest = gather_half(blocks, base_came)
+    halves, rest = gather_half(own_half, [block[rows:] for block in base_came])
     inverse, white, geno_var = solve(
         place, halves, rest, terms + [block[:rows] for block in base_came], live
     )
     dof = float(subjects * devices - covs - 2) ** 0.5
 
     start = widths[0]
-    for index in range(1, len(widths)):
-        parts = product(place, left, ahead[index - 1], chips, rows, half)
+    for index in range(1, last):
+        tag = index + 1
+        parts = product(
+            place, left, ahead[0], phenotype, start, widths[index + 1 : index + 2], chips, rows, half
+        )
+        ahead = parts[4:]
         start += widths[index]
-        sums.append(near_sums(parts))
+        sums.append(near_sums(parts[:4], apart=tag == last))
+        if tag == last:
+            last_half = far_terms([sums[-1][2]] * (chips - 1))
         came.append(far_terms(sums[-1][1]))
     out = None
     start = 0
     for index, width in enumerate(widths):
-        terms, blocks = sums[index]
-        halves, rest = gather_half(blocks, came[index])
-        out = finish(
-            out, verts, place, start, dof, inverse, white, geno_var, halves, rest, terms + came[index]
-        )
+        tag = index + 1
+        terms, _, own_half = sums[index]
+        if tag < last:
+            half_came = [block[rows:] for block in came[index]]
+            halves, rest = gather_half(own_half, half_came)
+            out = finish(
+                out, verts, place, start, dof, inverse, white, geno_var, halves, rest, terms + came[index]
+            )
+        else:
+            halves, rest = gather_half(own_half, last_half)
+            cross, pheno_var = fit(place, inverse, white, halves, rest, terms)
+            out = close(out, verts, start, dof, geno_var, pheno_var, [cross] + came[index])
         start += width
     return out
 

time: 124 us -> 120 us (0.968)
  local copies, waits for them, and re-layouts: 2.57 us -> 0.01 us
  Pallas kernels: 48.3 us -> 46 us
  starting transfers between devices: 17.2 us -> 19 us
    pallas_call x6, Pallas kernels: 18.1 us -> 13 us  [finish(): pl.pallas_call(functools.partial(finish_kernel, dof, len(terms)), grid=(w...]
    pallas_call x5 -> x9, Pallas kernels: 16.1 us -> 21.2 us  [the longest x6 17.8 us: product(): pl.pallas_call(functools.partial(product_kernel, rows, half, start + widt...]
    unnamed x4 -> x0, local copies, waits for them, and re-layouts: 2.56 us -> none
    ppermute x7 -> x9, starting transfers between devices: 11.6 us -> 14.1 us  [far_terms(): came.append(lax.ppermute(block, 'subj', moves))]
    pallas_call x1, Pallas kernels: 8.09 us -> 5.82 us  [open_up(): pl.pallas_call(functools.partial(open_kernel, chips, rows, half, widths),...]
    ppermute x7 -> x9, waiting for transfers between devices: 53.5 us -> 51.2 us  [far_terms(): came.append(lax.ppermute(block, 'subj', moves))]
    ppermute x7 -> x8, starting transfers between devices: 2.21 us -> 0.83 us  [near_sums(): got_near = lax.ppermute(give_near, 'subj', sibling)]
    ppermute x7 -> x8, waiting for transfers between devices: 0.83 us -> 2.2 us  [gather_half(): rest = lax.ppermute(halves, 'subj', sibling)]
  transfers between devices with their start and end apart: 28 -> 33, of which waited for: 9 -> 9; matrix products, arithmetic and copies ran while one was open for 0% -> 0% of each run, Pallas kernels for 31% -> 18%
where the time goes in v3:
time: 120 us
  waiting for transfers between devices  53.9 us (45%)
  Pallas kernels  46 us (38%)
  starting transfers between devices  19 us (16%)
    ppermute x9, waiting for transfers between devices, far_terms(): came.append(lax.ppermute(block, 'subj', moves))  51.2 us
    pallas_call x6, Pallas kernels, product(): pl.pallas_call(functools.partial(product_kernel, rows, half, start + widt...  17.8 us
    ppermute x9, starting transfers between devices, far_terms(): came.append(lax.ppermute(block, 'subj', moves))  14.1 us
    pallas_call x6, Pallas kernels, finish(): pl.pallas_call(functools.partial(finish_kernel, dof, len(terms)), grid=(w...  13 us
    pallas_call x1, Pallas kernels, solve(): pl.pallas_call(functools.partial(solve_kernel, live, half, len(terms)), o...  6.05 us
    pallas_call x1, Pallas kernels, open_up(): pl.pallas_call(functools.partial(open_kernel, chips, rows, half, widths),...  5.82 us
  transfers between devices with their start and end apart: 33, of which 9 were waited for; matrix products, arithmetic and copies ran while one was open for 0% of the time, Pallas kernels for 18%

profile of v3, /device:TPU:0, one launch (start us, length us, event | category | flops | bytes accessed | tf_op | source)
XLA Modules:
  0.0 119.8 jit_solution(14282215061226170429)
XLA Ops:
  0.0 0.1 pad_add_fusion.place_ref.refs_0_
  0.1 5.8 %open.1 = (bf16[656,2048]{1,0:T(8,128)(2,1)S(1)}, bf16[2048,512]{1,0:T(8,128)(2,1)S(1)}, f32[152,512]{1,0:T(8,128)S(1)}, f32[128,512]{1,0:T(8,128)S(1)}, f32[152...) custom-call(s32[2]{0:T(128)S(1)} %pad_add_fusion.place_ref.refs_0_, ...), custom_call_target="tpu_custom_call" | custom-call | flops 1375731712 | bytes 4194304 | tf_op jit(solution)/shard_map/open/pallas_call | solution.py:197
  5.9 2.8 %shard_map.37 = (f32[152,512]{1,0:T(8,128)S(1)}, f32[128,512]{1,0:T(8,128)S(1)}, f32[152,512]{1,0:T(8,128)S(1)}, f32[128,512]{1,0:T(8,128)S(1)}, bf16[2048,1024]{1,0:T(8,128)(2,1)S(1)}) custom-call(s32[2]{0:T(128)S(1)} %pad_add_fusion.place_ref.refs_0_, bf16[656,2048]{1,0:T(8,128)(2,1)S(1)} %get-tuple-element.50.left_ref, ...), custom_call_target="tpu_custom_call" | custom-call | flops 1375731712 | bytes 2097152 | tf_op jit(solution)/shard_map/pallas_call | solution.py:236
  8.7 3.5 %shard_map.38 = (f32[152,1024]{1,0:T(8,128)S(1)}, f32[128,1024]{1,0:T(8,128)S(1)}, f32[152,1024]{1,0:T(8,128)S(1)}, f32[128,1024]{1,0:T(8,128)S(1)}, bf16[2048,1024]{1,0:T(8,128)(2,1)S(1)}) custom-call(s32[2]{0:T(128)S(1)} %pad_add_fusion.place_ref.refs_0_, bf16[656,2048]{1,0:T(8,128)(2,1)S(1)} %get-tuple-element.50.left_ref, ...), custom_call_target="tpu_custom_call" | custom-call | flops 2751463424 | bytes 4194304 | tf_op jit(solution)/shard_map/pallas_call | solution.py:236
  12.2 3.5 %shard_map.39 = (f32[152,1024]{1,0:T(8,128)S(1)}, f32[128,1024]{1,0:T(8,128)S(1)}, f32[152,1024]{1,0:T(8,128)S(1)}, f32[128,1024]{1,0:T(8,128)S(1)}, bf16[2048,1024]{1,0:T(8,128)(2,1)S(1)}) custom-call(s32[2]{0:T(128)S(1)} %pad_add_fusion.place_ref.refs_0_, bf16[656,2048]{1,0:T(8,128)(2,1)S(1)} %get-tuple-element.50.left_ref, ...), custom_call_target="tpu_custom_call" | custom-call | flops 2751463424 | bytes 4194304 | tf_op jit(solution)/shard_map/pallas_call | solution.py:236
  15.8 3.5 %shard_map.40 = (f32[152,1024]{1,0:T(8,128)S(1)}, f32[128,1024]{1,0:T(8,128)S(1)}, f32[152,1024]{1,0:T(8,128)S(1)}, f32[128,1024]{1,0:T(8,128)S(1)}, bf16[2048,512]{1,0:T(8,128)(2,1)S(1)}) custom-call(s32[2]{0:T(128)S(1)} %pad_add_fusion.place_ref.refs_0_, bf16[656,2048]{1,0:T(8,128)(2,1)S(1)} %get-tuple-element.50.left_ref, ...), custom_call_target="tpu_custom_call" | custom-call | flops 2751463424 | bytes 4194304 | tf_op jit(solution)/shard_map/pallas_call | solution.py:236
  19.3 2.2 %shard_map.41 = (f32[152,512]{1,0:T(8,128)S(1)}, f32[128,512]{1,0:T(8,128)S(1)}, f32[152,512]{1,0:T(8,128)S(1)}, f32[128,512]{1,0:T(8,128)S(1)}, bf16[2048,512]{1,0:T(8,128)(2,1)S(1)}) custom-call(s32[2]{0:T(128)S(1)} %pad_add_fusion.place_ref.refs_0_, bf16[656,2048]{1,0:T(8,128)(2,1)S(1)} %get-tuple-element.50.left_ref, ...), custom_call_target="tpu_custom_call" | custom-call | flops 1375731712 | bytes 2097152 | tf_op jit(solution)/shard_map/pallas_call | solution.py:236
  21.5 2.3 %shard_map.42 = (f32[152,512]{1,0:T(8,128)S(1)}, f32[128,512]{1,0:T(8,128)S(1)}, f32[152,512]{1,0:T(8,128)S(1)}, f32[128,512]{1,0:T(8,128)S(1)}) custom-call(s32[2]{0:T(128)S(1)} %pad_add_fusion.place_ref.refs_0_, bf16[656,2048]{1,0:T(8,128)(2,1)S(1)} %get-tuple-element.50.left_ref, bf16[2048,512]{1,0:T(8,128)(2,1)S(1)} %get-tuple-element.64.here_ref, ...), custom_call_target="tpu_custom_call" | custom-call | flops 1375731712 | bytes 2097152 | tf_op jit(solution)/shard_map/pallas_call | solution.py:236
  23.8 0.5 collective-permute-start.4
  24.3 0.1 collective-permute-start.21
  24.4 1.3 %with_design.1 = (f32[152,128]{1,0:T(8,128)S(1)}, f32[128,128]{1,0:T(8,128)S(1)}, f32[152,128]{1,0:T(8,128)S(1)}, f32[128,128]{1,0:T(8,128)S(1)}) custom-call(s32[2]{0:T(128)S(1)} %pad_add_fusion.place_ref.refs_0_, bf16[656,2048]{1,0:T(8,128)(2,1)S(1)} %get-tuple-element.50.left_ref, bf16[2048,512]{1,0:T(8,128)(2,1)S(1)} %get-tuple-element.51.geno_ref), custom_call_target="tpu_custom_call" | custom-call | flops 301989888 | bytes 2097152 | tf_op jit(solution)/shard_map/with_design/pallas_call | solution.py:119
  25.8 0.5 collective-permute-start
  26.2 0.1 collective-permute-start.3
  26.3 0.4 collective-permute-start.29
  26.8 0.4 collective-permute-done
  27.2 0.4 collective-permute-start.25
  27.5 0.2 collective-permute-start.9
  27.8 0.0 collective-permute-done.4
  27.8 2.8 %collective-permute-start.1 = (f32[152,128]{1,0:T(8,128)S(1)}, f32[152,128]{1,0:T(8,128)S(1)}, u32[]{:S(2)}, u32[]{:S(2)}) collective-permute-start(f32[152,128]{1,0:T(8,128)S(1)} %add.52), channel_id=1, source_target_pairs={{0,8},{4,12},{8,0},{12,4},{1,9},{5,13},{9,1},{13,5},{2,10},{6,14},... | collective-permute-start | bytes 233480 | tf_op jit(solution)/shard_map/ppermute | solution.py:450
  30.6 2.7 %collective-permute-done.1 = f32[152,128]{1,0:T(8,128)S(1)} collective-permute-done((f32[152,128]{1,0:T(8,128)S(1)}, f32[152,128]{1,0:T(8,128)S(1)}, u32[]{:S(2)}, u32[]{:S(2)}) %collective-permute-start.1) | collective-permute-done | bytes 77856 | tf_op jit(solution)/shard_map/ppermute | solution.py:450
  33.3 1.7 %collective-permute-start.5 = (f32[24,512]{1,0:T(8,128)S(1)}, f32[24,512]{1,0:T(8,128)S(1)}, u32[]{:S(2)}, u32[]{:S(2)}) collective-permute-start(f32[24,512]{1,0:T(8,128)S(1)} %slice_add_fusion.7), channel_id=1, source_target_pairs={{0,8},{4,12},{8,0},{12,4},{1,9},{5,13},{9,1},{13,5},{2,10},{6,14},... | collective-permute-start | bytes 147464 | tf_op jit(solution)/shard_map/ppermute | solution.py:450
  35.0 0.0 collective-permute-done.29
  35.0 2.3 %collective-permute-done.5 = f32[24,512]{1,0:T(8,128)S(1)} collective-permute-done((f32[24,512]{1,0:T(8,128)S(1)}, f32[24,512]{1,0:T(8,128)S(1)}, u32[]{:S(2)}, u32[]{:S(2)}) %collective-permute-start.5) | collective-permute-done | bytes 49184 | tf_op jit(solution)/shard_map/ppermute | solution.py:450
  37.4 0.0 collective-permute-start.17
  37.4 0.5 collective-permute-start.2
  38.0 0.1 add.63
  38.0 1.4 %collective-permute-done.2.refs_2_ = f32[24,128]{1,0:T(8,128)S(1)} collective-permute-done((f32[24,128]{1,0:T(8,128)S(1)}, f32[24,128]{1,0:T(8,128)S(1)}, u32[]{:S(2)}, u32[]{:S(2)}) %collective-permute-start.2) | collective-permute-done | bytes 12320 | tf_op jit(solution)/shard_map/ppermute | solution.py:456
  39.4 0.1 collective-permute-start.13
  39.6 1.7 %collective-permute-start.30 = (f32[152,512]{1,0:T(8,128)S(1)}, f32[152,512]{1,0:T(8,128)S(1)}, u32[]{:S(2)}, u32[]{:S(2)}) collective-permute-start(f32[152,512]{1,0:T(8,128)S(1)} %add.67), channel_id=1, source_target_pairs={{0,8},{4,12},{8,0},{12,4},{1,9},{5,13},{9,1},{13,5},{2,10},{6,14},... | collective-permute-start | bytes 933896 | tf_op jit(solution)/shard_map/ppermute | solution.py:450
  41.3 0.1 collective-permute-start.6
  41.4 0.0 collective-permute-done.9
  41.4 0.3 collective-permute-start.22
  41.8 6.0 %solve.1 = (f32[48,128]{1,0:T(8,128)S(1)}, f32[128,128]{1,0:T(8,128)S(1)}, f32[128,128]{1,0:T(8,128)S(1)}) custom-call(s32[2]{0:T(128)S(1)} %pad_add_fusion.place_ref.refs_0_, f32[24,128]{1,0:T(8,128)S(1)} %slice_add_fusion.8.refs_1_, f32[24,128]{1,0:T(8,128)S(1)} %collective-permute-done.2.refs_2_, f32[128,128]{1,0:T(8,128)S(1)} %get-tuple-element.54.refs_3_, ...), custom_call_target="tpu_custom_call" | custom-call | flops 5000000000 | bytes 65536 | tf_op jit(solution)/shard_map/solve/pallas_call | solution.py:283
  47.9 0.0 collective-permute-done.6.refs_4_
  47.9 0.1 collective-permute-start.32
  48.0 0.0 collective-permute-done.17
  48.0 1.7 %collective-permute-start.26 = (f32[152,512]{1,0:T(8,128)S(1)}, f32[152,512]{1,0:T(8,128)S(1)}, u32[]{:S(2)}, u32[]{:S(2)}) collective-permute-start(f32[152,512]{1,0:T(8,128)S(1)} %add.65), channel_id=1, source_target_pairs={{0,8},{4,12},{8,0},{12,4},{1,9},{5,13},{9,1},{13,5},{2,10},{6,14},... | collective-permute-start | bytes 933896 | tf_op jit(solution)/shard_map/ppermute | solution.py:450
  49.9 1.1 fit.1
  51.0 0.1 add.61
  51.1 0.2 collective-permute-start.28
  51.2 0.1 add.59
  51.3 0.4 collective-permute-start.18
  51.8 0.1 collective-permute-start.24
  51.9 17.9 %collective-permute-done.26.refs_8_ = f32[152,512]{1,0:T(8,128)S(1)} collective-permute-done((f32[152,512]{1,0:T(8,128)S(1)}, f32[152,512]{1,0:T(8,128)S(1)}, u32[]{:S(2)}, u32[]{:S(2)}) %collective-permute-start.26) | collective-permute-done | bytes 311328 | tf_op jit(solution)/shard_map/ppermute | solution.py:450
  69.8 1.7 %collective-permute-start.14 = (f32[152,1024]{1,0:T(8,128)S(1)}, f32[152,1024]{1,0:T(8,128)S(1)}, u32[]{:S(2)}, u32[]{:S(2)}) collective-permute-start(f32[152,1024]{1,0:T(8,128)S(1)} %add.59), channel_id=1, source_target_pairs={{0,8},{4,12},{8,0},{12,4},{1,9},{5,13},{9,1},{13,5},{2,10},{6,14},... | collective-permute-start | bytes 1867784 | tf_op jit(solution)/shard_map/ppermute | solution.py:450
  71.6 0.3 collective-permute-start.16
  71.9 11.3 %collective-permute-done.18.refs_8_ = f32[152,1024]{1,0:T(8,128)S(1)} collective-permute-done((f32[152,1024]{1,0:T(8,128)S(1)}, f32[152,1024]{1,0:T(8,128)S(1)}, u32[]{:S(2)}, u32[]{:S(2)}) %collective-permute-start.18) | collective-permute-done | bytes 622624 | tf_op jit(solution)/shard_map/ppermute | solution.py:450
  83.2 1.7 %collective-permute-start.10 = (f32[152,512]{1,0:T(8,128)S(1)}, f32[152,512]{1,0:T(8,128)S(1)}, u32[]{:S(2)}, u32[]{:S(2)}) collective-permute-start(f32[152,512]{1,0:T(8,128)S(1)} %add.57), channel_id=1, source_target_pairs={{0,8},{4,12},{8,0},{12,4},{1,9},{5,13},{9,1},{13,5},{2,10},{6,14},... | collective-permute-start | bytes 933896 | tf_op jit(solution)/shard_map/ppermute | solution.py:450
  84.9 0.1 collective-permute-start.31
  85.0 0.5 collective-permute-start.27
  85.5 11.0 %collective-permute-done.14.refs_8_ = f32[152,1024]{1,0:T(8,128)S(1)} collective-permute-done((f32[152,1024]{1,0:T(8,128)S(1)}, f32[152,1024]{1,0:T(8,128)S(1)}, u32[]{:S(2)}, u32[]{:S(2)}) %collective-permute-start.14) | collective-permute-done | bytes 622624 | tf_op jit(solution)/shard_map/ppermute | solution.py:450
  96.5 6.1 %collective-permute-done.10.refs_8_ = f32[152,512]{1,0:T(8,128)S(1)} collective-permute-done((f32[152,512]{1,0:T(8,128)S(1)}, f32[152,512]{1,0:T(8,128)S(1)}, u32[]{:S(2)}, u32[]{:S(2)}) %collective-permute-start.10) | collective-permute-done | bytes 311328 | tf_op jit(solution)/shard_map/ppermute | solution.py:450
  102.6 1.7 %collective-permute-start.8 = (f32[128,512]{1,0:T(8,128)S(1)}, f32[128,512]{1,0:T(8,128)S(1)}, u32[]{:S(2)}, u32[]{:S(2)}) collective-permute-start(f32[128,512]{1,0:T(8,128)S(1)} %slice_add_fusion), channel_id=1, source_target_pairs={{0,8},{4,12},{8,0},{12,4},{1,9},{5,13},{9,1},{13,5},{2,10},{6,14},... | collective-permute-start | bytes 786440 | tf_op jit(solution)/shard_map/ppermute | solution.py:450
  104.3 0.2 collective-permute-start.19
  104.6 0.3 collective-permute-start.15
  104.9 0.8 collective-permute-done.19.refs_5_
  105.6 0.2 collective-permute-start.11
  105.9 1.8 %shard_map.43.refs_9_ = f32[128,5120]{1,0:T(8,128)} custom-call(s32[2]{0:T(128)S(1)} %pad_add_fusion.place_ref.refs_0_, f32[48,128]{1,0:T(8,128)S(1)} %get-tuple-element.57.refs_1_, f32[128,128]{1,0:T(8,128)S(1)} %get-tuple-element.58.refs_2_, f32[128,128]{1,0:T(8,128)S(1)} %get-tuple-element.56.refs_3_.refs_0_, f32[24,512]{1,0:T(8,128)S(1)} %slice_add_fusion.4.refs_4_, ...), custom_call_target="tpu_custom_call" | custom-call | flops 67108864 | bytes 1048576 | tf_op jit(solution)/shard_map/pallas_call | solution.py:325
  107.7 1.8 %shard_map.44.refs_9_ = f32[128,5120]{1,0:T(8,128)} custom-call(s32[2]{0:T(128)S(1)} %pad_add_fusion.place_ref.refs_0_, f32[48,128]{1,0:T(8,128)S(1)} %get-tuple-element.57.refs_1_, f32[128,128]{1,0:T(8,128)S(1)} %get-tuple-element.58.refs_2_, f32[128,128]{1,0:T(8,128)S(1)} %get-tuple-element.56.refs_3_.refs_0_, ...), custom_call_target="tpu_custom_call", output_to_operand_aliasing={{}: (9, {})} | custom-call | flops 67108864 | bytes 1048576 | tf_op jit(solution)/shard_map/pallas_call | solution.py:325
  109.6 2.5 %shard_map.45.refs_9_ = f32[128,5120]{1,0:T(8,128)} custom-call(s32[2]{0:T(128)S(1)} %pad_add_fusion.place_ref.refs_0_, f32[48,128]{1,0:T(8,128)S(1)} %get-tuple-element.57.refs_1_, f32[128,128]{1,0:T(8,128)S(1)} %get-tuple-element.58.refs_2_, f32[128,128]{1,0:T(8,128)S(1)} %get-tuple-element.56.refs_3_.refs_0_, ...), custom_call_target="tpu_custom_call", output_to_operand_aliasing={{}: (9, {})} | custom-call | flops 134217728 | bytes 2097152 | tf_op jit(solution)/shard_map/pallas_call | solution.py:325
  112.0 2.5 %shard_map.46.refs_9_ = f32[128,5120]{1,0:T(8,128)} custom-call(s32[2]{0:T(128)S(1)} %pad_add_fusion.place_ref.refs_0_, f32[48,128]{1,0:T(8,128)S(1)} %get-tuple-element.57.refs_1_, f32[128,128]{1,0:T(8,128)S(1)} %get-tuple-element.58.refs_2_, f32[128,128]{1,0:T(8,128)S(1)} %get-tuple-element.56.refs_3_.refs_0_, ...), custom_call_target="tpu_custom_call", output_to_operand_aliasing={{}: (9, {})} | custom-call | flops 134217728 | bytes 2097152 | tf_op jit(solution)/shard_map/pallas_call | solution.py:325
  114.5 2.5 %shard_map.47.refs_9_ = f32[128,5120]{1,0:T(8,128)} custom-call(s32[2]{0:T(128)S(1)} %pad_add_fusion.place_ref.refs_0_, f32[48,128]{1,0:T(8,128)S(1)} %get-tuple-element.57.refs_1_, f32[128,128]{1,0:T(8,128)S(1)} %get-tuple-element.58.refs_2_, f32[128,128]{1,0:T(8,128)S(1)} %get-tuple-element.56.refs_3_.refs_0_, ...), custom_call_target="tpu_custom_call", output_to_operand_aliasing={{}: (9, {})} | custom-call | flops 134217728 | bytes 2097152 | tf_op jit(solution)/shard_map/pallas_call | solution.py:325
  117.1 1.9 %shard_map.48.refs_4_ = f32[128,5120]{1,0:T(8,128)} custom-call(s32[2]{0:T(128)S(1)} %pad_add_fusion.place_ref.refs_0_, f32[48,128]{1,0:T(8,128)S(1)} %get-tuple-element.57.refs_1_, f32[128,128]{1,0:T(8,128)S(1)} %get-tuple-element.58.refs_2_, f32[128,128]{1,0:T(8,128)S(1)} %get-tuple-element.56.refs_3_.refs_0_, ...), custom_call_target="tpu_custom_call", output_to_operand_aliasing={{}: (9, {})} | custom-call | flops 67108864 | bytes 1048576 | tf_op jit(solution)/shard_map/pallas_call | solution.py:325
  118.9 0.9 close.1
  (38 shorter events, 0.3 us)
Async XLA Ops:
  23.8 4.0 %collective-permute-start.4 = (f32[152,512]{1,0:T(8,128)S(1)}, f32[152,512]{1,0:T(8,128)S(1)}, u32[]{:S(2)}, u32[]{:S(2)}) collective-permute-start(f32[152,512]{1,0:T(8,128)S(1)} %get-tuple-element.66), channel_id=1, source_target_pairs={{0,4},{4,0},{8,12},{12,8},{1,5},{5,1},{9,13},{13,9},{2,6},{6,2},{1... | collective-permute-start | bytes 933896 | tf_op jit(solution)/shard_map/ppermute | solution.py:433
  24.3 13.0 %collective-permute-start.21 = (f32[152,1024]{1,0:T(8,128)S(1)}, f32[152,1024]{1,0:T(8,128)S(1)}, u32[]{:S(2)}, u32[]{:S(2)}) collective-permute-start(f32[152,1024]{1,0:T(8,128)S(1)} %get-tuple-element.84), channel_id=1, source_target_pairs={{0,4},{4,0},{8,12},{12,8},{1,5},{5,1},{9,13},{13,9},{2,6},{6,2},{1... | collective-permute-start | bytes 1867784 | tf_op jit(solution)/shard_map/ppermute | solution.py:433
  25.8 1.4 %collective-permute-start = (f32[152,128]{1,0:T(8,128)S(1)}, f32[152,128]{1,0:T(8,128)S(1)}, u32[]{:S(2)}, u32[]{:S(2)}) collective-permute-start(f32[152,128]{1,0:T(8,128)S(1)} %get-tuple-element.53), channel_id=1, source_target_pairs={{0,4},{4,0},{8,12},{12,8},{1,5},{5,1},{9,13},{13,9},{2,6},{6,2},{1... | collective-permute-start | bytes 233480 | tf_op jit(solution)/shard_map/ppermute | solution.py:433
  26.2 1.3 %collective-permute-start.3 = (f32[128,128]{1,0:T(8,128)S(1)}, f32[128,128]{1,0:T(8,128)S(1)}, u32[]{:S(2)}, u32[]{:S(2)}) collective-permute-start(f32[128,128]{1,0:T(8,128)S(1)} %get-tuple-element.55), channel_id=1, source_target_pairs={{0,4},{4,0},{8,12},{12,8},{1,5},{5,1},{9,13},{13,9},{2,6},{6,2},{1... | collective-permute-start | bytes 196616 | tf_op jit(solution)/shard_map/ppermute | solution.py:434
  26.3 8.7 %collective-permute-start.29 = (f32[152,512]{1,0:T(8,128)S(1)}, f32[152,512]{1,0:T(8,128)S(1)}, u32[]{:S(2)}, u32[]{:S(2)}) collective-permute-start(f32[152,512]{1,0:T(8,128)S(1)} %get-tuple-element.92), channel_id=1, source_target_pairs={{0,4},{4,0},{8,12},{12,8},{1,5},{5,1},{9,13},{13,9},{2,6},{6,2},{1... | collective-permute-start | bytes 933896 | tf_op jit(solution)/shard_map/ppermute | solution.py:433
  27.2 14.2 %collective-permute-start.25 = (f32[152,512]{1,0:T(8,128)S(1)}, f32[152,512]{1,0:T(8,128)S(1)}, u32[]{:S(2)}, u32[]{:S(2)}) collective-permute-start(f32[152,512]{1,0:T(8,128)S(1)} %get-tuple-element.88), channel_id=1, source_target_pairs={{0,4},{4,0},{8,12},{12,8},{1,5},{5,1},{9,13},{13,9},{2,6},{6,2},{1... | collective-permute-start | bytes 933896 | tf_op jit(solution)/shard_map/ppermute | solution.py:433
  27.5 13.9 %collective-permute-start.9 = (f32[152,512]{1,0:T(8,128)S(1)}, f32[152,512]{1,0:T(8,128)S(1)}, u32[]{:S(2)}, u32[]{:S(2)}) collective-permute-start(f32[152,512]{1,0:T(8,128)S(1)} %get-tuple-element.72), channel_id=1, source_target_pairs={{0,4},{4,0},{8,12},{12,8},{1,5},{5,1},{9,13},{13,9},{2,6},{6,2},{1... | collective-permute-start | bytes 933896 | tf_op jit(solution)/shard_map/ppermute | solution.py:433
  27.8 5.5 %collective-permute-start.1 = (f32[152,128]{1,0:T(8,128)S(1)}, f32[152,128]{1,0:T(8,128)S(1)}, u32[]{:S(2)}, u32[]{:S(2)}) collective-permute-start(f32[152,128]{1,0:T(8,128)S(1)} %add.52), channel_id=1, source_target_pairs={{0,8},{4,12},{8,0},{12,4},{1,9},{5,13},{9,1},{13,5},{2,10},{6,14},... | collective-permute-start | bytes 233480 | tf_op jit(solution)/shard_map/ppermute | solution.py:450
  33.3 4.1 %collective-permute-start.5 = (f32[24,512]{1,0:T(8,128)S(1)}, f32[24,512]{1,0:T(8,128)S(1)}, u32[]{:S(2)}, u32[]{:S(2)}) collective-permute-start(f32[24,512]{1,0:T(8,128)S(1)} %slice_add_fusion.7), channel_id=1, source_target_pairs={{0,8},{4,12},{8,0},{12,4},{1,9},{5,13},{9,1},{13,5},{2,10},{6,14},... | collective-permute-start | bytes 147464 | tf_op jit(solution)/shard_map/ppermute | solution.py:450
  35.0 4.6 %collective-permute-start.7 = (f32[128,512]{1,0:T(8,128)S(1)}, f32[128,512]{1,0:T(8,128)S(1)}, u32[]{:S(2)}, u32[]{:S(2)}) collective-permute-start(f32[128,512]{1,0:T(8,128)S(1)} %get-tuple-element.68), channel_id=1, source_target_pairs={{0,4},{4,0},{8,12},{12,8},{1,5},{5,1},{9,13},{13,9},{2,6},{6,2},{1... | collective-permute-start | bytes 786440 | tf_op jit(solution)/shard_map/ppermute | solution.py:434
  37.4 10.7 %collective-permute-start.17 = (f32[152,1024]{1,0:T(8,128)S(1)}, f32[152,1024]{1,0:T(8,128)S(1)}, u32[]{:S(2)}, u32[]{:S(2)}) collective-permute-start(f32[152,1024]{1,0:T(8,128)S(1)} %get-tuple-element.80), channel_id=1, source_target_pairs={{0,4},{4,0},{8,12},{12,8},{1,5},{5,1},{9,13},{13,9},{2,6},{6,2},{1... | collective-permute-start | bytes 1867784 | tf_op jit(solution)/shard_map/ppermute | solution.py:433
  37.4 2.1 %collective-permute-start.2 = (f32[24,128]{1,0:T(8,128)S(1)}, f32[24,128]{1,0:T(8,128)S(1)}, u32[]{:S(2)}, u32[]{:S(2)}) collective-permute-start(f32[24,128]{1,0:T(8,128)S(1)} %slice_add_fusion.8.refs_1_), channel_id=1, source_target_pairs={{0,4},{4,0},{8,12},{12,8},{1,5},{5,1},{9,13},{13,9},{2,6},{6,2},{1... | collective-permute-start | bytes 36872 | tf_op jit(solution)/shard_map/ppermute | solution.py:456
  39.4 11.6 %collective-permute-start.13 = (f32[152,1024]{1,0:T(8,128)S(1)}, f32[152,1024]{1,0:T(8,128)S(1)}, u32[]{:S(2)}, u32[]{:S(2)}) collective-permute-start(f32[152,1024]{1,0:T(8,128)S(1)} %get-tuple-element.76), channel_id=1, source_target_pairs={{0,4},{4,0},{8,12},{12,8},{1,5},{5,1},{9,13},{13,9},{2,6},{6,2},{1... | collective-permute-start | bytes 1867784 | tf_op jit(solution)/shard_map/ppermute | solution.py:433
  39.6 11.7 %collective-permute-start.30 = (f32[152,512]{1,0:T(8,128)S(1)}, f32[152,512]{1,0:T(8,128)S(1)}, u32[]{:S(2)}, u32[]{:S(2)}) collective-permute-start(f32[152,512]{1,0:T(8,128)S(1)} %add.67), channel_id=1, source_target_pairs={{0,8},{4,12},{8,0},{12,4},{1,9},{5,13},{9,1},{13,5},{2,10},{6,14},... | collective-permute-start | bytes 933896 | tf_op jit(solution)/shard_map/ppermute | solution.py:450
  41.3 6.6 %collective-permute-start.6 = (f32[24,512]{1,0:T(8,128)S(1)}, f32[24,512]{1,0:T(8,128)S(1)}, u32[]{:S(2)}, u32[]{:S(2)}) collective-permute-start(f32[24,512]{1,0:T(8,128)S(1)} %add.55.refs_3_), channel_id=1, source_target_pairs={{0,4},{4,0},{8,12},{12,8},{1,5},{5,1},{9,13},{13,9},{2,6},{6,2},{1... | collective-permute-start | bytes 147464 | tf_op jit(solution)/shard_map/ppermute | solution.py:456
  41.4 28.4 %collective-permute-start.22 = (f32[152,1024]{1,0:T(8,128)S(1)}, f32[152,1024]{1,0:T(8,128)S(1)}, u32[]{:S(2)}, u32[]{:S(2)}) collective-permute-start(f32[152,1024]{1,0:T(8,128)S(1)} %add.63), channel_id=1, source_target_pairs={{0,8},{4,12},{8,0},{12,4},{1,9},{5,13},{9,1},{13,5},{2,10},{6,14},... | collective-permute-start | bytes 1867784 | tf_op jit(solution)/shard_map/ppermute | solution.py:450
  47.9 3.9 %collective-permute-start.32 = (f32[128,512]{1,0:T(8,128)S(1)}, f32[128,512]{1,0:T(8,128)S(1)}, u32[]{:S(2)}, u32[]{:S(2)}) collective-permute-start(f32[128,512]{1,0:T(8,128)S(1)} %get-tuple-element.94), channel_id=1, source_target_pairs={{0,4},{4,0},{8,12},{12,8},{1,5},{5,1},{9,13},{13,9},{2,6},{6,2},{1... | collective-permute-start | bytes 786440 | tf_op jit(solution)/shard_map/ppermute | solution.py:434
  48.0 21.8 %collective-permute-start.26 = (f32[152,512]{1,0:T(8,128)S(1)}, f32[152,512]{1,0:T(8,128)S(1)}, u32[]{:S(2)}, u32[]{:S(2)}) collective-permute-start(f32[152,512]{1,0:T(8,128)S(1)} %add.65), channel_id=1, source_target_pairs={{0,8},{4,12},{8,0},{12,4},{1,9},{5,13},{9,1},{13,5},{2,10},{6,14},... | collective-permute-start | bytes 933896 | tf_op jit(solution)/shard_map/ppermute | solution.py:450
  51.1 20.5 %collective-permute-start.28 = (f32[128,512]{1,0:T(8,128)S(1)}, f32[128,512]{1,0:T(8,128)S(1)}, u32[]{:S(2)}, u32[]{:S(2)}) collective-permute-start(f32[128,512]{1,0:T(8,128)S(1)} %get-tuple-element.90), channel_id=1, source_target_pairs={{0,4},{4,0},{8,12},{12,8},{1,5},{5,1},{9,13},{13,9},{2,6},{6,2},{1... | collective-permute-start | bytes 786440 | tf_op jit(solution)/shard_map/ppermute | solution.py:434
  51.3 31.8 %collective-permute-start.18 = (f32[152,1024]{1,0:T(8,128)S(1)}, f32[152,1024]{1,0:T(8,128)S(1)}, u32[]{:S(2)}, u32[]{:S(2)}) collective-permute-start(f32[152,1024]{1,0:T(8,128)S(1)} %add.61), channel_id=1, source_target_pairs={{0,8},{4,12},{8,0},{12,4},{1,9},{5,13},{9,1},{13,5},{2,10},{6,14},... | collective-permute-start | bytes 1867784 | tf_op jit(solution)/shard_map/ppermute | solution.py:450
  51.8 33.2 %collective-permute-start.24 = (f32[128,1024]{1,0:T(8,128)S(1)}, f32[128,1024]{1,0:T(8,128)S(1)}, u32[]{:S(2)}, u32[]{:S(2)}) collective-permute-start(f32[128,1024]{1,0:T(8,128)S(1)} %get-tuple-element.86), channel_id=1, source_target_pairs={{0,4},{4,0},{8,12},{12,8},{1,5},{5,1},{9,13},{13,9},{2,6},{6,2},{1... | collective-permute-start | bytes 1572872 | tf_op jit(solution)/shard_map/ppermute | solution.py:434
  69.8 15.2 %collective-permute-start.20 = (f32[128,1024]{1,0:T(8,128)S(1)}, f32[128,1024]{1,0:T(8,128)S(1)}, u32[]{:S(2)}, u32[]{:S(2)}) collective-permute-start(f32[128,1024]{1,0:T(8,128)S(1)} %get-tuple-element.82), channel_id=1, source_target_pairs={{0,4},{4,0},{8,12},{12,8},{1,5},{5,1},{9,13},{13,9},{2,6},{6,2},{1... | collective-permute-start | bytes 1572872 | tf_op jit(solution)/shard_map/ppermute | solution.py:434
  69.8 26.7 %collective-permute-start.14 = (f32[152,1024]{1,0:T(8,128)S(1)}, f32[152,1024]{1,0:T(8,128)S(1)}, u32[]{:S(2)}, u32[]{:S(2)}) collective-permute-start(f32[152,1024]{1,0:T(8,128)S(1)} %add.59), channel_id=1, source_target_pairs={{0,8},{4,12},{8,0},{12,4},{1,9},{5,13},{9,1},{13,5},{2,10},{6,14},... | collective-permute-start | bytes 1867784 | tf_op jit(solution)/shard_map/ppermute | solution.py:450
  71.6 42.9 %collective-permute-start.16 = (f32[128,1024]{1,0:T(8,128)S(1)}, f32[128,1024]{1,0:T(8,128)S(1)}, u32[]{:S(2)}, u32[]{:S(2)}) collective-permute-start(f32[128,1024]{1,0:T(8,128)S(1)} %get-tuple-element.78), channel_id=1, source_target_pairs={{0,4},{4,0},{8,12},{12,8},{1,5},{5,1},{9,13},{13,9},{2,6},{6,2},{1... | collective-permute-start | bytes 1572872 | tf_op jit(solution)/shard_map/ppermute | solution.py:434
  83.2 19.4 %collective-permute-start.10 = (f32[152,512]{1,0:T(8,128)S(1)}, f32[152,512]{1,0:T(8,128)S(1)}, u32[]{:S(2)}, u32[]{:S(2)}) collective-permute-start(f32[152,512]{1,0:T(8,128)S(1)} %add.57), channel_id=1, source_target_pairs={{0,8},{4,12},{8,0},{12,4},{1,9},{5,13},{9,1},{13,5},{2,10},{6,14},... | collective-permute-start | bytes 933896 | tf_op jit(solution)/shard_map/ppermute | solution.py:450
  84.9 17.7 %collective-permute-start.31 = (f32[24,512]{1,0:T(8,128)S(1)}, f32[24,512]{1,0:T(8,128)S(1)}, u32[]{:S(2)}, u32[]{:S(2)}) collective-permute-start(f32[24,512]{1,0:T(8,128)S(1)} %slice_add_fusion.4.refs_4_), channel_id=1, source_target_pairs={{0,4},{4,0},{8,12},{12,8},{1,5},{5,1},{9,13},{13,9},{2,6},{6,2},{1... | collective-permute-start | bytes 147464 | tf_op jit(solution)/shard_map/ppermute | solution.py:456
  85.0 19.3 %collective-permute-start.27 = (f32[24,512]{1,0:T(8,128)S(1)}, f32[24,512]{1,0:T(8,128)S(1)}, u32[]{:S(2)}, u32[]{:S(2)}) collective-permute-start(f32[24,512]{1,0:T(8,128)S(1)} %slice_add_fusion.5.refs_4_), channel_id=1, source_target_pairs={{0,4},{4,0},{8,12},{12,8},{1,5},{5,1},{9,13},{13,9},{2,6},{6,2},{1... | collective-permute-start | bytes 147464 | tf_op jit(solution)/shard_map/ppermute | solution.py:456
  96.5 8.1 %collective-permute-start.23 = (f32[24,1024]{1,0:T(8,128)S(1)}, f32[24,1024]{1,0:T(8,128)S(1)}, u32[]{:S(2)}, u32[]{:S(2)}) collective-permute-start(f32[24,1024]{1,0:T(8,128)S(1)} %slice_add_fusion.1.refs_4_), channel_id=1, source_target_pairs={{0,4},{4,0},{8,12},{12,8},{1,5},{5,1},{9,13},{13,9},{2,6},{6,2},{1... | collective-permute-start | bytes 294920 | tf_op jit(solution)/shard_map/ppermute | solution.py:456
  102.6 14.5 %collective-permute-start.12 = (f32[128,512]{1,0:T(8,128)S(1)}, f32[128,512]{1,0:T(8,128)S(1)}, u32[]{:S(2)}, u32[]{:S(2)}) collective-permute-start(f32[128,512]{1,0:T(8,128)S(1)} %get-tuple-element.74), channel_id=1, source_target_pairs={{0,4},{4,0},{8,12},{12,8},{1,5},{5,1},{9,13},{13,9},{2,6},{6,2},{1... | collective-permute-start | bytes 786440 | tf_op jit(solution)/shard_map/ppermute | solution.py:434
  102.6 16.3 %collective-permute-start.8 = (f32[128,512]{1,0:T(8,128)S(1)}, f32[128,512]{1,0:T(8,128)S(1)}, u32[]{:S(2)}, u32[]{:S(2)}) collective-permute-start(f32[128,512]{1,0:T(8,128)S(1)} %slice_add_fusion), channel_id=1, source_target_pairs={{0,8},{4,12},{8,0},{12,4},{1,9},{5,13},{9,1},{13,5},{2,10},{6,14},... | collective-permute-start | bytes 786440 | tf_op jit(solution)/shard_map/ppermute | solution.py:450
  104.3 1.3 %collective-permute-start.19 = (f32[24,1024]{1,0:T(8,128)S(1)}, f32[24,1024]{1,0:T(8,128)S(1)}, u32[]{:S(2)}, u32[]{:S(2)}) collective-permute-start(f32[24,1024]{1,0:T(8,128)S(1)} %slice_add_fusion.2.refs_4_), channel_id=1, source_target_pairs={{0,4},{4,0},{8,12},{12,8},{1,5},{5,1},{9,13},{13,9},{2,6},{6,2},{1... | collective-permute-start | bytes 294920 | tf_op jit(solution)/shard_map/ppermute | solution.py:456
  104.6 10.0 %collective-permute-start.15 = (f32[24,1024]{1,0:T(8,128)S(1)}, f32[24,1024]{1,0:T(8,128)S(1)}, u32[]{:S(2)}, u32[]{:S(2)}) collective-permute-start(f32[24,1024]{1,0:T(8,128)S(1)} %slice_add_fusion.3.refs_4_), channel_id=1, source_target_pairs={{0,4},{4,0},{8,12},{12,8},{1,5},{5,1},{9,13},{13,9},{2,6},{6,2},{1... | collective-permute-start | bytes 294920 | tf_op jit(solution)/shard_map/ppermute | solution.py:456
  105.6 11.4 %collective-permute-start.11 = (f32[24,512]{1,0:T(8,128)S(1)}, f32[24,512]{1,0:T(8,128)S(1)}, u32[]{:S(2)}, u32[]{:S(2)}) collective-permute-start(f32[24,512]{1,0:T(8,128)S(1)} %slice_add_fusion.6.refs_4_), channel_id=1, source_target_pairs={{0,4},{4,0},{8,12},{12,8},{1,5},{5,1},{9,13},{13,9},{2,6},{6,2},{1... | collective-permute-start | bytes 147464 | tf_op jit(solution)/shard_map/ppermute | solution.py:456

commit v4 on v3

--- a/solution.py
+++ b/solution.py
@@ -18,7 +18,7 @@
 OPEN_LIMIT = 20 * 2**20
 LIMIT = 12 * 2**20
 PIECES = 4
-GROUPS = 4
+EARLY = 2
 LAST = (((1,), (1,)), ((), ()))
 
 
@@ -48,11 +48,10 @@
     return ref.at[:, start : start + width]
 
 
-def multiply(left_ref, pheno_ref, copies, outs, small, core, rows, half):
-    give_far, give_near, keep_far, keep_near = outs
+def multiply_far(left_ref, pheno_ref, copies, give_far, keep_far, small, core, half):
     width = give_far.shape[1]
     far = give_far.shape[0] - half
-    split = far + rows
+    size = 2 * half
     step = min(STRIP, width) if copies else min(TILE, width)
     for low in range(0, width, step):
         high = low + step
@@ -61,18 +60,24 @@
         pheno = pheno_ref[:, low:high]
         result = jnp.dot(left_ref[...], pheno, preferred_element_type=F32)
         give_far[0:far, low:high] = result[:far]
-        give_near[:, low:high] = result[far:split]
-        keep_far[0:far, low:high] = result[split : split + far]
-        keep_near[:, low:high] = result[split + far : 2 * split]
-        upper = result[2 * split : 2 * split + 2 * half]
-        middle = result[2 * split + 2 * half : 2 * split + 4 * half]
-        lower = result[2 * split + 4 * half :]
+        keep_far[0:far, low:high] = result[far : 2 * far]
+        design = result[2 * far :]
         wide = pheno.astype(F32)
         square = jnp.sum(wide * wide, axis=0, keepdims=True)
-        place = lax.broadcasted_iota(jnp.int32, upper.shape, 0)
-        small[:, low:high] = jnp.where(place == SQUARE, square, (lower + middle) + upper)
+        place = lax.broadcasted_iota(jnp.int32, (size, step), 0)
+        total = (design[2 * size :] + design[size : 2 * size]) + design[:size]
+        small[:, low:high] = jnp.where(place == SQUARE, square, total)
     give_far[far:, :] = small[pl.ds(pl.multiple_of((1 - core) * half, half), half), :]
     keep_far[far:, :] = small[pl.ds(pl.multiple_of(core * half, half), half), :]
+
+
+def multiply_near(left_ref, pheno_ref, give_near, keep_near):
+    rows, width = give_near.shape
+    step = min(TILE, width)
+    for low in range(0, width, step):
+        result = jnp.dot(left_ref[...], pheno_ref[:, low : low + step], preferred_element_type=F32)
+        give_near[:, low : low + step] = result[:rows]
+        keep_near[:, low : low + step] = result[rows:]
 
 
 def part_shapes(chips, rows, half, width):
@@ -83,93 +88,139 @@
 
 def design_kernel(chips, rows, half, place_ref, left_ref, geno_ref, *refs):
     outs, (small, table) = refs[:4], refs[4:]
-    give_far, _, keep_far, _ = outs
+    give_far, give_near, keep_far, _ = outs
     chip, core = place_ref[0], place_ref[1]
-    far = give_far.shape[0] - half
     snps = geno_ref.shape[1]
     size = 2 * half
-    design = left_ref[snps:, :]
+    far = (chips - 1) * size
+    design = left_ref[2 * (chips - 1) * rows :, :]
     product = jnp.dot(design, geno_ref[...], preferred_element_type=F32)
     product = (product[2 * size :] + product[size : 2 * size]) + product[:size]
     wide = geno_ref[...].astype(F32)
     square = jnp.sum(wide * wide, axis=0, keepdims=True)
     row = lax.broadcasted_iota(jnp.int32, (size, snps), 0)
     product = jnp.where(row == SQUARE, square, product)
-    product = jnp.concatenate([product, jnp.zeros((LANES - size, snps), F32)], axis=0)
-    table[...] = product.T
+    direct = rows % LANES == 0
+    if direct:
+        table[...] = product
+    else:
+        table[...] = jnp.concatenate([product, jnp.zeros((LANES - size, snps), F32)], axis=0).T
+    lanes = give_near.shape[1]
     for slot in range(chips):
         target = lax.rem(chip + slot + 1, chips) * (2 * rows)
         for side, own in ((0, 1 - core), (1, core)):
             start = pl.multiple_of(target + own * rows, rows)
+            if direct:
+                block = table[:, pl.ds(start, rows)]
+            else:
+                block = table[pl.ds(start, rows), :].T[:size]
+                block = jnp.concatenate([block, jnp.zeros((size, lanes - rows), F32)], axis=1)
             if slot < chips - 1:
-                outs[2 * side][slot * rows : (slot + 1) * rows, :] = table[pl.ds(start, rows), :]
+                outs[2 * side][slot * size : (slot + 1) * size, :] = block
             else:
-                outs[2 * side + 1][...] = table[pl.ds(start, rows), :]
+                outs[2 * side + 1][...] = block
     gram = lax.dot_general(design, design, LAST, preferred_element_type=F32)
     total = jnp.zeros((size, size), F32)
     for tall, flat in ((2, 0), (0, 2), (1, 1), (1, 0), (0, 1), (0, 0)):
         total = total + gram[tall * size : (tall + 1) * size, flat * size : (flat + 1) * size]
-    small[...] = jnp.concatenate([total, jnp.zeros((size, LANES - size), F32)], axis=1)
+    small[...] = jnp.concatenate([total, jnp.zeros((size, lanes - size), F32)], axis=1)
     give_far[far:, :] = small[pl.ds(pl.multiple_of((1 - core) * half, half), half), :]
     keep_far[far:, :] = small[pl.ds(pl.multiple_of(core * half, half), half), :]
 
 
 def with_design(place, left, geno, chips, rows, half):
     subjects, snps = geno.shape
+    lanes = round_up(rows, LANES)
     return pl.pallas_call(
         functools.partial(design_kernel, chips, rows, half),
-        out_shape=part_shapes(chips, rows, half, LANES),
+        out_shape=part_shapes(chips, 2 * half, half, lanes),
         in_specs=[SMEM, VMEM, VMEM],
         out_specs=(VMEM,) * 4,
-        scratch_shapes=[pltpu.VMEM((2 * half, LANES), F32), pltpu.VMEM((snps, LANES), F32)],
+        scratch_shapes=[
+            pltpu.VMEM((2 * half, lanes), F32),
+            pltpu.VMEM((2 * half, snps) if rows % LANES == 0 else (snps, LANES), F32),
+        ],
         compiler_params=pltpu.CompilerParams(vmem_limit_bytes=LIMIT),
         cost_estimate=cost(2 * 6 * half * subjects * snps, 2 * subjects * snps),
         name="with_design",
     )(place, left, geno)
 
 
-def open_kernel(chips, rows, half, widths, place_ref, geno_ref, cov_ref, pheno_ref, *refs):
-    left_ref, geno, outs = refs[0], refs[1], refs[2:6]
-    ahead_refs = refs[6:-5]
-    turned, design, first, small, sems = refs[-5:]
+def open_kernel(chips, rows, half, place_ref, geno_ref, cov_ref, pheno_ref, *refs):
+    left_ref, geno, give_far, keep_far = refs[:4]
+    heres, (turned, design, small, sems) = refs[4:-4], refs[-4:]
     chip, core = place_ref[0], place_ref[1]
     covs, subjects = cov_ref.shape
-    snps = 2 * chips * rows
+    far = (chips - 1) * rows
+    size = 2 * half
     cov_copy = pltpu.make_async_copy(cov_ref, design.at[8 : 8 + covs], sems.at[0])
     cov_copy.start()
     geno_copies = block_copies(geno_ref, geno, sems, 1, 0)
-    first_copies = block_copies(column_block(pheno_ref, 0, widths[0]), first, sems, 1 + PIECES, 1)
-    used = 1 + PIECES + len(first_copies)
-    ahead_copies = []
-    start = widths[0]
-    for index, ahead_ref in enumerate(ahead_refs):
-        block = column_block(pheno_ref, start, ahead_ref.shape[1])
-        ahead_copies += block_copies(block, ahead_ref, sems, used + index * PIECES, 0)
-        start += ahead_ref.shape[1]
+    first = heres[0]
+    first_copies = block_copies(column_block(pheno_ref, 0, first.shape[1]), first, sems, 1 + PIECES, 1)
     for copy in geno_copies + first_copies:
         copy.start()
+    used, start = 1 + PIECES + len(first_copies), first.shape[1]
+    later_copies = []
+    for here in heres[1:]:
+        later_copies += block_copies(column_block(pheno_ref, start, here.shape[1]), here, sems, used, 0)
+        used, start = used + PIECES, start + here.shape[1]
     top = lax.broadcasted_iota(jnp.int32, (8, subjects), 0)
     design[0:8, :] = jnp.where(top == 0, 1.0, 0.0)
-    if 2 * half > 8 + covs:
-        design[8 + covs :, :] = jnp.zeros((2 * half - 8 - covs, subjects), F32)
+    if size > 8 + covs:
+        design[8 + covs :, :] = jnp.zeros((size - 8 - covs, subjects), F32)
     cov_copy.wait()
     for index, part in enumerate(split_three(design[...])):
-        left_ref[snps + index * 2 * half : snps + (index + 1) * 2 * half, :] = part
-    step = subjects // GROUPS
-    for index in range(GROUPS):
-        for copy in geno_copies[index * PIECES // GROUPS : (index + 1) * PIECES // GROUPS]:
-            copy.wait()
-        turned[:, index * step : (index + 1) * step] = geno[index * step : (index + 1) * step, :].T
-    for copy in ahead_copies:
+        left_ref[2 * far + index * size : 2 * far + (index + 1) * size, :] = part
+    step = subjects // PIECES
+    direct = 2 * rows % LANES == 0
+    for index, copy in enumerate(geno_copies):
+        copy.wait()
+        low, high = index * step, (index + 1) * step
+        if direct:
+            for slot in range(chips - 1):
+                target = pl.multiple_of(lax.rem(chip + slot + 1, chips) * (2 * rows), 2 * rows)
+                base = slot * 2 * rows
+                turned[base : base + 2 * rows, low:high] = geno[low:high, pl.ds(target, 2 * rows)].T
+        else:
+            turned[:, low:high] = geno[low:high, :].T
+    for copy in later_copies:
         copy.start()
-    for slot in range(chips):
-        target = lax.rem(chip + slot + 1, chips) * (2 * rows)
+    for slot in range(chips - 1):
+        target = slot * 2 * rows if direct else lax.rem(chip + slot + 1, chips) * (2 * rows)
         for side, own in ((0, 1 - core), (1, core)):
-            low = (side * chips + slot) * rows
-            start = pl.multiple_of(target + own * rows, rows)
-            left_ref[low : low + rows, :] = turned[pl.ds(start, rows), :]
-    multiply(left_ref, first, first_copies, outs, small, core, rows, half)
-    for copy in ahead_copies:
+            low = side * far + slot * rows
+            left_ref[low : low + rows, :] = turned[pl.ds(pl.multiple_of(target + own * rows, rows), rows), :]
+    multiply_far(left_ref, first, first_copies, give_far, keep_far, small, core, half)
+    for copy in later_copies:
+        copy.wait()
+
+
+def near_kernel(rows, start, early, place_ref, geno_ref, pheno_ref, *refs):
+    heres, left_ref, outs = refs[:early], refs[early], refs[early + 1 : 3 * early + 1]
+    later, (turned, sems) = refs[3 * early + 1 : -2], refs[-2:]
+    chip, core = place_ref[0], place_ref[1]
+    copies = []
+    for target in later:
+        copies += block_copies(column_block(pheno_ref, start, target.shape[1]), target, sems, 0, 0)
+    for copy in copies:
+        copy.start()
+
+    @pl.when(core >= 0)
+    def _():
+        if 2 * rows % LANES == 0:
+            turned[0 : 2 * rows, :] = geno_ref[:, pl.ds(pl.multiple_of(chip * (2 * rows), 2 * rows), 2 * rows)].T
+            base = 0
+        else:
+            turned[...] = geno_ref[...].T
+            base = chip * (2 * rows)
+        for side, own in ((0, 1 - core), (1, core)):
+            low = pl.multiple_of(base + own * rows, rows)
+            left_ref[side * rows : (side + 1) * rows, :] = turned[pl.ds(low, rows), :]
+        for index, here in enumerate(heres):
+            multiply_near(left_ref, here, outs[2 * index], outs[2 * index + 1])
+
+    for copy in copies:
         copy.wait()
 
 
@@ -187,24 +238,23 @@
 
 
 def open_up(place, dosage, cov_rows, phenotype, chips, rows, half, widths):
+    subjects, snps = dosage.shape
     width = widths[0]
-    subjects, snps = dosage.shape
-    height = snps + 6 * half
+    height = 2 * (chips - 1) * rows + 6 * half
     left = jax.ShapeDtypeStruct((height, subjects), BF16)
-    ahead = [jax.ShapeDtypeStruct((subjects, later), BF16) for later in widths[1:2]]
     geno = jax.ShapeDtypeStruct((subjects, snps), BF16)
-    parts = part_shapes(chips, rows, half, width)
-    return pl.pallas_call(
-        functools.partial(open_kernel, chips, rows, half, widths),
-        out_shape=(left, geno, *parts, *ahead),
+    heres = [jax.ShapeDtypeStruct((subjects, size), BF16) for size in widths]
+    part = part_shapes(chips, rows, half, width)[0]
+    return pl.pallas_call(
+        functools.partial(open_kernel, chips, rows, half),
+        out_shape=(left, geno, part, part, *heres),
         in_specs=[SMEM, HBM, HBM, HBM],
-        out_specs=(VMEM,) * (6 + len(ahead)),
+        out_specs=(VMEM,) * (4 + len(heres)),
         scratch_shapes=[
             pltpu.VMEM((snps, subjects), BF16),
             pltpu.VMEM((2 * half, subjects), F32),
-            pltpu.VMEM((subjects, width), BF16),
             pltpu.VMEM((2 * half, width), F32),
-            pltpu.SemaphoreType.DMA((1 + 2 * PIECES + max(width // STRIP, 1),)),
+            pltpu.SemaphoreType.DMA((1 + len(heres) * PIECES + max(width // STRIP, 1),)),
         ],
         compiler_params=pltpu.CompilerParams(vmem_limit_bytes=OPEN_LIMIT),
         cost_estimate=cost(2 * height * subjects * width, 4 * snps * subjects),
@@ -212,8 +262,46 @@
     )(place, in_hbm(dosage), in_hbm(cov_rows), in_hbm(phenotype))
 
 
-def product_kernel(rows, half, start, place_ref, left_ref, here_ref, pheno_ref, *refs):
-    outs, later, (small, sems) = refs[:4], refs[4:-2], refs[-2:]
+def open_near(place, geno, heres, phenotype, later, rows):
+    subjects, snps = geno.shape
+    widths = [here.shape[1] for here in heres]
+    parts = [jax.ShapeDtypeStruct((rows, width), F32) for width in widths for _ in range(2)]
+    left = jax.ShapeDtypeStruct((2 * rows, subjects), BF16)
+    ahead = [jax.ShapeDtypeStruct((subjects, size), BF16) for size in later]
+    return pl.pallas_call(
+        functools.partial(near_kernel, rows, sum(widths), len(heres)),
+        out_shape=(left, *parts, *ahead),
+        in_specs=[SMEM, VMEM, HBM] + [VMEM] * len(heres),
+        out_specs=(VMEM,) * (1 + len(parts) + len(ahead)),
+        scratch_shapes=[pltpu.VMEM((snps, subjects), BF16), pltpu.SemaphoreType.DMA((PIECES,))],
+        compiler_params=pltpu.CompilerParams(vmem_limit_bytes=LIMIT),
+        cost_estimate=cost(4 * rows * subjects * sum(widths), 4 * snps * subjects),
+        name="open_near",
+    )(place, geno, in_hbm(phenotype), *heres)
+
+
+def far_kernel(half, place_ref, far_ref, here_ref, give_far, keep_far, small):
+    multiply_far(far_ref, here_ref, [], give_far, keep_far, small, place_ref[1], half)
+
+
+def far_product(place, left, here, chips, rows, half):
+    height, subjects = left.shape
+    width = here.shape[1]
+    part = part_shapes(chips, rows, half, width)[0]
+    return pl.pallas_call(
+        functools.partial(far_kernel, half),
+        out_shape=(part, part),
+        in_specs=[SMEM, VMEM, VMEM],
+        out_specs=(VMEM, VMEM),
+        scratch_shapes=[pltpu.VMEM((2 * half, width), F32)],
+        compiler_params=pltpu.CompilerParams(vmem_limit_bytes=LIMIT),
+        cost_estimate=cost(2 * height * subjects * width, 2 * subjects * width),
+    )(place, left, here)
+
+
+def product_kernel(half, start, place_ref, far_ref, near_ref, here_ref, pheno_ref, *refs):
+    give_far, give_near, keep_far, keep_near = refs[:4]
+    later, (small, sems) = refs[4:-2], refs[-2:]
     core = place_ref[1]
     copies = []
     for target in later:
@@ -223,25 +311,26 @@
 
     @pl.when(core >= 0)
     def _():
-        multiply(left_ref, here_ref, [], outs, small, core, rows, half)
+        multiply_far(far_ref, here_ref, [], give_far, keep_far, small, core, half)
+        multiply_near(near_ref, here_ref, give_near, keep_near)
 
     for copy in copies:
         copy.wait()
 
 
-def product(place, left, here, phenotype, start, later, chips, rows, half):
+def product(place, left, near, here, phenotype, start, later, chips, rows, half):
     height, subjects = left.shape
     width = here.shape[1]
     ahead = [jax.ShapeDtypeStruct((subjects, size), BF16) for size in later]
     return pl.pallas_call(
-        functools.partial(product_kernel, rows, half, start + width),
+        functools.partial(product_kernel, half, start + width),
         out_shape=(*part_shapes(chips, rows, half, width), *ahead),
-        in_specs=[SMEM, VMEM, VMEM, HBM],
+        in_specs=[SMEM, VMEM, VMEM, VMEM, HBM],
         out_specs=(VMEM,) * (4 + len(ahead)),
         scratch_shapes=[pltpu.VMEM((2 * half, width), F32), pltpu.SemaphoreType.DMA((PIECES,))],
         compiler_params=pltpu.CompilerParams(vmem_limit_bytes=LIMIT),
-        cost_estimate=cost(2 * height * subjects * width, 2 * subjects * width),
-    )(place, left, here, in_hbm(phenotype))
+        cost_estimate=cost(2 * (height + 2 * rows) * subjects * width, 2 * subjects * width),
+    )(place, left, near, here, in_hbm(phenotype))
 
 
 def solve_kernel(live, half, count, *refs):
@@ -269,17 +358,17 @@
     own = terms[0][...]
     for term in terms[1:]:
         own = own + term[...]
-    wide = jnp.concatenate([scaled, jnp.zeros((LANES - size, LANES), F32)], axis=0)
-    white = lax.dot_general(own, wide, LAST, precision=HI, preferred_element_type=F32)
-    white_ref[...] = white
-    var_ref[...] = jnp.broadcast_to(
-        own[:, SQUARE : SQUARE + 1] - jnp.sum(white * white, axis=1, keepdims=True), var_ref.shape
-    )
-
-
-def solve(place, half_rows, rest_rows, terms, live):
+    rows = white_ref.shape[0]
+    white = jnp.dot(scaled[:, :size], own, precision=HI, preferred_element_type=F32)
+    geno_var = own[SQUARE : SQUARE + 1] - jnp.sum(white * white, axis=0, keepdims=True)
+    white = jnp.concatenate([white, jnp.zeros((LANES - size, own.shape[1]), F32)], axis=0)
+    white_ref[...] = white.T[:rows]
+    var_ref[...] = jnp.broadcast_to(geno_var, (LANES, own.shape[1])).T[:rows]
+
+
+def solve(place, half_rows, rest_rows, terms, live, rows):
     half = half_rows.shape[0]
-    wide = jax.ShapeDtypeStruct(terms[0].shape, F32)
+    wide = jax.ShapeDtypeStruct((rows, LANES), F32)
     return pl.pallas_call(
         functools.partial(solve_kernel, live, half, len(terms)),
         out_shape=(jax.ShapeDtypeStruct((2 * half, LANES), F32), wide, wide),
@@ -423,24 +512,28 @@
     rows = snps // devices
     half = round_up(8 + covs, 16) // 2
     live = [0] + list(range(8, 8 + covs))
-    far = (chips - 1) * rows
     place_index = lax.axis_index("subj")
     place = jnp.stack([place_index // 2, lax.rem(place_index, 2)]).astype(jnp.int32)
     sibling = [(i, i ^ 1) for i in range(devices)]
 
-    def near_sums(parts, apart=False):
+    def far_got(give_far):
+        return lax.ppermute(give_far, "subj", sibling)
+
+    def near_sums(parts, apart=False, got_far=None, unit=rows):
+        far = (chips - 1) * unit
         give_far, give_near, keep_far, keep_near = parts
-        got_far = lax.ppermute(give_far, "subj", sibling)
+        if got_far is None:
+            got_far = far_got(give_far)
         got_near = lax.ppermute(give_near, "subj", sibling)
         terms = [keep_near, got_near]
         if apart:
-            blocks = [keep_far[low : low + rows] + got_far[low : low + rows] for low in range(0, far, rows)]
+            blocks = [keep_far[low : low + unit] + got_far[low : low + unit] for low in range(0, far, unit)]
             return terms, blocks, keep_far[far:] + got_far[far:]
         summed = keep_far + got_far
         if chips == 2:
-            return terms, [summed], summed[rows:]
+            return terms, [summed], summed[unit:]
         own_half = summed[far:]
-        blocks = [jnp.concatenate([summed[low : low + rows], own_half], axis=0) for low in range(0, far, rows)]
+        blocks = [jnp.concatenate([summed[low : low + unit], own_half], axis=0) for low in range(0, far, unit)]
         return terms, blocks, own_half
 
     def far_terms(blocks):
@@ -458,27 +551,32 @@
 
     widths = chunk_widths(verts)
     last = len(widths)
-    left, geno, *parts = open_up(
-        place, dosage, covariates.T, phenotype, chips, rows, half, widths
-    )
-    ahead = parts[4:]
-    sums = [near_sums(parts[:4])]
-    came = [far_terms(sums[0][1])]
+    early = widths[:EARLY]
+    left, geno, give_far, keep_far, *heres = open_up(place, dosage, covariates.T, phenotype, chips, rows, half, early)
+    fars = [(give_far, keep_far, far_got(give_far))]
+    for index in range(1, len(early)):
+        give_far, keep_far = far_product(place, left, heres[index], chips, rows, half)
+        fars.append((give_far, keep_far, far_got(give_far)))
+    near, *nears = open_near(place, geno, heres, phenotype, widths[EARLY : EARLY + 1], rows)
+    ahead = nears[2 * len(early) :]
+    sums, came = [], []
+    for index, (give_far, keep_far, got_far) in enumerate(fars):
+        give_near, keep_near = nears[2 * index : 2 * index + 2]
+        sums.append(near_sums((give_far, give_near, keep_far, keep_near), got_far=got_far))
+        came.append(far_terms(sums[-1][1]))
     parts = with_design(place, left, geno, chips, rows, half)
-    terms, blocks, own_half = near_sums(parts)
+    terms, blocks, own_half = near_sums(parts, unit=2 * half)
     base_came = far_terms(blocks)
-    halves, rest = gather_half(own_half, [block[rows:] for block in base_came])
+    halves, rest = gather_half(own_half, [block[2 * half :] for block in base_came])
     inverse, white, geno_var = solve(
-        place, halves, rest, terms + [block[:rows] for block in base_came], live
+        place, halves, rest, terms + [block[: 2 * half] for block in base_came], live, rows
     )
     dof = float(subjects * devices - covs - 2) ** 0.5
 
-    start = widths[0]
-    for index in range(1, last):
+    start = sum(early)
+    for index in range(EARLY, last):
         tag = index + 1
-        parts = product(
-            place, left, ahead[0], phenotype, start, widths[index + 1 : index + 2], chips, rows, half
-        )
+        parts = product(place, left, near, ahead[0], phenotype, start, widths[index + 1 : index + 2], chips, rows, half)
         ahead = parts[4:]
         start += widths[index]
         sums.append(near_sums(parts[:4], apart=tag == last))

time: 120 us -> 119 us (level)
  waiting for transfers between devices: 53.9 us -> 52.5 us
    pallas_call x7 -> x8, Pallas kernels: 23.7 us -> 24 us  [the longest x5 15 us: product(): pl.pallas_call(functools.partial(product_kernel, half, start + width), ou...]
  transfers between devices with their start and end apart: 33 -> 33, of which waited for: 9 -> 8; matrix products, arithmetic and copies ran while one was open for 0% -> 0% of each run, Pallas kernels for 18% -> 19%
where the time goes in v4:
time: 119 us
  waiting for transfers between devices  52.5 us (44%)
  Pallas kernels  46.2 us (39%)
  starting transfers between devices  19.5 us (16%)
    ppermute x9, waiting for transfers between devices, far_terms(): came.append(lax.ppermute(block, 'subj', moves))  50.2 us
    pallas_call x5, Pallas kernels, product(): pl.pallas_call(functools.partial(product_kernel, half, start + width), ou...  15 us
    ppermute x9, starting transfers between devices, far_terms(): came.append(lax.ppermute(block, 'subj', moves))  14.4 us
    pallas_call x6, Pallas kernels, finish(): pl.pallas_call(functools.partial(finish_kernel, dof, len(terms)), grid=(w...  13 us
    pallas_call x1, Pallas kernels, solve(): pl.pallas_call(functools.partial(solve_kernel, live, half, len(terms)), o...  5.97 us
    pallas_call x1, Pallas kernels, open_up(): pl.pallas_call(functools.partial(open_kernel, chips, rows, half), out_sha...  4.6 us
    pallas_call x1, Pallas kernels, open_near(): pl.pallas_call(functools.partial(near_kernel, rows, sum(widths), len(here...  2.76 us
  transfers between devices with their start and end apart: 33, of which 8 were waited for; matrix products, arithmetic and copies ran while one was open for 0% of the time, Pallas kernels for 19%

profile of v4, /device:TPU:0, one launch (start us, length us, event | category | flops | bytes accessed | tf_op | source)
XLA Modules:
  0.0 118.9 jit_solution(14915084413171591938)
XLA Ops:
  0.0 0.1 pad_add_fusion.place_ref.refs_0_
  0.1 4.6 %open.1 = (bf16[400,2048]{1,0:T(8,128)(2,1)S(1)}, bf16[2048,512]{1,0:T(8,128)(2,1)S(1)}, f32[152,512]{1,0:T(8,128)S(1)}, f32[152,512]{1,0:T(8,128)S(1)}, bf16[20...) custom-call(s32[2]{0:T(128)S(1)} %pad_add_fusion.place_ref.refs_0_, bf16[2048,512]{1,0:T(8,128)(2,1)} %geno_ref.1, ...), custom_call_target="tpu_custom_call" | custom-call | flops 838860800 | bytes 4194304 | tf_op jit(solution)/shard_map/open/pallas_call | solution.py:248
  4.7 2.8 %open_near.1 = (bf16[256,2048]{1,0:T(8,128)(2,1)S(1)}, f32[128,512]{1,0:T(8,128)S(1)}, f32[128,512]{1,0:T(8,128)S(1)}, f32[128,512]{1,0:T(8,128)S(1)}, f32[128,5...) custom-call(s32[2]{0:T(128)S(1)} %pad_add_fusion.place_ref.refs_0_, bf16[2048,512]{1,0:T(8,128)(2,1)S(1)} %get-tuple-element.53.geno_ref, ...), custom_call_target="tpu_custom_call" | custom-call | flops 1073741824 | bytes 4194304 | tf_op jit(solution)/shard_map/open_near/pallas_call | solution.py:271
  7.5 3.5 %shard_map.37 = (f32[152,1024]{1,0:T(8,128)S(1)}, f32[128,1024]{1,0:T(8,128)S(1)}, f32[152,1024]{1,0:T(8,128)S(1)}, f32[128,1024]{1,0:T(8,128)S(1)}, bf16[2048,1024]{1,0:T(8,128)(2,1)S(1)}) custom-call(s32[2]{0:T(128)S(1)} %pad_add_fusion.place_ref.refs_0_, bf16[400,2048]{1,0:T(8,128)(2,1)S(1)} %get-tuple-element.52.left_ref.far_ref, ...), custom_call_target="tpu_custom_call" | custom-call | flops 2751463424 | bytes 4194304 | tf_op jit(solution)/shard_map/pallas_call | solution.py:325
  11.0 3.5 %shard_map.38 = (f32[152,1024]{1,0:T(8,128)S(1)}, f32[128,1024]{1,0:T(8,128)S(1)}, f32[152,1024]{1,0:T(8,128)S(1)}, f32[128,1024]{1,0:T(8,128)S(1)}, bf16[2048,1024]{1,0:T(8,128)(2,1)S(1)}) custom-call(s32[2]{0:T(128)S(1)} %pad_add_fusion.place_ref.refs_0_, bf16[400,2048]{1,0:T(8,128)(2,1)S(1)} %get-tuple-element.52.left_ref.far_ref, ...), custom_call_target="tpu_custom_call" | custom-call | flops 2751463424 | bytes 4194304 | tf_op jit(solution)/shard_map/pallas_call | solution.py:325
  14.5 3.5 %shard_map.39 = (f32[152,1024]{1,0:T(8,128)S(1)}, f32[128,1024]{1,0:T(8,128)S(1)}, f32[152,1024]{1,0:T(8,128)S(1)}, f32[128,1024]{1,0:T(8,128)S(1)}, bf16[2048,512]{1,0:T(8,128)(2,1)S(1)}) custom-call(s32[2]{0:T(128)S(1)} %pad_add_fusion.place_ref.refs_0_, bf16[400,2048]{1,0:T(8,128)(2,1)S(1)} %get-tuple-element.52.left_ref.far_ref, ...), custom_call_target="tpu_custom_call" | custom-call | flops 2751463424 | bytes 4194304 | tf_op jit(solution)/shard_map/pallas_call | solution.py:325
  18.1 2.1 %shard_map.40 = (f32[152,512]{1,0:T(8,128)S(1)}, f32[128,512]{1,0:T(8,128)S(1)}, f32[152,512]{1,0:T(8,128)S(1)}, f32[128,512]{1,0:T(8,128)S(1)}, bf16[2048,512]{1,0:T(8,128)(2,1)S(1)}) custom-call(s32[2]{0:T(128)S(1)} %pad_add_fusion.place_ref.refs_0_, bf16[400,2048]{1,0:T(8,128)(2,1)S(1)} %get-tuple-element.52.left_ref.far_ref, ...), custom_call_target="tpu_custom_call" | custom-call | flops 1375731712 | bytes 2097152 | tf_op jit(solution)/shard_map/pallas_call | solution.py:325
  20.2 2.3 %shard_map.41 = (f32[152,512]{1,0:T(8,128)S(1)}, f32[128,512]{1,0:T(8,128)S(1)}, f32[152,512]{1,0:T(8,128)S(1)}, f32[128,512]{1,0:T(8,128)S(1)}) custom-call(s32[2]{0:T(128)S(1)} %pad_add_fusion.place_ref.refs_0_, bf16[400,2048]{1,0:T(8,128)(2,1)S(1)} %get-tuple-element.52.left_ref.far_ref, bf16[256,2048]{1,0:T(8,128)(2,1)S(1)} %get-tuple-element.63.near_ref, ...), custom_call_target="tpu_custom_call" | custom-call | flops 1375731712 | bytes 2097152 | tf_op jit(solution)/shard_map/pallas_call | solution.py:325
  22.5 0.6 collective-permute-start.4
  23.1 0.1 collective-permute-start.21
  23.2 0.4 collective-permute-start.29
  23.6 1.3 %with_design.1 = (f32[72,128]{1,0:T(8,128)S(1)}, f32[48,128]{1,0:T(8,128)S(1)}, f32[72,128]{1,0:T(8,128)S(1)}, f32[48,128]{1,0:T(8,128)S(1)}) custom-call(s32[2]{0:T(128)S(1)} %pad_add_fusion.place_ref.refs_0_, bf16[400,2048]{1,0:T(8,128)(2,1)S(1)} %get-tuple-element.52.left_ref.far_ref, bf16[2048,512]{1,0:T(8,128)(2,1)S(1)} %get-tuple-element.53.geno_ref), custom_call_target="tpu_custom_call" | custom-call | flops 301989888 | bytes 2097152 | tf_op jit(solution)/shard_map/with_design/pallas_call | solution.py:134
  24.9 0.1 collective-permute-start
  25.0 0.4 collective-permute-start.3
  25.4 1.6 %shard_map.42 = (f32[152,512]{1,0:T(8,128)S(1)}, f32[152,512]{1,0:T(8,128)S(1)}) custom-call(s32[2]{0:T(128)S(1)} %pad_add_fusion.place_ref.refs_0_, bf16[400,2048]{1,0:T(8,128)(2,1)S(1)} %get-tuple-element.52.left_ref.far_ref, bf16[2048,512]{1,0:T(8,128)(2,1)S(1)} %get-tuple-element.62.refs_1_.here_ref), custom_call_target="tpu_custom_call" | custom-call | flops 838860800 | bytes 2097152 | tf_op jit(solution)/shard_map/pallas_call | solution.py:291
  27.0 0.1 collective-permute-start.25
  27.2 0.0 collective-permute-done.3.refs_4_
  27.2 0.5 collective-permute-start.9
  27.7 0.0 collective-permute-done.4
  27.7 2.6 %collective-permute-start.1 = (f32[72,128]{1,0:T(8,128)S(1)}, f32[72,128]{1,0:T(8,128)S(1)}, u32[]{:S(2)}, u32[]{:S(2)}) collective-permute-start(f32[72,128]{1,0:T(8,128)S(1)} %add.52), channel_id=1, source_target_pairs={{0,8},{4,12},{8,0},{12,4},{1,9},{5,13},{9,1},{13,5},{2,10},{6,14},... | collective-permute-start | bytes 110600 | tf_op jit(solution)/shard_map/ppermute | solution.py:543
  30.2 2.1 %collective-permute-done.1 = f32[72,128]{1,0:T(8,128)S(1)} collective-permute-done((f32[72,128]{1,0:T(8,128)S(1)}, f32[72,128]{1,0:T(8,128)S(1)}, u32[]{:S(2)}, u32[]{:S(2)}) %collective-permute-start.1) | collective-permute-done | bytes 36896 | tf_op jit(solution)/shard_map/ppermute | solution.py:543
  32.3 1.9 %collective-permute-start.5 = (f32[24,512]{1,0:T(8,128)S(1)}, f32[24,512]{1,0:T(8,128)S(1)}, u32[]{:S(2)}, u32[]{:S(2)}) collective-permute-start(f32[24,512]{1,0:T(8,128)S(1)} %slice_add_fusion.7), channel_id=1, source_target_pairs={{0,8},{4,12},{8,0},{12,4},{1,9},{5,13},{9,1},{13,5},{2,10},{6,14},... | collective-permute-start | bytes 147464 | tf_op jit(solution)/shard_map/ppermute | solution.py:543
  34.2 0.0 collective-permute-done.29
  34.2 0.0 collective-permute-start.7
  34.2 2.2 %collective-permute-done.5 = f32[24,512]{1,0:T(8,128)S(1)} collective-permute-done((f32[24,512]{1,0:T(8,128)S(1)}, f32[24,512]{1,0:T(8,128)S(1)}, u32[]{:S(2)}, u32[]{:S(2)}) %collective-permute-start.5) | collective-permute-done | bytes 49184 | tf_op jit(solution)/shard_map/ppermute | solution.py:543
  36.4 0.0 collective-permute-start.17
  36.4 0.5 collective-permute-start.2
  37.0 0.1 add.63
  37.1 1.4 %collective-permute-done.2.refs_2_ = f32[24,128]{1,0:T(8,128)S(1)} collective-permute-done((f32[24,128]{1,0:T(8,128)S(1)}, f32[24,128]{1,0:T(8,128)S(1)}, u32[]{:S(2)}, u32[]{:S(2)}) %collective-permute-start.2) | collective-permute-done | bytes 12320 | tf_op jit(solution)/shard_map/ppermute | solution.py:549
  38.5 0.1 collective-permute-start.13
  38.6 0.0 collective-permute-done.7.refs_6_
  38.6 1.9 %collective-permute-start.30 = (f32[152,512]{1,0:T(8,128)S(1)}, f32[152,512]{1,0:T(8,128)S(1)}, u32[]{:S(2)}, u32[]{:S(2)}) collective-permute-start(f32[152,512]{1,0:T(8,128)S(1)} %add.67), channel_id=1, source_target_pairs={{0,8},{4,12},{8,0},{12,4},{1,9},{5,13},{9,1},{13,5},{2,10},{6,14},... | collective-permute-start | bytes 933896 | tf_op jit(solution)/shard_map/ppermute | solution.py:543
  40.5 0.1 collective-permute-start.6
  40.6 0.3 collective-permute-start.22
  40.9 6.0 %solve.1 = (f32[48,128]{1,0:T(8,128)S(1)}, f32[128,128]{1,0:T(8,128)S(1)}, f32[128,128]{1,0:T(8,128)S(1)}) custom-call(s32[2]{0:T(128)S(1)} %pad_add_fusion.place_ref.refs_0_, f32[24,128]{1,0:T(8,128)S(1)} %slice_add_fusion.8.refs_1_, f32[24,128]{1,0:T(8,128)S(1)} %collective-permute-done.2.refs_2_, f32[48,128]{1,0:T(8,128)S(1)} %get-tuple-element.56.refs_3_, ...), custom_call_target="tpu_custom_call" | custom-call | flops 5000000000 | bytes 65536 | tf_op jit(solution)/shard_map/solve/pallas_call | solution.py:372
  47.0 0.1 collective-permute-start.32
  47.1 1.7 %collective-permute-start.26 = (f32[152,512]{1,0:T(8,128)S(1)}, f32[152,512]{1,0:T(8,128)S(1)}, u32[]{:S(2)}, u32[]{:S(2)}) collective-permute-start(f32[152,512]{1,0:T(8,128)S(1)} %add.65), channel_id=1, source_target_pairs={{0,8},{4,12},{8,0},{12,4},{1,9},{5,13},{9,1},{13,5},{2,10},{6,14},... | collective-permute-start | bytes 933896 | tf_op jit(solution)/shard_map/ppermute | solution.py:543
  49.0 1.1 fit.1
  50.1 0.1 add.61
  50.2 0.2 collective-permute-start.28
  50.3 0.1 add.59
  50.4 0.4 collective-permute-start.18
  50.9 0.1 collective-permute-start.24
  51.0 17.8 %collective-permute-done.26.refs_8_ = f32[152,512]{1,0:T(8,128)S(1)} collective-permute-done((f32[152,512]{1,0:T(8,128)S(1)}, f32[152,512]{1,0:T(8,128)S(1)}, u32[]{:S(2)}, u32[]{:S(2)}) %collective-permute-start.26) | collective-permute-done | bytes 311328 | tf_op jit(solution)/shard_map/ppermute | solution.py:543
  68.8 1.9 %collective-permute-start.14 = (f32[152,1024]{1,0:T(8,128)S(1)}, f32[152,1024]{1,0:T(8,128)S(1)}, u32[]{:S(2)}, u32[]{:S(2)}) collective-permute-start(f32[152,1024]{1,0:T(8,128)S(1)} %add.59), channel_id=1, source_target_pairs={{0,8},{4,12},{8,0},{12,4},{1,9},{5,13},{9,1},{13,5},{2,10},{6,14},... | collective-permute-start | bytes 1867784 | tf_op jit(solution)/shard_map/ppermute | solution.py:543
  70.8 0.3 collective-permute-start.16
  71.1 11.1 %collective-permute-done.18.refs_8_ = f32[152,1024]{1,0:T(8,128)S(1)} collective-permute-done((f32[152,1024]{1,0:T(8,128)S(1)}, f32[152,1024]{1,0:T(8,128)S(1)}, u32[]{:S(2)}, u32[]{:S(2)}) %collective-permute-start.18) | collective-permute-done | bytes 622624 | tf_op jit(solution)/shard_map/ppermute | solution.py:543
  82.2 1.9 %collective-permute-start.10 = (f32[152,512]{1,0:T(8,128)S(1)}, f32[152,512]{1,0:T(8,128)S(1)}, u32[]{:S(2)}, u32[]{:S(2)}) collective-permute-start(f32[152,512]{1,0:T(8,128)S(1)} %add.57), channel_id=1, source_target_pairs={{0,8},{4,12},{8,0},{12,4},{1,9},{5,13},{9,1},{13,5},{2,10},{6,14},... | collective-permute-start | bytes 933896 | tf_op jit(solution)/shard_map/ppermute | solution.py:543
  84.1 0.1 collective-permute-start.31
  84.2 0.5 collective-permute-start.27
  84.7 10.8 %collective-permute-done.14.refs_8_ = f32[152,1024]{1,0:T(8,128)S(1)} collective-permute-done((f32[152,1024]{1,0:T(8,128)S(1)}, f32[152,1024]{1,0:T(8,128)S(1)}, u32[]{:S(2)}, u32[]{:S(2)}) %collective-permute-start.14) | collective-permute-done | bytes 622624 | tf_op jit(solution)/shard_map/ppermute | solution.py:543
  95.5 6.2 %collective-permute-done.10.refs_8_ = f32[152,512]{1,0:T(8,128)S(1)} collective-permute-done((f32[152,512]{1,0:T(8,128)S(1)}, f32[152,512]{1,0:T(8,128)S(1)}, u32[]{:S(2)}, u32[]{:S(2)}) %collective-permute-start.10) | collective-permute-done | bytes 311328 | tf_op jit(solution)/shard_map/ppermute | solution.py:543
  101.8 1.7 %collective-permute-start.8 = (f32[128,512]{1,0:T(8,128)S(1)}, f32[128,512]{1,0:T(8,128)S(1)}, u32[]{:S(2)}, u32[]{:S(2)}) collective-permute-start(f32[128,512]{1,0:T(8,128)S(1)} %slice_add_fusion), channel_id=1, source_target_pairs={{0,8},{4,12},{8,0},{12,4},{1,9},{5,13},{9,1},{13,5},{2,10},{6,14},... | collective-permute-start | bytes 786440 | tf_op jit(solution)/shard_map/ppermute | solution.py:543
  103.5 0.2 collective-permute-start.19
  103.7 0.3 collective-permute-start.15
  104.0 0.8 collective-permute-done.19.refs_5_
  104.8 0.2 collective-permute-start.11
  105.0 1.9 %shard_map.43.refs_9_ = f32[128,5120]{1,0:T(8,128)} custom-call(s32[2]{0:T(128)S(1)} %pad_add_fusion.place_ref.refs_0_, f32[48,128]{1,0:T(8,128)S(1)} %get-tuple-element.59.refs_1_, f32[128,128]{1,0:T(8,128)S(1)} %get-tuple-element.60.refs_2_, f32[128,128]{1,0:T(8,128)S(1)} %get-tuple-element.58.refs_3_.refs_0_, f32[24,512]{1,0:T(8,128)S(1)} %slice_add_fusion.4.refs_4_, ...), custom_call_target="tpu_custom_call" | custom-call | flops 67108864 | bytes 1048576 | tf_op jit(solution)/shard_map/pallas_call | solution.py:414
  106.9 1.9 %shard_map.44.refs_9_ = f32[128,5120]{1,0:T(8,128)} custom-call(s32[2]{0:T(128)S(1)} %pad_add_fusion.place_ref.refs_0_, f32[48,128]{1,0:T(8,128)S(1)} %get-tuple-element.59.refs_1_, f32[128,128]{1,0:T(8,128)S(1)} %get-tuple-element.60.refs_2_, f32[128,128]{1,0:T(8,128)S(1)} %get-tuple-element.58.refs_3_.refs_0_, ...), custom_call_target="tpu_custom_call", output_to_operand_aliasing={{}: (9, {})} | custom-call | flops 67108864 | bytes 1048576 | tf_op jit(solution)/shard_map/pallas_call | solution.py:414
  108.7 2.5 %shard_map.45.refs_9_ = f32[128,5120]{1,0:T(8,128)} custom-call(s32[2]{0:T(128)S(1)} %pad_add_fusion.place_ref.refs_0_, f32[48,128]{1,0:T(8,128)S(1)} %get-tuple-element.59.refs_1_, f32[128,128]{1,0:T(8,128)S(1)} %get-tuple-element.60.refs_2_, f32[128,128]{1,0:T(8,128)S(1)} %get-tuple-element.58.refs_3_.refs_0_, ...), custom_call_target="tpu_custom_call", output_to_operand_aliasing={{}: (9, {})} | custom-call | flops 134217728 | bytes 2097152 | tf_op jit(solution)/shard_map/pallas_call | solution.py:414
  111.2 2.5 %shard_map.46.refs_9_ = f32[128,5120]{1,0:T(8,128)} custom-call(s32[2]{0:T(128)S(1)} %pad_add_fusion.place_ref.refs_0_, f32[48,128]{1,0:T(8,128)S(1)} %get-tuple-element.59.refs_1_, f32[128,128]{1,0:T(8,128)S(1)} %get-tuple-element.60.refs_2_, f32[128,128]{1,0:T(8,128)S(1)} %get-tuple-element.58.refs_3_.refs_0_, ...), custom_call_target="tpu_custom_call", output_to_operand_aliasing={{}: (9, {})} | custom-call | flops 134217728 | bytes 2097152 | tf_op jit(solution)/shard_map/pallas_call | solution.py:414
  113.7 2.5 %shard_map.47.refs_9_ = f32[128,5120]{1,0:T(8,128)} custom-call(s32[2]{0:T(128)S(1)} %pad_add_fusion.place_ref.refs_0_, f32[48,128]{1,0:T(8,128)S(1)} %get-tuple-element.59.refs_1_, f32[128,128]{1,0:T(8,128)S(1)} %get-tuple-element.60.refs_2_, f32[128,128]{1,0:T(8,128)S(1)} %get-tuple-element.58.refs_3_.refs_0_, ...), custom_call_target="tpu_custom_call", output_to_operand_aliasing={{}: (9, {})} | custom-call | flops 134217728 | bytes 2097152 | tf_op jit(solution)/shard_map/pallas_call | solution.py:414
  116.2 1.9 %shard_map.48.refs_4_ = f32[128,5120]{1,0:T(8,128)} custom-call(s32[2]{0:T(128)S(1)} %pad_add_fusion.place_ref.refs_0_, f32[48,128]{1,0:T(8,128)S(1)} %get-tuple-element.59.refs_1_, f32[128,128]{1,0:T(8,128)S(1)} %get-tuple-element.60.refs_2_, f32[128,128]{1,0:T(8,128)S(1)} %get-tuple-element.58.refs_3_.refs_0_, ...), custom_call_target="tpu_custom_call", output_to_operand_aliasing={{}: (9, {})} | custom-call | flops 67108864 | bytes 1048576 | tf_op jit(solution)/shard_map/pallas_call | solution.py:414
  118.1 0.9 close.1
  (39 shorter events, 0.3 us)
Async XLA Ops:
  22.5 5.1 %collective-permute-start.4 = (f32[152,512]{1,0:T(8,128)S(1)}, f32[152,512]{1,0:T(8,128)S(1)}, u32[]{:S(2)}, u32[]{:S(2)}) collective-permute-start(f32[152,512]{1,0:T(8,128)S(1)} %get-tuple-element.70), channel_id=1, source_target_pairs={{0,4},{4,0},{8,12},{12,8},{1,5},{5,1},{9,13},{13,9},{2,6},{6,2},{1... | collective-permute-start | bytes 933896 | tf_op jit(solution)/shard_map/ppermute | solution.py:520
  23.1 13.3 %collective-permute-start.21 = (f32[152,1024]{1,0:T(8,128)S(1)}, f32[152,1024]{1,0:T(8,128)S(1)}, u32[]{:S(2)}, u32[]{:S(2)}) collective-permute-start(f32[152,1024]{1,0:T(8,128)S(1)} %get-tuple-element.88), channel_id=1, source_target_pairs={{0,4},{4,0},{8,12},{12,8},{1,5},{5,1},{9,13},{13,9},{2,6},{6,2},{1... | collective-permute-start | bytes 1867784 | tf_op jit(solution)/shard_map/ppermute | solution.py:520
  23.2 11.0 %collective-permute-start.29 = (f32[152,512]{1,0:T(8,128)S(1)}, f32[152,512]{1,0:T(8,128)S(1)}, u32[]{:S(2)}, u32[]{:S(2)}) collective-permute-start(f32[152,512]{1,0:T(8,128)S(1)} %get-tuple-element.96), channel_id=1, source_target_pairs={{0,4},{4,0},{8,12},{12,8},{1,5},{5,1},{9,13},{13,9},{2,6},{6,2},{1... | collective-permute-start | bytes 933896 | tf_op jit(solution)/shard_map/ppermute | solution.py:520
  24.9 2.1 %collective-permute-start = (f32[72,128]{1,0:T(8,128)S(1)}, f32[72,128]{1,0:T(8,128)S(1)}, u32[]{:S(2)}, u32[]{:S(2)}) collective-permute-start(f32[72,128]{1,0:T(8,128)S(1)} %get-tuple-element.55), channel_id=1, source_target_pairs={{0,4},{4,0},{8,12},{12,8},{1,5},{5,1},{9,13},{13,9},{2,6},{6,2},{1... | collective-permute-start | bytes 110600 | tf_op jit(solution)/shard_map/ppermute | solution.py:520
  25.0 2.2 %collective-permute-start.3 = (f32[48,128]{1,0:T(8,128)S(1)}, f32[48,128]{1,0:T(8,128)S(1)}, u32[]{:S(2)}, u32[]{:S(2)}) collective-permute-start(f32[48,128]{1,0:T(8,128)S(1)} %get-tuple-element.57), channel_id=1, source_target_pairs={{0,4},{4,0},{8,12},{12,8},{1,5},{5,1},{9,13},{13,9},{2,6},{6,2},{1... | collective-permute-start | bytes 73736 | tf_op jit(solution)/shard_map/ppermute | solution.py:527
  27.0 13.5 %collective-permute-start.25 = (f32[152,512]{1,0:T(8,128)S(1)}, f32[152,512]{1,0:T(8,128)S(1)}, u32[]{:S(2)}, u32[]{:S(2)}) collective-permute-start(f32[152,512]{1,0:T(8,128)S(1)} %get-tuple-element.92), channel_id=1, source_target_pairs={{0,4},{4,0},{8,12},{12,8},{1,5},{5,1},{9,13},{13,9},{2,6},{6,2},{1... | collective-permute-start | bytes 933896 | tf_op jit(solution)/shard_map/ppermute | solution.py:520
  27.2 13.4 %collective-permute-start.9 = (f32[152,512]{1,0:T(8,128)S(1)}, f32[152,512]{1,0:T(8,128)S(1)}, u32[]{:S(2)}, u32[]{:S(2)}) collective-permute-start(f32[152,512]{1,0:T(8,128)S(1)} %get-tuple-element.76), channel_id=1, source_target_pairs={{0,4},{4,0},{8,12},{12,8},{1,5},{5,1},{9,13},{13,9},{2,6},{6,2},{1... | collective-permute-start | bytes 933896 | tf_op jit(solution)/shard_map/ppermute | solution.py:520
  27.7 4.6 %collective-permute-start.1 = (f32[72,128]{1,0:T(8,128)S(1)}, f32[72,128]{1,0:T(8,128)S(1)}, u32[]{:S(2)}, u32[]{:S(2)}) collective-permute-start(f32[72,128]{1,0:T(8,128)S(1)} %add.52), channel_id=1, source_target_pairs={{0,8},{4,12},{8,0},{12,4},{1,9},{5,13},{9,1},{13,5},{2,10},{6,14},... | collective-permute-start | bytes 110600 | tf_op jit(solution)/shard_map/ppermute | solution.py:543
  32.3 4.1 %collective-permute-start.5 = (f32[24,512]{1,0:T(8,128)S(1)}, f32[24,512]{1,0:T(8,128)S(1)}, u32[]{:S(2)}, u32[]{:S(2)}) collective-permute-start(f32[24,512]{1,0:T(8,128)S(1)} %slice_add_fusion.7), channel_id=1, source_target_pairs={{0,8},{4,12},{8,0},{12,4},{1,9},{5,13},{9,1},{13,5},{2,10},{6,14},... | collective-permute-start | bytes 147464 | tf_op jit(solution)/shard_map/ppermute | solution.py:543
  34.2 4.4 %collective-permute-start.7 = (f32[128,512]{1,0:T(8,128)S(1)}, f32[128,512]{1,0:T(8,128)S(1)}, u32[]{:S(2)}, u32[]{:S(2)}) collective-permute-start(f32[128,512]{1,0:T(8,128)S(1)} %get-tuple-element.72), channel_id=1, source_target_pairs={{0,4},{4,0},{8,12},{12,8},{1,5},{5,1},{9,13},{13,9},{2,6},{6,2},{1... | collective-permute-start | bytes 786440 | tf_op jit(solution)/shard_map/ppermute | solution.py:527
  36.4 10.7 %collective-permute-start.17 = (f32[152,1024]{1,0:T(8,128)S(1)}, f32[152,1024]{1,0:T(8,128)S(1)}, u32[]{:S(2)}, u32[]{:S(2)}) collective-permute-start(f32[152,1024]{1,0:T(8,128)S(1)} %get-tuple-element.84), channel_id=1, source_target_pairs={{0,4},{4,0},{8,12},{12,8},{1,5},{5,1},{9,13},{13,9},{2,6},{6,2},{1... | collective-permute-start | bytes 1867784 | tf_op jit(solution)/shard_map/ppermute | solution.py:520
  36.4 2.1 %collective-permute-start.2 = (f32[24,128]{1,0:T(8,128)S(1)}, f32[24,128]{1,0:T(8,128)S(1)}, u32[]{:S(2)}, u32[]{:S(2)}) collective-permute-start(f32[24,128]{1,0:T(8,128)S(1)} %slice_add_fusion.8.refs_1_), channel_id=1, source_target_pairs={{0,4},{4,0},{8,12},{12,8},{1,5},{5,1},{9,13},{13,9},{2,6},{6,2},{1... | collective-permute-start | bytes 36872 | tf_op jit(solution)/shard_map/ppermute | solution.py:549
  38.5 11.7 %collective-permute-start.13 = (f32[152,1024]{1,0:T(8,128)S(1)}, f32[152,1024]{1,0:T(8,128)S(1)}, u32[]{:S(2)}, u32[]{:S(2)}) collective-permute-start(f32[152,1024]{1,0:T(8,128)S(1)} %get-tuple-element.80), channel_id=1, source_target_pairs={{0,4},{4,0},{8,12},{12,8},{1,5},{5,1},{9,13},{13,9},{2,6},{6,2},{1... | collective-permute-start | bytes 1867784 | tf_op jit(solution)/shard_map/ppermute | solution.py:520
  38.6 11.8 %collective-permute-start.30 = (f32[152,512]{1,0:T(8,128)S(1)}, f32[152,512]{1,0:T(8,128)S(1)}, u32[]{:S(2)}, u32[]{:S(2)}) collective-permute-start(f32[152,512]{1,0:T(8,128)S(1)} %add.67), channel_id=1, source_target_pairs={{0,8},{4,12},{8,0},{12,4},{1,9},{5,13},{9,1},{13,5},{2,10},{6,14},... | collective-permute-start | bytes 933896 | tf_op jit(solution)/shard_map/ppermute | solution.py:543
  40.5 6.5 %collective-permute-start.6 = (f32[24,512]{1,0:T(8,128)S(1)}, f32[24,512]{1,0:T(8,128)S(1)}, u32[]{:S(2)}, u32[]{:S(2)}) collective-permute-start(f32[24,512]{1,0:T(8,128)S(1)} %add.55.refs_3_), channel_id=1, source_target_pairs={{0,4},{4,0},{8,12},{12,8},{1,5},{5,1},{9,13},{13,9},{2,6},{6,2},{1... | collective-permute-start | bytes 147464 | tf_op jit(solution)/shard_map/ppermute | solution.py:549
  40.6 28.3 %collective-permute-start.22 = (f32[152,1024]{1,0:T(8,128)S(1)}, f32[152,1024]{1,0:T(8,128)S(1)}, u32[]{:S(2)}, u32[]{:S(2)}) collective-permute-start(f32[152,1024]{1,0:T(8,128)S(1)} %add.63), channel_id=1, source_target_pairs={{0,8},{4,12},{8,0},{12,4},{1,9},{5,13},{9,1},{13,5},{2,10},{6,14},... | collective-permute-start | bytes 1867784 | tf_op jit(solution)/shard_map/ppermute | solution.py:543
  47.0 3.9 %collective-permute-start.32 = (f32[128,512]{1,0:T(8,128)S(1)}, f32[128,512]{1,0:T(8,128)S(1)}, u32[]{:S(2)}, u32[]{:S(2)}) collective-permute-start(f32[128,512]{1,0:T(8,128)S(1)} %get-tuple-element.98), channel_id=1, source_target_pairs={{0,4},{4,0},{8,12},{12,8},{1,5},{5,1},{9,13},{13,9},{2,6},{6,2},{1... | collective-permute-start | bytes 786440 | tf_op jit(solution)/shard_map/ppermute | solution.py:527
  47.1 21.7 %collective-permute-start.26 = (f32[152,512]{1,0:T(8,128)S(1)}, f32[152,512]{1,0:T(8,128)S(1)}, u32[]{:S(2)}, u32[]{:S(2)}) collective-permute-start(f32[152,512]{1,0:T(8,128)S(1)} %add.65), channel_id=1, source_target_pairs={{0,8},{4,12},{8,0},{12,4},{1,9},{5,13},{9,1},{13,5},{2,10},{6,14},... | collective-permute-start | bytes 933896 | tf_op jit(solution)/shard_map/ppermute | solution.py:543
  50.2 20.6 %collective-permute-start.28 = (f32[128,512]{1,0:T(8,128)S(1)}, f32[128,512]{1,0:T(8,128)S(1)}, u32[]{:S(2)}, u32[]{:S(2)}) collective-permute-start(f32[128,512]{1,0:T(8,128)S(1)} %get-tuple-element.94), channel_id=1, source_target_pairs={{0,4},{4,0},{8,12},{12,8},{1,5},{5,1},{9,13},{13,9},{2,6},{6,2},{1... | collective-permute-start | bytes 786440 | tf_op jit(solution)/shard_map/ppermute | solution.py:527
  50.4 31.8 %collective-permute-start.18 = (f32[152,1024]{1,0:T(8,128)S(1)}, f32[152,1024]{1,0:T(8,128)S(1)}, u32[]{:S(2)}, u32[]{:S(2)}) collective-permute-start(f32[152,1024]{1,0:T(8,128)S(1)} %add.61), channel_id=1, source_target_pairs={{0,8},{4,12},{8,0},{12,4},{1,9},{5,13},{9,1},{13,5},{2,10},{6,14},... | collective-permute-start | bytes 1867784 | tf_op jit(solution)/shard_map/ppermute | solution.py:543
  50.9 33.2 %collective-permute-start.24 = (f32[128,1024]{1,0:T(8,128)S(1)}, f32[128,1024]{1,0:T(8,128)S(1)}, u32[]{:S(2)}, u32[]{:S(2)}) collective-permute-start(f32[128,1024]{1,0:T(8,128)S(1)} %get-tuple-element.90), channel_id=1, source_target_pairs={{0,4},{4,0},{8,12},{12,8},{1,5},{5,1},{9,13},{13,9},{2,6},{6,2},{1... | collective-permute-start | bytes 1572872 | tf_op jit(solution)/shard_map/ppermute | solution.py:527
  68.8 15.3 %collective-permute-start.20 = (f32[128,1024]{1,0:T(8,128)S(1)}, f32[128,1024]{1,0:T(8,128)S(1)}, u32[]{:S(2)}, u32[]{:S(2)}) collective-permute-start(f32[128,1024]{1,0:T(8,128)S(1)} %get-tuple-element.86), channel_id=1, source_target_pairs={{0,4},{4,0},{8,12},{12,8},{1,5},{5,1},{9,13},{13,9},{2,6},{6,2},{1... | collective-permute-start | bytes 1572872 | tf_op jit(solution)/shard_map/ppermute | solution.py:527
  68.8 26.7 %collective-permute-start.14 = (f32[152,1024]{1,0:T(8,128)S(1)}, f32[152,1024]{1,0:T(8,128)S(1)}, u32[]{:S(2)}, u32[]{:S(2)}) collective-permute-start(f32[152,1024]{1,0:T(8,128)S(1)} %add.59), channel_id=1, source_target_pairs={{0,8},{4,12},{8,0},{12,4},{1,9},{5,13},{9,1},{13,5},{2,10},{6,14},... | collective-permute-start | bytes 1867784 | tf_op jit(solution)/shard_map/ppermute | solution.py:543
  70.8 42.9 %collective-permute-start.16 = (f32[128,1024]{1,0:T(8,128)S(1)}, f32[128,1024]{1,0:T(8,128)S(1)}, u32[]{:S(2)}, u32[]{:S(2)}) collective-permute-start(f32[128,1024]{1,0:T(8,128)S(1)} %get-tuple-element.82), channel_id=1, source_target_pairs={{0,4},{4,0},{8,12},{12,8},{1,5},{5,1},{9,13},{13,9},{2,6},{6,2},{1... | collective-permute-start | bytes 1572872 | tf_op jit(solution)/shard_map/ppermute | solution.py:527
  82.2 19.6 %collective-permute-start.10 = (f32[152,512]{1,0:T(8,128)S(1)}, f32[152,512]{1,0:T(8,128)S(1)}, u32[]{:S(2)}, u32[]{:S(2)}) collective-permute-start(f32[152,512]{1,0:T(8,128)S(1)} %add.57), channel_id=1, source_target_pairs={{0,8},{4,12},{8,0},{12,4},{1,9},{5,13},{9,1},{13,5},{2,10},{6,14},... | collective-permute-start | bytes 933896 | tf_op jit(solution)/shard_map/ppermute | solution.py:543
  84.1 17.7 %collective-permute-start.31 = (f32[24,512]{1,0:T(8,128)S(1)}, f32[24,512]{1,0:T(8,128)S(1)}, u32[]{:S(2)}, u32[]{:S(2)}) collective-permute-start(f32[24,512]{1,0:T(8,128)S(1)} %slice_add_fusion.4.refs_4_), channel_id=1, source_target_pairs={{0,4},{4,0},{8,12},{12,8},{1,5},{5,1},{9,13},{13,9},{2,6},{6,2},{1... | collective-permute-start | bytes 147464 | tf_op jit(solution)/shard_map/ppermute | solution.py:549
  84.2 19.3 %collective-permute-start.27 = (f32[24,512]{1,0:T(8,128)S(1)}, f32[24,512]{1,0:T(8,128)S(1)}, u32[]{:S(2)}, u32[]{:S(2)}) collective-permute-start(f32[24,512]{1,0:T(8,128)S(1)} %slice_add_fusion.5.refs_4_), channel_id=1, source_target_pairs={{0,4},{4,0},{8,12},{12,8},{1,5},{5,1},{9,13},{13,9},{2,6},{6,2},{1... | collective-permute-start | bytes 147464 | tf_op jit(solution)/shard_map/ppermute | solution.py:549
  95.5 8.2 %collective-permute-start.23 = (f32[24,1024]{1,0:T(8,128)S(1)}, f32[24,1024]{1,0:T(8,128)S(1)}, u32[]{:S(2)}, u32[]{:S(2)}) collective-permute-start(f32[24,1024]{1,0:T(8,128)S(1)} %slice_add_fusion.1.refs_4_), channel_id=1, source_target_pairs={{0,4},{4,0},{8,12},{12,8},{1,5},{5,1},{9,13},{13,9},{2,6},{6,2},{1... | collective-permute-start | bytes 294920 | tf_op jit(solution)/shard_map/ppermute | solution.py:549
  101.8 14.5 %collective-permute-start.12 = (f32[128,512]{1,0:T(8,128)S(1)}, f32[128,512]{1,0:T(8,128)S(1)}, u32[]{:S(2)}, u32[]{:S(2)}) collective-permute-start(f32[128,512]{1,0:T(8,128)S(1)} %get-tuple-element.78), channel_id=1, source_target_pairs={{0,4},{4,0},{8,12},{12,8},{1,5},{5,1},{9,13},{13,9},{2,6},{6,2},{1... | collective-permute-start | bytes 786440 | tf_op jit(solution)/shard_map/ppermute | solution.py:527
  101.8 16.3 %collective-permute-start.8 = (f32[128,512]{1,0:T(8,128)S(1)}, f32[128,512]{1,0:T(8,128)S(1)}, u32[]{:S(2)}, u32[]{:S(2)}) collective-permute-start(f32[128,512]{1,0:T(8,128)S(1)} %slice_add_fusion), channel_id=1, source_target_pairs={{0,8},{4,12},{8,0},{12,4},{1,9},{5,13},{9,1},{13,5},{2,10},{6,14},... | collective-permute-start | bytes 786440 | tf_op jit(solution)/shard_map/ppermute | solution.py:543
  103.5 1.3 %collective-permute-start.19 = (f32[24,1024]{1,0:T(8,128)S(1)}, f32[24,1024]{1,0:T(8,128)S(1)}, u32[]{:S(2)}, u32[]{:S(2)}) collective-permute-start(f32[24,1024]{1,0:T(8,128)S(1)} %slice_add_fusion.2.refs_4_), channel_id=1, source_target_pairs={{0,4},{4,0},{8,12},{12,8},{1,5},{5,1},{9,13},{13,9},{2,6},{6,2},{1... | collective-permute-start | bytes 294920 | tf_op jit(solution)/shard_map/ppermute | solution.py:549
  103.7 10.0 %collective-permute-start.15 = (f32[24,1024]{1,0:T(8,128)S(1)}, f32[24,1024]{1,0:T(8,128)S(1)}, u32[]{:S(2)}, u32[]{:S(2)}) collective-permute-start(f32[24,1024]{1,0:T(8,128)S(1)} %slice_add_fusion.3.refs_4_), channel_id=1, source_target_pairs={{0,4},{4,0},{8,12},{12,8},{1,5},{5,1},{9,13},{13,9},{2,6},{6,2},{1... | collective-permute-start | bytes 294920 | tf_op jit(solution)/shard_map/ppermute | solution.py:549
  104.8 11.4 %collective-permute-start.11 = (f32[24,512]{1,0:T(8,128)S(1)}, f32[24,512]{1,0:T(8,128)S(1)}, u32[]{:S(2)}, u32[]{:S(2)}) collective-permute-start(f32[24,512]{1,0:T(8,128)S(1)} %slice_add_fusion.6.refs_4_), channel_id=1, source_target_pairs={{0,4},{4,0},{8,12},{12,8},{1,5},{5,1},{9,13},{13,9},{2,6},{6,2},{1... | collective-permute-start | bytes 147464 | tf_op jit(solution)/shard_map/ppermute | solution.py:549

commit v5 on v4

--- a/solution.py
+++ b/solution.py
@@ -174,8 +174,9 @@
         left_ref[2 * far + index * size : 2 * far + (index + 1) * size, :] = part
     step = subjects // PIECES
     direct = 2 * rows % LANES == 0
-    for index, copy in enumerate(geno_copies):
+    for copy in geno_copies:
         copy.wait()
+    for index in range(PIECES):
         low, high = index * step, (index + 1) * step
         if direct:
             for slot in range(chips - 1):
@@ -191,7 +192,9 @@
         for side, own in ((0, 1 - core), (1, core)):
             low = side * far + slot * rows
             left_ref[low : low + rows, :] = turned[pl.ds(pl.multiple_of(target + own * rows, rows), rows), :]
-    multiply_far(left_ref, first, first_copies, give_far, keep_far, small, core, half)
+    for copy in first_copies:
+        copy.wait()
+    multiply_far(left_ref, first, [], give_far, keep_far, small, core, half)
     for copy in later_copies:
         copy.wait()
 
@@ -472,7 +475,7 @@
 
 def close(done, total, start, dof, geno_var, pheno_var, terms):
     rows, width = terms[0].shape
-    tile = min(STRIP, width)
+    tile = min(TILE, width)
     first = start // tile
     args = [geno_var, pheno_var, *terms]
     specs = [VMEM] * len(args)

time: 119 us -> 118 us (level)
  no operation moved by 1% of the time
where the time goes in v5:
time: 118 us
  waiting for transfers between devices  52.5 us (44%)
  Pallas kernels  45.5 us (39%)
  starting transfers between devices  19.5 us (17%)
    ppermute x9, waiting for transfers between devices, far_terms(): came.append(lax.ppermute(block, 'subj', moves))  50.2 us
    pallas_call x5, Pallas kernels, product(): pl.pallas_call(functools.partial(product_kernel, half, start + width), ou...  15 us
    ppermute x9, starting transfers between devices, far_terms(): came.append(lax.ppermute(block, 'subj', moves))  14.4 us
    pallas_call x6, Pallas kernels, finish(): pl.pallas_call(functools.partial(finish_kernel, dof, len(terms)), grid=(w...  13 us
    pallas_call x1, Pallas kernels, solve(): pl.pallas_call(functools.partial(solve_kernel, live, half, len(terms)), o...  5.97 us
    pallas_call x1, Pallas kernels, open_up(): pl.pallas_call(functools.partial(open_kernel, chips, rows, half), out_sha...  3.96 us
    pallas_call x1, Pallas kernels, open_near(): pl.pallas_call(functools.partial(near_kernel, rows, sum(widths), len(here...  2.76 us
  transfers between devices with their start and end apart: 33, of which 8 were waited for; matrix products, arithmetic and copies ran while one was open for 0% of the time, Pallas kernels for 19%

profile of v5, /device:TPU:0, one launch (start us, length us, event | category | flops | bytes accessed | tf_op | source)
XLA Modules:
  0.0 118.3 jit_solution(14769294391642457553)
XLA Ops:
  0.0 0.1 pad_add_fusion.place_ref.refs_0_
  0.1 4.0 %open.1 = (bf16[400,2048]{1,0:T(8,128)(2,1)S(1)}, bf16[2048,512]{1,0:T(8,128)(2,1)S(1)}, f32[152,512]{1,0:T(8,128)S(1)}, f32[152,512]{1,0:T(8,128)S(1)}, bf16[20...) custom-call(s32[2]{0:T(128)S(1)} %pad_add_fusion.place_ref.refs_0_, bf16[2048,512]{1,0:T(8,128)(2,1)} %geno_ref.1, ...), custom_call_target="tpu_custom_call" | custom-call | flops 838860800 | bytes 4194304 | tf_op jit(solution)/shard_map/open/pallas_call | solution.py:251
  4.0 2.8 %open_near.1 = (bf16[256,2048]{1,0:T(8,128)(2,1)S(1)}, f32[128,512]{1,0:T(8,128)S(1)}, f32[128,512]{1,0:T(8,128)S(1)}, f32[128,512]{1,0:T(8,128)S(1)}, f32[128,5...) custom-call(s32[2]{0:T(128)S(1)} %pad_add_fusion.place_ref.refs_0_, bf16[2048,512]{1,0:T(8,128)(2,1)S(1)} %get-tuple-element.53.geno_ref, ...), custom_call_target="tpu_custom_call" | custom-call | flops 1073741824 | bytes 4194304 | tf_op jit(solution)/shard_map/open_near/pallas_call | solution.py:274
  6.8 3.5 %shard_map.37 = (f32[152,1024]{1,0:T(8,128)S(1)}, f32[128,1024]{1,0:T(8,128)S(1)}, f32[152,1024]{1,0:T(8,128)S(1)}, f32[128,1024]{1,0:T(8,128)S(1)}, bf16[2048,1024]{1,0:T(8,128)(2,1)S(1)}) custom-call(s32[2]{0:T(128)S(1)} %pad_add_fusion.place_ref.refs_0_, bf16[400,2048]{1,0:T(8,128)(2,1)S(1)} %get-tuple-element.52.left_ref.far_ref, ...), custom_call_target="tpu_custom_call" | custom-call | flops 2751463424 | bytes 4194304 | tf_op jit(solution)/shard_map/pallas_call | solution.py:328
  10.3 3.5 %shard_map.38 = (f32[152,1024]{1,0:T(8,128)S(1)}, f32[128,1024]{1,0:T(8,128)S(1)}, f32[152,1024]{1,0:T(8,128)S(1)}, f32[128,1024]{1,0:T(8,128)S(1)}, bf16[2048,1024]{1,0:T(8,128)(2,1)S(1)}) custom-call(s32[2]{0:T(128)S(1)} %pad_add_fusion.place_ref.refs_0_, bf16[400,2048]{1,0:T(8,128)(2,1)S(1)} %get-tuple-element.52.left_ref.far_ref, ...), custom_call_target="tpu_custom_call" | custom-call | flops 2751463424 | bytes 4194304 | tf_op jit(solution)/shard_map/pallas_call | solution.py:328
  13.9 3.5 %shard_map.39 = (f32[152,1024]{1,0:T(8,128)S(1)}, f32[128,1024]{1,0:T(8,128)S(1)}, f32[152,1024]{1,0:T(8,128)S(1)}, f32[128,1024]{1,0:T(8,128)S(1)}, bf16[2048,512]{1,0:T(8,128)(2,1)S(1)}) custom-call(s32[2]{0:T(128)S(1)} %pad_add_fusion.place_ref.refs_0_, bf16[400,2048]{1,0:T(8,128)(2,1)S(1)} %get-tuple-element.52.left_ref.far_ref, ...), custom_call_target="tpu_custom_call" | custom-call | flops 2751463424 | bytes 4194304 | tf_op jit(solution)/shard_map/pallas_call | solution.py:328
  17.4 2.1 %shard_map.40 = (f32[152,512]{1,0:T(8,128)S(1)}, f32[128,512]{1,0:T(8,128)S(1)}, f32[152,512]{1,0:T(8,128)S(1)}, f32[128,512]{1,0:T(8,128)S(1)}, bf16[2048,512]{1,0:T(8,128)(2,1)S(1)}) custom-call(s32[2]{0:T(128)S(1)} %pad_add_fusion.place_ref.refs_0_, bf16[400,2048]{1,0:T(8,128)(2,1)S(1)} %get-tuple-element.52.left_ref.far_ref, ...), custom_call_target="tpu_custom_call" | custom-call | flops 1375731712 | bytes 2097152 | tf_op jit(solution)/shard_map/pallas_call | solution.py:328
  19.6 2.3 %shard_map.41 = (f32[152,512]{1,0:T(8,128)S(1)}, f32[128,512]{1,0:T(8,128)S(1)}, f32[152,512]{1,0:T(8,128)S(1)}, f32[128,512]{1,0:T(8,128)S(1)}) custom-call(s32[2]{0:T(128)S(1)} %pad_add_fusion.place_ref.refs_0_, bf16[400,2048]{1,0:T(8,128)(2,1)S(1)} %get-tuple-element.52.left_ref.far_ref, bf16[256,2048]{1,0:T(8,128)(2,1)S(1)} %get-tuple-element.63.near_ref, ...), custom_call_target="tpu_custom_call" | custom-call | flops 1375731712 | bytes 2097152 | tf_op jit(solution)/shard_map/pallas_call | solution.py:328
  21.9 0.6 collective-permute-start.4
  22.4 0.1 collective-permute-start.21
  22.5 0.4 collective-permute-start.29
  23.0 1.3 %with_design.1 = (f32[72,128]{1,0:T(8,128)S(1)}, f32[48,128]{1,0:T(8,128)S(1)}, f32[72,128]{1,0:T(8,128)S(1)}, f32[48,128]{1,0:T(8,128)S(1)}) custom-call(s32[2]{0:T(128)S(1)} %pad_add_fusion.place_ref.refs_0_, bf16[400,2048]{1,0:T(8,128)(2,1)S(1)} %get-tuple-element.52.left_ref.far_ref, bf16[2048,512]{1,0:T(8,128)(2,1)S(1)} %get-tuple-element.53.geno_ref), custom_call_target="tpu_custom_call" | custom-call | flops 301989888 | bytes 2097152 | tf_op jit(solution)/shard_map/with_design/pallas_call | solution.py:134
  24.2 0.1 collective-permute-start
  24.4 0.4 collective-permute-start.3
  24.8 1.6 %shard_map.42 = (f32[152,512]{1,0:T(8,128)S(1)}, f32[152,512]{1,0:T(8,128)S(1)}) custom-call(s32[2]{0:T(128)S(1)} %pad_add_fusion.place_ref.refs_0_, bf16[400,2048]{1,0:T(8,128)(2,1)S(1)} %get-tuple-element.52.left_ref.far_ref, bf16[2048,512]{1,0:T(8,128)(2,1)S(1)} %get-tuple-element.62.refs_1_.here_ref), custom_call_target="tpu_custom_call" | custom-call | flops 838860800 | bytes 2097152 | tf_op jit(solution)/shard_map/pallas_call | solution.py:294
  26.4 0.1 collective-permute-start.25
  26.5 0.0 collective-permute-done.3.refs_4_
  26.5 0.5 collective-permute-start.9
  27.0 0.0 collective-permute-done.4
  27.0 2.6 %collective-permute-start.1 = (f32[72,128]{1,0:T(8,128)S(1)}, f32[72,128]{1,0:T(8,128)S(1)}, u32[]{:S(2)}, u32[]{:S(2)}) collective-permute-start(f32[72,128]{1,0:T(8,128)S(1)} %add.52), channel_id=1, source_target_pairs={{0,8},{4,12},{8,0},{12,4},{1,9},{5,13},{9,1},{13,5},{2,10},{6,14},... | collective-permute-start | bytes 110600 | tf_op jit(solution)/shard_map/ppermute | solution.py:546
  29.6 2.1 %collective-permute-done.1 = f32[72,128]{1,0:T(8,128)S(1)} collective-permute-done((f32[72,128]{1,0:T(8,128)S(1)}, f32[72,128]{1,0:T(8,128)S(1)}, u32[]{:S(2)}, u32[]{:S(2)}) %collective-permute-start.1) | collective-permute-done | bytes 36896 | tf_op jit(solution)/shard_map/ppermute | solution.py:546
  31.7 1.9 %collective-permute-start.5 = (f32[24,512]{1,0:T(8,128)S(1)}, f32[24,512]{1,0:T(8,128)S(1)}, u32[]{:S(2)}, u32[]{:S(2)}) collective-permute-start(f32[24,512]{1,0:T(8,128)S(1)} %slice_add_fusion.7), channel_id=1, source_target_pairs={{0,8},{4,12},{8,0},{12,4},{1,9},{5,13},{9,1},{13,5},{2,10},{6,14},... | collective-permute-start | bytes 147464 | tf_op jit(solution)/shard_map/ppermute | solution.py:546
  33.5 0.0 collective-permute-done.29
  33.5 0.0 collective-permute-start.7
  33.6 2.2 %collective-permute-done.5 = f32[24,512]{1,0:T(8,128)S(1)} collective-permute-done((f32[24,512]{1,0:T(8,128)S(1)}, f32[24,512]{1,0:T(8,128)S(1)}, u32[]{:S(2)}, u32[]{:S(2)}) %collective-permute-start.5) | collective-permute-done | bytes 49184 | tf_op jit(solution)/shard_map/ppermute | solution.py:546
  35.7 0.0 collective-permute-start.17
  35.8 0.5 collective-permute-start.2
  36.3 0.1 add.63
  36.4 1.4 %collective-permute-done.2.refs_2_ = f32[24,128]{1,0:T(8,128)S(1)} collective-permute-done((f32[24,128]{1,0:T(8,128)S(1)}, f32[24,128]{1,0:T(8,128)S(1)}, u32[]{:S(2)}, u32[]{:S(2)}) %collective-permute-start.2) | collective-permute-done | bytes 12320 | tf_op jit(solution)/shard_map/ppermute | solution.py:552
  37.8 0.1 collective-permute-start.13
  38.0 0.0 collective-permute-done.7.refs_6_
  38.0 1.9 %collective-permute-start.30 = (f32[152,512]{1,0:T(8,128)S(1)}, f32[152,512]{1,0:T(8,128)S(1)}, u32[]{:S(2)}, u32[]{:S(2)}) collective-permute-start(f32[152,512]{1,0:T(8,128)S(1)} %add.67), channel_id=1, source_target_pairs={{0,8},{4,12},{8,0},{12,4},{1,9},{5,13},{9,1},{13,5},{2,10},{6,14},... | collective-permute-start | bytes 933896 | tf_op jit(solution)/shard_map/ppermute | solution.py:546
  39.9 0.1 collective-permute-start.6
  39.9 0.3 collective-permute-start.22
  40.3 6.0 %solve.1 = (f32[48,128]{1,0:T(8,128)S(1)}, f32[128,128]{1,0:T(8,128)S(1)}, f32[128,128]{1,0:T(8,128)S(1)}) custom-call(s32[2]{0:T(128)S(1)} %pad_add_fusion.place_ref.refs_0_, f32[24,128]{1,0:T(8,128)S(1)} %slice_add_fusion.8.refs_1_, f32[24,128]{1,0:T(8,128)S(1)} %collective-permute-done.2.refs_2_, f32[48,128]{1,0:T(8,128)S(1)} %get-tuple-element.56.refs_3_, ...), custom_call_target="tpu_custom_call" | custom-call | flops 5000000000 | bytes 65536 | tf_op jit(solution)/shard_map/solve/pallas_call | solution.py:375
  46.3 0.1 collective-permute-start.32
  46.5 1.7 %collective-permute-start.26 = (f32[152,512]{1,0:T(8,128)S(1)}, f32[152,512]{1,0:T(8,128)S(1)}, u32[]{:S(2)}, u32[]{:S(2)}) collective-permute-start(f32[152,512]{1,0:T(8,128)S(1)} %add.65), channel_id=1, source_target_pairs={{0,8},{4,12},{8,0},{12,4},{1,9},{5,13},{9,1},{13,5},{2,10},{6,14},... | collective-permute-start | bytes 933896 | tf_op jit(solution)/shard_map/ppermute | solution.py:546
  48.3 1.1 fit.1
  49.4 0.1 add.61
  49.5 0.2 collective-permute-start.28
  49.7 0.1 add.59
  49.8 0.4 collective-permute-start.18
  50.2 0.1 collective-permute-start.24
  50.4 17.8 %collective-permute-done.26.refs_8_ = f32[152,512]{1,0:T(8,128)S(1)} collective-permute-done((f32[152,512]{1,0:T(8,128)S(1)}, f32[152,512]{1,0:T(8,128)S(1)}, u32[]{:S(2)}, u32[]{:S(2)}) %collective-permute-start.26) | collective-permute-done | bytes 311328 | tf_op jit(solution)/shard_map/ppermute | solution.py:546
  68.2 1.9 %collective-permute-start.14 = (f32[152,1024]{1,0:T(8,128)S(1)}, f32[152,1024]{1,0:T(8,128)S(1)}, u32[]{:S(2)}, u32[]{:S(2)}) collective-permute-start(f32[152,1024]{1,0:T(8,128)S(1)} %add.59), channel_id=1, source_target_pairs={{0,8},{4,12},{8,0},{12,4},{1,9},{5,13},{9,1},{13,5},{2,10},{6,14},... | collective-permute-start | bytes 1867784 | tf_op jit(solution)/shard_map/ppermute | solution.py:546
  70.1 0.3 collective-permute-start.16
  70.4 11.1 %collective-permute-done.18.refs_8_ = f32[152,1024]{1,0:T(8,128)S(1)} collective-permute-done((f32[152,1024]{1,0:T(8,128)S(1)}, f32[152,1024]{1,0:T(8,128)S(1)}, u32[]{:S(2)}, u32[]{:S(2)}) %collective-permute-start.18) | collective-permute-done | bytes 622624 | tf_op jit(solution)/shard_map/ppermute | solution.py:546
  81.5 1.9 %collective-permute-start.10 = (f32[152,512]{1,0:T(8,128)S(1)}, f32[152,512]{1,0:T(8,128)S(1)}, u32[]{:S(2)}, u32[]{:S(2)}) collective-permute-start(f32[152,512]{1,0:T(8,128)S(1)} %add.57), channel_id=1, source_target_pairs={{0,8},{4,12},{8,0},{12,4},{1,9},{5,13},{9,1},{13,5},{2,10},{6,14},... | collective-permute-start | bytes 933896 | tf_op jit(solution)/shard_map/ppermute | solution.py:546
  83.5 0.1 collective-permute-start.31
  83.5 0.5 collective-permute-start.27
  84.0 10.8 %collective-permute-done.14.refs_8_ = f32[152,1024]{1,0:T(8,128)S(1)} collective-permute-done((f32[152,1024]{1,0:T(8,128)S(1)}, f32[152,1024]{1,0:T(8,128)S(1)}, u32[]{:S(2)}, u32[]{:S(2)}) %collective-permute-start.14) | collective-permute-done | bytes 622624 | tf_op jit(solution)/shard_map/ppermute | solution.py:546
  94.9 6.2 %collective-permute-done.10.refs_8_ = f32[152,512]{1,0:T(8,128)S(1)} collective-permute-done((f32[152,512]{1,0:T(8,128)S(1)}, f32[152,512]{1,0:T(8,128)S(1)}, u32[]{:S(2)}, u32[]{:S(2)}) %collective-permute-start.10) | collective-permute-done | bytes 311328 | tf_op jit(solution)/shard_map/ppermute | solution.py:546
  101.1 1.7 %collective-permute-start.8 = (f32[128,512]{1,0:T(8,128)S(1)}, f32[128,512]{1,0:T(8,128)S(1)}, u32[]{:S(2)}, u32[]{:S(2)}) collective-permute-start(f32[128,512]{1,0:T(8,128)S(1)} %slice_add_fusion), channel_id=1, source_target_pairs={{0,8},{4,12},{8,0},{12,4},{1,9},{5,13},{9,1},{13,5},{2,10},{6,14},... | collective-permute-start | bytes 786440 | tf_op jit(solution)/shard_map/ppermute | solution.py:546
  102.9 0.2 collective-permute-start.19
  103.1 0.3 collective-permute-start.15
  103.4 0.8 collective-permute-done.19.refs_5_
  104.2 0.2 collective-permute-start.11
  104.4 1.9 %shard_map.43.refs_9_ = f32[128,5120]{1,0:T(8,128)} custom-call(s32[2]{0:T(128)S(1)} %pad_add_fusion.place_ref.refs_0_, f32[48,128]{1,0:T(8,128)S(1)} %get-tuple-element.59.refs_1_, f32[128,128]{1,0:T(8,128)S(1)} %get-tuple-element.60.refs_2_, f32[128,128]{1,0:T(8,128)S(1)} %get-tuple-element.58.refs_3_.refs_0_, f32[24,512]{1,0:T(8,128)S(1)} %slice_add_fusion.4.refs_4_, ...), custom_call_target="tpu_custom_call" | custom-call | flops 67108864 | bytes 1048576 | tf_op jit(solution)/shard_map/pallas_call | solution.py:417
  106.2 1.9 %shard_map.44.refs_9_ = f32[128,5120]{1,0:T(8,128)} custom-call(s32[2]{0:T(128)S(1)} %pad_add_fusion.place_ref.refs_0_, f32[48,128]{1,0:T(8,128)S(1)} %get-tuple-element.59.refs_1_, f32[128,128]{1,0:T(8,128)S(1)} %get-tuple-element.60.refs_2_, f32[128,128]{1,0:T(8,128)S(1)} %get-tuple-element.58.refs_3_.refs_0_, ...), custom_call_target="tpu_custom_call", output_to_operand_aliasing={{}: (9, {})} | custom-call | flops 67108864 | bytes 1048576 | tf_op jit(solution)/shard_map/pallas_call | solution.py:417
  108.1 2.5 %shard_map.45.refs_9_ = f32[128,5120]{1,0:T(8,128)} custom-call(s32[2]{0:T(128)S(1)} %pad_add_fusion.place_ref.refs_0_, f32[48,128]{1,0:T(8,128)S(1)} %get-tuple-element.59.refs_1_, f32[128,128]{1,0:T(8,128)S(1)} %get-tuple-element.60.refs_2_, f32[128,128]{1,0:T(8,128)S(1)} %get-tuple-element.58.refs_3_.refs_0_, ...), custom_call_target="tpu_custom_call", output_to_operand_aliasing={{}: (9, {})} | custom-call | flops 134217728 | bytes 2097152 | tf_op jit(solution)/shard_map/pallas_call | solution.py:417
  110.6 2.5 %shard_map.46.refs_9_ = f32[128,5120]{1,0:T(8,128)} custom-call(s32[2]{0:T(128)S(1)} %pad_add_fusion.place_ref.refs_0_, f32[48,128]{1,0:T(8,128)S(1)} %get-tuple-element.59.refs_1_, f32[128,128]{1,0:T(8,128)S(1)} %get-tuple-element.60.refs_2_, f32[128,128]{1,0:T(8,128)S(1)} %get-tuple-element.58.refs_3_.refs_0_, ...), custom_call_target="tpu_custom_call", output_to_operand_aliasing={{}: (9, {})} | custom-call | flops 134217728 | bytes 2097152 | tf_op jit(solution)/shard_map/pallas_call | solution.py:417
  113.1 2.5 %shard_map.47.refs_9_ = f32[128,5120]{1,0:T(8,128)} custom-call(s32[2]{0:T(128)S(1)} %pad_add_fusion.place_ref.refs_0_, f32[48,128]{1,0:T(8,128)S(1)} %get-tuple-element.59.refs_1_, f32[128,128]{1,0:T(8,128)S(1)} %get-tuple-element.60.refs_2_, f32[128,128]{1,0:T(8,128)S(1)} %get-tuple-element.58.refs_3_.refs_0_, ...), custom_call_target="tpu_custom_call", output_to_operand_aliasing={{}: (9, {})} | custom-call | flops 134217728 | bytes 2097152 | tf_op jit(solution)/shard_map/pallas_call | solution.py:417
  115.6 1.9 %shard_map.48.refs_4_ = f32[128,5120]{1,0:T(8,128)} custom-call(s32[2]{0:T(128)S(1)} %pad_add_fusion.place_ref.refs_0_, f32[48,128]{1,0:T(8,128)S(1)} %get-tuple-element.59.refs_1_, f32[128,128]{1,0:T(8,128)S(1)} %get-tuple-element.60.refs_2_, f32[128,128]{1,0:T(8,128)S(1)} %get-tuple-element.58.refs_3_.refs_0_, ...), custom_call_target="tpu_custom_call", output_to_operand_aliasing={{}: (9, {})} | custom-call | flops 67108864 | bytes 1048576 | tf_op jit(solution)/shard_map/pallas_call | solution.py:417
  117.4 0.8 close.1
  (39 shorter events, 0.3 us)
Async XLA Ops:
  21.9 5.1 %collective-permute-start.4 = (f32[152,512]{1,0:T(8,128)S(1)}, f32[152,512]{1,0:T(8,128)S(1)}, u32[]{:S(2)}, u32[]{:S(2)}) collective-permute-start(f32[152,512]{1,0:T(8,128)S(1)} %get-tuple-element.70), channel_id=1, source_target_pairs={{0,4},{4,0},{8,12},{12,8},{1,5},{5,1},{9,13},{13,9},{2,6},{6,2},{1... | collective-permute-start | bytes 933896 | tf_op jit(solution)/shard_map/ppermute | solution.py:523
  22.4 13.3 %collective-permute-start.21 = (f32[152,1024]{1,0:T(8,128)S(1)}, f32[152,1024]{1,0:T(8,128)S(1)}, u32[]{:S(2)}, u32[]{:S(2)}) collective-permute-start(f32[152,1024]{1,0:T(8,128)S(1)} %get-tuple-element.88), channel_id=1, source_target_pairs={{0,4},{4,0},{8,12},{12,8},{1,5},{5,1},{9,13},{13,9},{2,6},{6,2},{1... | collective-permute-start | bytes 1867784 | tf_op jit(solution)/shard_map/ppermute | solution.py:523
  22.5 11.0 %collective-permute-start.29 = (f32[152,512]{1,0:T(8,128)S(1)}, f32[152,512]{1,0:T(8,128)S(1)}, u32[]{:S(2)}, u32[]{:S(2)}) collective-permute-start(f32[152,512]{1,0:T(8,128)S(1)} %get-tuple-element.96), channel_id=1, source_target_pairs={{0,4},{4,0},{8,12},{12,8},{1,5},{5,1},{9,13},{13,9},{2,6},{6,2},{1... | collective-permute-start | bytes 933896 | tf_op jit(solution)/shard_map/ppermute | solution.py:523
  24.2 2.1 %collective-permute-start = (f32[72,128]{1,0:T(8,128)S(1)}, f32[72,128]{1,0:T(8,128)S(1)}, u32[]{:S(2)}, u32[]{:S(2)}) collective-permute-start(f32[72,128]{1,0:T(8,128)S(1)} %get-tuple-element.55), channel_id=1, source_target_pairs={{0,4},{4,0},{8,12},{12,8},{1,5},{5,1},{9,13},{13,9},{2,6},{6,2},{1... | collective-permute-start | bytes 110600 | tf_op jit(solution)/shard_map/ppermute | solution.py:523
  24.4 2.2 %collective-permute-start.3 = (f32[48,128]{1,0:T(8,128)S(1)}, f32[48,128]{1,0:T(8,128)S(1)}, u32[]{:S(2)}, u32[]{:S(2)}) collective-permute-start(f32[48,128]{1,0:T(8,128)S(1)} %get-tuple-element.57), channel_id=1, source_target_pairs={{0,4},{4,0},{8,12},{12,8},{1,5},{5,1},{9,13},{13,9},{2,6},{6,2},{1... | collective-permute-start | bytes 73736 | tf_op jit(solution)/shard_map/ppermute | solution.py:530
  26.4 13.5 %collective-permute-start.25 = (f32[152,512]{1,0:T(8,128)S(1)}, f32[152,512]{1,0:T(8,128)S(1)}, u32[]{:S(2)}, u32[]{:S(2)}) collective-permute-start(f32[152,512]{1,0:T(8,128)S(1)} %get-tuple-element.92), channel_id=1, source_target_pairs={{0,4},{4,0},{8,12},{12,8},{1,5},{5,1},{9,13},{13,9},{2,6},{6,2},{1... | collective-permute-start | bytes 933896 | tf_op jit(solution)/shard_map/ppermute | solution.py:523
  26.5 13.4 %collective-permute-start.9 = (f32[152,512]{1,0:T(8,128)S(1)}, f32[152,512]{1,0:T(8,128)S(1)}, u32[]{:S(2)}, u32[]{:S(2)}) collective-permute-start(f32[152,512]{1,0:T(8,128)S(1)} %get-tuple-element.76), channel_id=1, source_target_pairs={{0,4},{4,0},{8,12},{12,8},{1,5},{5,1},{9,13},{13,9},{2,6},{6,2},{1... | collective-permute-start | bytes 933896 | tf_op jit(solution)/shard_map/ppermute | solution.py:523
  27.0 4.6 %collective-permute-start.1 = (f32[72,128]{1,0:T(8,128)S(1)}, f32[72,128]{1,0:T(8,128)S(1)}, u32[]{:S(2)}, u32[]{:S(2)}) collective-permute-start(f32[72,128]{1,0:T(8,128)S(1)} %add.52), channel_id=1, source_target_pairs={{0,8},{4,12},{8,0},{12,4},{1,9},{5,13},{9,1},{13,5},{2,10},{6,14},... | collective-permute-start | bytes 110600 | tf_op jit(solution)/shard_map/ppermute | solution.py:546
  31.7 4.1 %collective-permute-start.5 = (f32[24,512]{1,0:T(8,128)S(1)}, f32[24,512]{1,0:T(8,128)S(1)}, u32[]{:S(2)}, u32[]{:S(2)}) collective-permute-start(f32[24,512]{1,0:T(8,128)S(1)} %slice_add_fusion.7), channel_id=1, source_target_pairs={{0,8},{4,12},{8,0},{12,4},{1,9},{5,13},{9,1},{13,5},{2,10},{6,14},... | collective-permute-start | bytes 147464 | tf_op jit(solution)/shard_map/ppermute | solution.py:546
  33.5 4.4 %collective-permute-start.7 = (f32[128,512]{1,0:T(8,128)S(1)}, f32[128,512]{1,0:T(8,128)S(1)}, u32[]{:S(2)}, u32[]{:S(2)}) collective-permute-start(f32[128,512]{1,0:T(8,128)S(1)} %get-tuple-element.72), channel_id=1, source_target_pairs={{0,4},{4,0},{8,12},{12,8},{1,5},{5,1},{9,13},{13,9},{2,6},{6,2},{1... | collective-permute-start | bytes 786440 | tf_op jit(solution)/shard_map/ppermute | solution.py:530
  35.7 10.7 %collective-permute-start.17 = (f32[152,1024]{1,0:T(8,128)S(1)}, f32[152,1024]{1,0:T(8,128)S(1)}, u32[]{:S(2)}, u32[]{:S(2)}) collective-permute-start(f32[152,1024]{1,0:T(8,128)S(1)} %get-tuple-element.84), channel_id=1, source_target_pairs={{0,4},{4,0},{8,12},{12,8},{1,5},{5,1},{9,13},{13,9},{2,6},{6,2},{1... | collective-permute-start | bytes 1867784 | tf_op jit(solution)/shard_map/ppermute | solution.py:523
  35.8 2.1 %collective-permute-start.2 = (f32[24,128]{1,0:T(8,128)S(1)}, f32[24,128]{1,0:T(8,128)S(1)}, u32[]{:S(2)}, u32[]{:S(2)}) collective-permute-start(f32[24,128]{1,0:T(8,128)S(1)} %slice_add_fusion.8.refs_1_), channel_id=1, source_target_pairs={{0,4},{4,0},{8,12},{12,8},{1,5},{5,1},{9,13},{13,9},{2,6},{6,2},{1... | collective-permute-start | bytes 36872 | tf_op jit(solution)/shard_map/ppermute | solution.py:552
  37.8 11.7 %collective-permute-start.13 = (f32[152,1024]{1,0:T(8,128)S(1)}, f32[152,1024]{1,0:T(8,128)S(1)}, u32[]{:S(2)}, u32[]{:S(2)}) collective-permute-start(f32[152,1024]{1,0:T(8,128)S(1)} %get-tuple-element.80), channel_id=1, source_target_pairs={{0,4},{4,0},{8,12},{12,8},{1,5},{5,1},{9,13},{13,9},{2,6},{6,2},{1... | collective-permute-start | bytes 1867784 | tf_op jit(solution)/shard_map/ppermute | solution.py:523
  38.0 11.8 %collective-permute-start.30 = (f32[152,512]{1,0:T(8,128)S(1)}, f32[152,512]{1,0:T(8,128)S(1)}, u32[]{:S(2)}, u32[]{:S(2)}) collective-permute-start(f32[152,512]{1,0:T(8,128)S(1)} %add.67), channel_id=1, source_target_pairs={{0,8},{4,12},{8,0},{12,4},{1,9},{5,13},{9,1},{13,5},{2,10},{6,14},... | collective-permute-start | bytes 933896 | tf_op jit(solution)/shard_map/ppermute | solution.py:546
  39.9 6.5 %collective-permute-start.6 = (f32[24,512]{1,0:T(8,128)S(1)}, f32[24,512]{1,0:T(8,128)S(1)}, u32[]{:S(2)}, u32[]{:S(2)}) collective-permute-start(f32[24,512]{1,0:T(8,128)S(1)} %add.55.refs_3_), channel_id=1, source_target_pairs={{0,4},{4,0},{8,12},{12,8},{1,5},{5,1},{9,13},{13,9},{2,6},{6,2},{1... | collective-permute-start | bytes 147464 | tf_op jit(solution)/shard_map/ppermute | solution.py:552
  39.9 28.3 %collective-permute-start.22 = (f32[152,1024]{1,0:T(8,128)S(1)}, f32[152,1024]{1,0:T(8,128)S(1)}, u32[]{:S(2)}, u32[]{:S(2)}) collective-permute-start(f32[152,1024]{1,0:T(8,128)S(1)} %add.63), channel_id=1, source_target_pairs={{0,8},{4,12},{8,0},{12,4},{1,9},{5,13},{9,1},{13,5},{2,10},{6,14},... | collective-permute-start | bytes 1867784 | tf_op jit(solution)/shard_map/ppermute | solution.py:546
  46.3 3.9 %collective-permute-start.32 = (f32[128,512]{1,0:T(8,128)S(1)}, f32[128,512]{1,0:T(8,128)S(1)}, u32[]{:S(2)}, u32[]{:S(2)}) collective-permute-start(f32[128,512]{1,0:T(8,128)S(1)} %get-tuple-element.98), channel_id=1, source_target_pairs={{0,4},{4,0},{8,12},{12,8},{1,5},{5,1},{9,13},{13,9},{2,6},{6,2},{1... | collective-permute-start | bytes 786440 | tf_op jit(solution)/shard_map/ppermute | solution.py:530
  46.5 21.7 %collective-permute-start.26 = (f32[152,512]{1,0:T(8,128)S(1)}, f32[152,512]{1,0:T(8,128)S(1)}, u32[]{:S(2)}, u32[]{:S(2)}) collective-permute-start(f32[152,512]{1,0:T(8,128)S(1)} %add.65), channel_id=1, source_target_pairs={{0,8},{4,12},{8,0},{12,4},{1,9},{5,13},{9,1},{13,5},{2,10},{6,14},... | collective-permute-start | bytes 933896 | tf_op jit(solution)/shard_map/ppermute | solution.py:546
  49.5 20.6 %collective-permute-start.28 = (f32[128,512]{1,0:T(8,128)S(1)}, f32[128,512]{1,0:T(8,128)S(1)}, u32[]{:S(2)}, u32[]{:S(2)}) collective-permute-start(f32[128,512]{1,0:T(8,128)S(1)} %get-tuple-element.94), channel_id=1, source_target_pairs={{0,4},{4,0},{8,12},{12,8},{1,5},{5,1},{9,13},{13,9},{2,6},{6,2},{1... | collective-permute-start | bytes 786440 | tf_op jit(solution)/shard_map/ppermute | solution.py:530
  49.8 31.8 %collective-permute-start.18 = (f32[152,1024]{1,0:T(8,128)S(1)}, f32[152,1024]{1,0:T(8,128)S(1)}, u32[]{:S(2)}, u32[]{:S(2)}) collective-permute-start(f32[152,1024]{1,0:T(8,128)S(1)} %add.61), channel_id=1, source_target_pairs={{0,8},{4,12},{8,0},{12,4},{1,9},{5,13},{9,1},{13,5},{2,10},{6,14},... | collective-permute-start | bytes 1867784 | tf_op jit(solution)/shard_map/ppermute | solution.py:546
  50.2 33.2 %collective-permute-start.24 = (f32[128,1024]{1,0:T(8,128)S(1)}, f32[128,1024]{1,0:T(8,128)S(1)}, u32[]{:S(2)}, u32[]{:S(2)}) collective-permute-start(f32[128,1024]{1,0:T(8,128)S(1)} %get-tuple-element.90), channel_id=1, source_target_pairs={{0,4},{4,0},{8,12},{12,8},{1,5},{5,1},{9,13},{13,9},{2,6},{6,2},{1... | collective-permute-start | bytes 1572872 | tf_op jit(solution)/shard_map/ppermute | solution.py:530
  68.2 15.3 %collective-permute-start.20 = (f32[128,1024]{1,0:T(8,128)S(1)}, f32[128,1024]{1,0:T(8,128)S(1)}, u32[]{:S(2)}, u32[]{:S(2)}) collective-permute-start(f32[128,1024]{1,0:T(8,128)S(1)} %get-tuple-element.86), channel_id=1, source_target_pairs={{0,4},{4,0},{8,12},{12,8},{1,5},{5,1},{9,13},{13,9},{2,6},{6,2},{1... | collective-permute-start | bytes 1572872 | tf_op jit(solution)/shard_map/ppermute | solution.py:530
  68.2 26.7 %collective-permute-start.14 = (f32[152,1024]{1,0:T(8,128)S(1)}, f32[152,1024]{1,0:T(8,128)S(1)}, u32[]{:S(2)}, u32[]{:S(2)}) collective-permute-start(f32[152,1024]{1,0:T(8,128)S(1)} %add.59), channel_id=1, source_target_pairs={{0,8},{4,12},{8,0},{12,4},{1,9},{5,13},{9,1},{13,5},{2,10},{6,14},... | collective-permute-start | bytes 1867784 | tf_op jit(solution)/shard_map/ppermute | solution.py:546
  70.1 42.9 %collective-permute-start.16 = (f32[128,1024]{1,0:T(8,128)S(1)}, f32[128,1024]{1,0:T(8,128)S(1)}, u32[]{:S(2)}, u32[]{:S(2)}) collective-permute-start(f32[128,1024]{1,0:T(8,128)S(1)} %get-tuple-element.82), channel_id=1, source_target_pairs={{0,4},{4,0},{8,12},{12,8},{1,5},{5,1},{9,13},{13,9},{2,6},{6,2},{1... | collective-permute-start | bytes 1572872 | tf_op jit(solution)/shard_map/ppermute | solution.py:530
  81.5 19.6 %collective-permute-start.10 = (f32[152,512]{1,0:T(8,128)S(1)}, f32[152,512]{1,0:T(8,128)S(1)}, u32[]{:S(2)}, u32[]{:S(2)}) collective-permute-start(f32[152,512]{1,0:T(8,128)S(1)} %add.57), channel_id=1, source_target_pairs={{0,8},{4,12},{8,0},{12,4},{1,9},{5,13},{9,1},{13,5},{2,10},{6,14},... | collective-permute-start | bytes 933896 | tf_op jit(solution)/shard_map/ppermute | solution.py:546
  83.5 17.7 %collective-permute-start.31 = (f32[24,512]{1,0:T(8,128)S(1)}, f32[24,512]{1,0:T(8,128)S(1)}, u32[]{:S(2)}, u32[]{:S(2)}) collective-permute-start(f32[24,512]{1,0:T(8,128)S(1)} %slice_add_fusion.4.refs_4_), channel_id=1, source_target_pairs={{0,4},{4,0},{8,12},{12,8},{1,5},{5,1},{9,13},{13,9},{2,6},{6,2},{1... | collective-permute-start | bytes 147464 | tf_op jit(solution)/shard_map/ppermute | solution.py:552
  83.5 19.3 %collective-permute-start.27 = (f32[24,512]{1,0:T(8,128)S(1)}, f32[24,512]{1,0:T(8,128)S(1)}, u32[]{:S(2)}, u32[]{:S(2)}) collective-permute-start(f32[24,512]{1,0:T(8,128)S(1)} %slice_add_fusion.5.refs_4_), channel_id=1, source_target_pairs={{0,4},{4,0},{8,12},{12,8},{1,5},{5,1},{9,13},{13,9},{2,6},{6,2},{1... | collective-permute-start | bytes 147464 | tf_op jit(solution)/shard_map/ppermute | solution.py:552
  94.9 8.2 %collective-permute-start.23 = (f32[24,1024]{1,0:T(8,128)S(1)}, f32[24,1024]{1,0:T(8,128)S(1)}, u32[]{:S(2)}, u32[]{:S(2)}) collective-permute-start(f32[24,1024]{1,0:T(8,128)S(1)} %slice_add_fusion.1.refs_4_), channel_id=1, source_target_pairs={{0,4},{4,0},{8,12},{12,8},{1,5},{5,1},{9,13},{13,9},{2,6},{6,2},{1... | collective-permute-start | bytes 294920 | tf_op jit(solution)/shard_map/ppermute | solution.py:552
  101.1 14.5 %collective-permute-start.12 = (f32[128,512]{1,0:T(8,128)S(1)}, f32[128,512]{1,0:T(8,128)S(1)}, u32[]{:S(2)}, u32[]{:S(2)}) collective-permute-start(f32[128,512]{1,0:T(8,128)S(1)} %get-tuple-element.78), channel_id=1, source_target_pairs={{0,4},{4,0},{8,12},{12,8},{1,5},{5,1},{9,13},{13,9},{2,6},{6,2},{1... | collective-permute-start | bytes 786440 | tf_op jit(solution)/shard_map/ppermute | solution.py:530
  101.1 16.3 %collective-permute-start.8 = (f32[128,512]{1,0:T(8,128)S(1)}, f32[128,512]{1,0:T(8,128)S(1)}, u32[]{:S(2)}, u32[]{:S(2)}) collective-permute-start(f32[128,512]{1,0:T(8,128)S(1)} %slice_add_fusion), channel_id=1, source_target_pairs={{0,8},{4,12},{8,0},{12,4},{1,9},{5,13},{9,1},{13,5},{2,10},{6,14},... | collective-permute-start | bytes 786440 | tf_op jit(solution)/shard_map/ppermute | solution.py:546
  102.9 1.3 %collective-permute-start.19 = (f32[24,1024]{1,0:T(8,128)S(1)}, f32[24,1024]{1,0:T(8,128)S(1)}, u32[]{:S(2)}, u32[]{:S(2)}) collective-permute-start(f32[24,1024]{1,0:T(8,128)S(1)} %slice_add_fusion.2.refs_4_), channel_id=1, source_target_pairs={{0,4},{4,0},{8,12},{12,8},{1,5},{5,1},{9,13},{13,9},{2,6},{6,2},{1... | collective-permute-start | bytes 294920 | tf_op jit(solution)/shard_map/ppermute | solution.py:552
  103.1 10.0 %collective-permute-start.15 = (f32[24,1024]{1,0:T(8,128)S(1)}, f32[24,1024]{1,0:T(8,128)S(1)}, u32[]{:S(2)}, u32[]{:S(2)}) collective-permute-start(f32[24,1024]{1,0:T(8,128)S(1)} %slice_add_fusion.3.refs_4_), channel_id=1, source_target_pairs={{0,4},{4,0},{8,12},{12,8},{1,5},{5,1},{9,13},{13,9},{2,6},{6,2},{1... | collective-permute-start | bytes 294920 | tf_op jit(solution)/shard_map/ppermute | solution.py:552
  104.2 11.4 %collective-permute-start.11 = (f32[24,512]{1,0:T(8,128)S(1)}, f32[24,512]{1,0:T(8,128)S(1)}, u32[]{:S(2)}, u32[]{:S(2)}) collective-permute-start(f32[24,512]{1,0:T(8,128)S(1)} %slice_add_fusion.6.refs_4_), channel_id=1, source_target_pairs={{0,4},{4,0},{8,12},{12,8},{1,5},{5,1},{9,13},{13,9},{2,6},{6,2},{1... | collective-permute-start | bytes 147464 | tf_op jit(solution)/shard_map/ppermute | solution.py:552
